TPU v7x, 16 devices: a whole 2x2x2 slice. The times are simulated.
16 devices in a mesh: tp: 2 (over z), dp: 8 (over y, x, core).
Axes of the slice: x: 2, y: 2, z: 2, core: 2. Of those that a mesh axis runs over, the one named last changes fastest.
Arguments:
- hidden: bfloat16 [24, 256, 896], P('dp')
- labels: int32 [24, 256], P('dp')
- loss_mask: int32 [24, 256], P('dp')
- norm_gain: bfloat16 [896], replicated
- embed_table: bfloat16 [151936, 896], P('tp')
Outputs:
- output 1: float32 [], replicated
- output 2: float32 [24, 256, 896], P('dp')
- output 3: float32 [151936, 896], P('tp', 'dp')
- output 4: float32 [896], replicated
All inputs are finite; a program needn't handle non-finite values.
Results may differ from a plain program's by a relative error of at most 0.001.
Values sent between devices are 32-bit elements.
A program may use at most 1 GiB of HBM per device.

v0:
```python
import jax
import jax.numpy as jnp
from jax import lax
from jax.sharding import PartitionSpec as P

EPSILON = 1e-6
ROW_CONTRACT = (((1,), (1,)), ((), ()))
TOKEN_CONTRACT = (((0,), (0,)), ((), ()))


def solution(mesh):
    def local_step(hidden, labels, loss_mask, norm_gain, embed_table):
        n_seq, seq_len, hid_width = hidden.shape
        vocab_loc = embed_table.shape[0]
        tokens = n_seq * seq_len
        offset = lax.axis_index("tp") * vocab_loc
        x_full = hidden.reshape(tokens, hid_width).astype(jnp.float32)
        inv_rms = lax.rsqrt(jnp.mean(x_full * x_full, axis=-1, keepdims=True) + EPSILON)
        x_hat = x_full * inv_rms
        gain32 = norm_gain.astype(jnp.float32)
        normed = (x_hat * gain32).astype(jnp.bfloat16)
        logits = lax.dot_general(normed, embed_table, ROW_CONTRACT, preferred_element_type=jnp.float32)
        is_label = jnp.arange(vocab_loc)[None, :] == (labels.reshape(tokens) - offset)[:, None]
        row_max = lax.pmax(jnp.max(logits, axis=-1), "tp")
        shifted = jnp.exp(logits - row_max[:, None])
        sum_exp = lax.psum(jnp.sum(shifted, axis=-1), "tp")
        target = lax.psum(jnp.sum(jnp.where(is_label, logits, 0.0), axis=-1), "tp")
        log_norm = row_max + jnp.log(sum_exp)
        mask_f = loss_mask.reshape(tokens).astype(jnp.float32)
        totals = lax.psum(jnp.stack([jnp.sum(mask_f), jnp.sum(mask_f * (log_norm - target))]), "dp")
        mask_count = totals[0]
        loss_value = totals[1] / mask_count
        weight = mask_f / mask_count
        grad_logit = ((shifted / sum_exp[:, None] - is_label.astype(jnp.float32)) * weight[:, None]).astype(jnp.bfloat16)
        grad_norm = lax.psum(jnp.dot(grad_logit, embed_table, preferred_element_type=jnp.float32), "tp")
        grad_gain = lax.psum(jnp.sum(grad_norm * x_hat, axis=0), "dp")
        value_a9 = grad_norm * gain32
        grad_hidden = inv_rms * (value_a9 - x_hat * jnp.mean(value_a9 * x_hat, axis=-1, keepdims=True))
        embed_part = lax.dot_general(grad_logit, normed, TOKEN_CONTRACT, preferred_element_type=jnp.float32)
        grad_embed = lax.psum_scatter(embed_part, "dp", scatter_dimension=1, tiled=True)
        return loss_value, grad_hidden.reshape(n_seq, seq_len, hid_width), grad_embed, grad_gain

    return jax.shard_map(
        local_step,
        mesh=mesh,
        in_specs=(P("dp", None, None), P("dp", None), P("dp", None), P(), P("tp", None)),
        out_specs=(P(), P("dp", None, None), P("tp", "dp"), P()),
        check_vma=False,
    )
```

profile of v0, /device:TPU:0, one launch (start us, length us, event | category | flops | bytes accessed | tf_op | source)
XLA Modules:
  0.0 3292.9 jit_solution(12578375695101776835)
XLA Ops:
  7.2 0.0 all-reduce.3.cloned.1.call-start
  7.2 1.4 convert_reduce_fusion
  8.6 0.7 convert_element_type.32
  9.3 0.7 broadcast_subtract_fusion
  10.0 0.6 sub.34
  10.6 0.7 convert_element_type.37
  11.2 0.0 copy-start.3
  11.2 0.6 convert_element_type.33
  11.8 1.7 multiply_reduce_fusion.2
  13.6 0.0 copy-start.5
  13.6 1.7 multiply_convert_fusion.1
  15.3 0.0 copy-start.1
  15.3 0.0 copy-start.8
  15.3 143.2 %fusion.2 = (f32[768]{0:T(1024)S(1)}, f32[768,75968]{0,1:T(8,128)}) fusion(bf16[768,896]{1,0:T(8,128)(2,1)S(1)} %multiply_convert_fusion.1, bf16[75968,896]{1,0:T(8,128)(2,1)} %param.9), kind=kOutput, calls=%fused_computation.19 | convolution fusion | flops 104609759232 | bytes 370887680 | tf_op jit(solution)/shard_map/dot_general | solution.py:22
  158.5 0.0 copy-done.3
  158.5 0.0 copy-done.5
  158.5 0.0 copy-done.1
  158.5 6.2 pmax.7
  164.7 0.0 copy-done.8
  164.7 0.0 copy-start.7
  164.7 70.8 %fusion = (f32[768]{0:T(1024)S(1)}, f32[768]{0:T(1024)S(1)}) fusion(f32[768,75968]{0,1:T(8,128)} %get-tuple-element.13, f32[768]{0:T(1024)S(1)} %pmax.7, s32[768]{0:T(1024)S(1)} %copy-done.8), kind=kLoop, calls=%fused_computation.4 | loop fusion | flops 291715584 | bytes 233385984 | tf_op jit(solution)/shard_map/reduce_sum | solution.py:26
  235.6 5.0 all-reduce
  240.6 0.0 copy-done.7
  240.6 0.6 multiply_reduce_fusion.3
  241.2 1.4 pad_maximum_fusion
  242.6 12.0 psum.37
  254.6 0.6 fusion.1
  255.1 0.6 broadcast_divide_fusion
  255.8 111.0 %multiply_convert_fusion = bf16[768,75968]{0,1:T(8,128)(2,1)} fusion(f32[768,75968]{0,1:T(8,128)} %get-tuple-element.13, f32[768]{0:T(1024)S(1)} %broadcast_divide_fusion, f32[768]{0:T(1024)S(1)} %get-tuple-element.9, s32[768]{0:T(1024)S(1)} %copy-done.8, f32[768]{0:T(1024)S(1)} %pmax.7), kind=kLoop, calls=%fused_computation | loop fusion | flops 408403968 | bytes 350072832 | tf_op jit(solution)/shard_map/convert_element_type | solution.py:34
  366.8 0.0 copy-start.2
  366.8 133.0 %fusion.3 = f32[768,896]{1,0:T(8,128)} fusion(bf16[768,75968]{0,1:T(8,128)(2,1)} %multiply_convert_fusion, bf16[75968,896]{1,0:T(8,128)(2,1)} %param.9), kind=kOutput, calls=%fused_computation.20 | convolution fusion | flops 104551415808 | bytes 255574016 | tf_op jit(solution)/shard_map/dot_general | solution.py:35
  499.7 0.0 all-reduce.3.cloned.1.call-update
  499.8 0.0 copy-done.2
  499.8 137.3 %fusion.4 = f32[75968,896]{0,1:T(8,128)} fusion(bf16[768,75968]{0,1:T(8,128)(2,1)} %multiply_convert_fusion, bf16[768,896]{1,0:T(8,128)(2,1)S(1)} %copy-done.2), kind=kOutput, calls=%fused_computation.21 | convolution fusion | flops 104551415808 | bytes 390332416 | tf_op jit(solution)/shard_map/dot_general | solution.py:39
  638.4 0.0 copy-start
  638.4 0.0 copy-start.4
  638.4 0.0 copy-start.6
  638.4 2627.6 %reduce_scatter.11 = f32[75968,112]{0,1:T(8,128)} reduce-scatter(f32[75968,896]{0,1:T(8,128)} %fusion.4), channel_id=1, replica_groups=mesh['tp'=2,'dp'=8] {'dp'}, use_global_device_ids=true, dimensions={1}, to_apply=%region_12.13 | reduce-scatter | bytes 306302976 | tf_op jit(solution)/shard_map/reduce_scatter | solution.py:40
  3266.0 0.0 all-reduce.3.cloned.1.call-done
  3266.0 0.0 copy-done
  3266.0 0.0 copy-done.4
  3266.0 0.0 copy-done.6
  3266.0 2.6 multiply_reduce_fusion
  3268.6 12.4 psum.39
  3281.0 3.9 subtract_multiply_fusion
  (3 shorter events, 0.0 us)
Async XLA Ops:
  7.2 3258.9 %all-reduce.3.cloned.1.call-start = ((), (), s32[]{:S(2)}) async-start(), calls=%async_computation.1 | async-start | bytes 5505024 | tf_op jit(solution)/shard_map/psum | solution.py:35
  11.2 147.3 %copy-start.3 = (f32[896]{0:T(1024)}, f32[896]{0:T(1024)S(1)}, u32[]{:S(2)}) copy-start(f32[896]{0:T(1024)S(1)} %convert_element_type.37) | copy-start | bytes 10756
  13.6 145.0 %copy-start.5 = (f32[768]{0:T(1024)}, f32[768]{0:T(1024)S(1)}, u32[]{:S(2)}) copy-start(f32[768]{0:T(1024)S(1)} %rsqrt.12) | copy-start | bytes 9220
  15.3 143.2 %copy-start.1 = (bf16[768,896]{1,0:T(8,128)(2,1)}, bf16[768,896]{1,0:T(8,128)(2,1)S(1)}, u32[]{:S(2)}) copy-start(bf16[768,896]{1,0:T(8,128)(2,1)S(1)} %multiply_convert_fusion.1) | copy-start | bytes 4128772
  15.3 149.4 %copy-start.8 = (s32[768]{0:T(1024)S(1)}, s32[768]{0:T(1024)}, u32[]{:S(2)}) copy-start(s32[768]{0:T(1024)} %sub.34) | copy-start | bytes 9220
  164.7 75.8 %copy-start.7 = (f32[768]{0:T(1024)S(1)}, f32[768]{0:T(1024)}, u32[]{:S(2)}) copy-start(f32[768]{0:T(1024)} %convert_element_type.33) | copy-start | bytes 9220
  366.8 133.0 %copy-start.2 = (bf16[768,896]{1,0:T(8,128)(2,1)S(1)}, bf16[768,896]{1,0:T(8,128)(2,1)}, u32[]{:S(2)}) copy-start(bf16[768,896]{1,0:T(8,128)(2,1)} %copy-done.1) | copy-start | bytes 4128772
  638.4 2627.6 %copy-start = (bf16[3,256,896]{2,1,0:T(8,128)(2,1)S(1)}, bf16[3,256,896]{2,1,0:T(8,128)(2,1)}, u32[]{:S(2)}) copy-start(bf16[3,256,896]{2,1,0:T(8,128)(2,1)} %param.5) | copy-start | bytes 4128772
  638.4 2627.6 %copy-start.4 = (f32[896]{0:T(1024)S(1)}, f32[896]{0:T(1024)}, u32[]{:S(2)}) copy-start(f32[896]{0:T(1024)} %copy-done.3) | copy-start | bytes 10756
  638.4 2627.6 %copy-start.6 = (f32[768]{0:T(1024)S(1)}, f32[768]{0:T(1024)}, u32[]{:S(2)}) copy-start(f32[768]{0:T(1024)} %copy-done.5) | copy-start | bytes 9220
Sparse Core Ops, SparseCore 0:
  499.9 73.8 all-reduce.2
where the time goes:
time: 3290 us
  blocking collectives  2660 us (81%)
  matrix products  413 us (13%)
  other arithmetic  198 us (6%)
    reduce_scatter x1, blocking collectives, local_step(): lax.psum_scatter(embed_part, 'dp', scatter_dimension=1, tiled=True)  2630 us
    dot_general x1, matrix products, local_step(): lax.dot_general(normed, embed_table, ROW_CONTRACT, preferred_element_type...  143 us
    dot_general x1, matrix products, local_step(): lax.dot_general(grad_logit, normed, TOKEN_CONTRACT, preferred_element_typ...  137 us
    dot_general x1, matrix products, local_step(): jnp.dot(grad_logit, embed_table, preferred_element_type=jnp.float32)  133 us
    convert_element_type x1, other arithmetic, local_step(): ((shifted / sum_exp[:, None] - is_label.astype(jnp.float32)) * weight[:,...  111 us
    reduce_sum x1, other arithmetic, local_step(): sum_exp = lax.psum(jnp.sum(shifted, axis=-1), 'tp')  70.8 us
  transfers between devices with their start and end apart: 1, of which 0 were waited for; matrix products, arithmetic and copies ran while one was open for 4% of the time, Pallas kernels for 0%

commit v1 on v0

v1 whole, which is shorter than its diff:
```python
import functools

import jax
import jax.numpy as jnp
from jax import lax
from jax.experimental import pallas as pl
from jax.experimental.pallas import tpu as pltpu
from jax.sharding import PartitionSpec as P


EPSILON = 1e-6
NEG = -1e30
VB = 256
NT = (((1,), (1,)), ((), ()))

CHUNKS = (2, 6, 5, 6)


def logit_kernel(vocab_loc, nblk, first, d_ref, *refs):
    pieces, (off_ref, gain_ref, e_ref), rest = refs[:2], refs[2:5], refs[5:]
    if first:
        z_ref, ut_ref, lab_ref, st_ref, eo_ref, u_s, m_s, s_s, t_s, l_s = rest
    else:
        _, _, _, z_ref, ut_ref, lab_ref, st_ref, u_s, m_s, s_s, t_s, l_s = rest
    j = pl.program_id(0)
    steps, width = nblk // 2, 2 * VB
    half = u_s.shape[0] // 2
    base = (d_ref[0] * nblk + 2 * j) * VB

    @pl.when(j == 0)
    def _():
        for part, h_ref in enumerate(pieces):
            for i in range(half // 256):
                x = h_ref[i * 256:(i + 1) * 256, :]
                r = lax.rsqrt(jnp.mean(x * x, axis=-1, keepdims=True) + EPSILON)
                y = ((x * r) * gain_ref[...]).astype(jnp.bfloat16)
                at = part * half + i * 256
                u_s[at:at + 256, :] = y
                ut_ref[:, at:at + 256] = y.T
            row = h_ref[half:half + 8, :][:1, :half].astype(jnp.int32) - off_ref[0]
            row = jnp.where(row < vocab_loc, row, -1)
            lab_ref[part * half:(part + 1) * half, :] = jnp.broadcast_to(row, (128, half)).T
        m_s[...] = jnp.full(m_s.shape, NEG, jnp.float32)
        s_s[...] = jnp.zeros(s_s.shape, jnp.float32)
        t_s[...] = jnp.zeros(t_s.shape, jnp.float32)
        l_s[...] = lab_ref[...] - lax.broadcasted_iota(jnp.int32, lab_ref.shape, 1)

    if first:
        rows = lax.broadcasted_iota(jnp.int32, e_ref.shape, 0) + base
        eo_ref[...] = jnp.where(rows < vocab_loc, e_ref[...].astype(jnp.float32), 0.0).astype(jnp.bfloat16)
        e_ref = eo_ref
    bias = jnp.where(lax.broadcasted_iota(jnp.int32, (1, width), 1) + base < vocab_loc, 0.0, NEG)
    for i in range(2 * half // 256):
        sl = slice(i * 256, (i + 1) * 256)
        z = lax.dot_general(u_s[sl, :], e_ref[...], NT, preferred_element_type=jnp.float32) + bias
        z_ref[0, sl, :] = z[:, :VB]
        z_ref[1, sl, :] = z[:, VB:]
        parts = [z[:, k:k + 128] for k in range(0, width, 128)]
        m_old = m_s[sl, :]
        m_new = functools.reduce(jnp.maximum, parts, m_old)
        m_s[sl, :] = m_new
        s_s[sl, :] = s_s[sl, :] * jnp.exp(m_old - m_new) + sum(jnp.exp(p - m_new) for p in parts)
        lab, target = l_s[sl, :], t_s[sl, :]
        for k, p in enumerate(parts):
            target = jnp.where(lab == base + k * 128, p, target)
        t_s[sl, :] = target

    @pl.when(j == steps - 1)
    def _():
        m_all = jnp.max(m_s[...], axis=-1, keepdims=True)
        s_all = jnp.sum(s_s[...] * jnp.exp(m_s[...] - m_all), axis=-1, keepdims=True)
        t_all = jnp.sum(t_s[...], axis=-1, keepdims=True)
        lane = lax.broadcasted_iota(jnp.int32, m_s.shape, 1)
        st_ref[...] = jnp.where(lane == 0, m_all, jnp.where(lane == 1, s_all, t_all)).T[:8, :]
        for part, h_ref in enumerate(pieces):
            st_ref[3:4, part * half:(part + 1) * half] = h_ref[half:half + 8, :][1:2, :half]


def logits_call(group, n_group, vocab_loc, nblk, half, dev, ha, hb, off, gain, embed, prev):
    ext, hid = ha.shape
    tg, width, steps = 2 * half, 2 * VB, nblk // 2
    first = prev is None
    last = (vocab_loc + width - 1) // width - 1
    one = pl.Buffered(1)
    if first:
        e_map = lambda j, d: (jnp.minimum(d[0] * steps + j, last), 0)
    else:
        e_map = lambda j, d: (j, 0)
    in_specs = [
        pl.BlockSpec((ext, hid), lambda j, d: (0, 0), pipeline_mode=one),
        pl.BlockSpec((ext, hid), lambda j, d: (0, 0), pipeline_mode=one),
        pl.BlockSpec(memory_space=pltpu.SMEM),
        pl.BlockSpec((1, hid), lambda j, d: (0, 0)),
        pl.BlockSpec((width, hid), e_map),
    ]
    out_specs = [
        pl.BlockSpec((2, tg, VB), lambda j, d: (j, group, 0)),
        pl.BlockSpec((hid, tg), lambda j, d: (0, group)),
        pl.BlockSpec((tg, 128), lambda j, d: (group, 0)),
        pl.BlockSpec((8, tg), lambda j, d: (0, 0)),
    ]
    out_shape = [
        jax.ShapeDtypeStruct((nblk, n_group * tg, VB), jnp.float32),
        jax.ShapeDtypeStruct((hid, n_group * tg), jnp.bfloat16),
        jax.ShapeDtypeStruct((n_group * tg, 128), jnp.int32),
        jax.ShapeDtypeStruct((8, tg), jnp.float32),
    ]
    args = [dev, ha, hb, off, gain, embed]
    alias = {}
    if first:
        out_specs.append(pl.BlockSpec((width, hid), lambda j, d: (j, 0)))
        out_shape.append(jax.ShapeDtypeStruct((nblk * VB, hid), jnp.bfloat16))
    else:
        in_specs += [pl.BlockSpec(memory_space=pl.ANY)] * 3
        alias = {6: 0, 7: 1, 8: 2}
        args += list(prev)
    return pl.pallas_call(
        functools.partial(logit_kernel, vocab_loc, nblk, first),
        grid_spec=pltpu.PrefetchScalarGridSpec(
            num_scalar_prefetch=1,
            grid=(steps,),
            in_specs=in_specs,
            out_specs=out_specs,
            scratch_shapes=[
                pltpu.VMEM((tg, hid), jnp.bfloat16),
                pltpu.VMEM((tg, 128), jnp.float32),
                pltpu.VMEM((tg, 128), jnp.float32),
                pltpu.VMEM((tg, 128), jnp.float32),
                pltpu.VMEM((tg, 128), jnp.int32),
            ],
        ),
        out_shape=out_shape,
        input_output_aliases=alias,
        compiler_params=pltpu.CompilerParams(vmem_limit_bytes=60 << 20),
        cost_estimate=pl.CostEstimate(flops=2 * tg * nblk * VB * hid, bytes_accessed=4 * tg * nblk * VB, transcendentals=0),
        name="logits",
    )(*args)


def grad_block(z, lse, wgt, lab, base):
    parts = []
    for k in range(VB // 128):
        p = jnp.exp(z[:, k * 128:(k + 1) * 128] - lse)
        p = jnp.where(lab == base + k * 128, p - 1.0, p)
        parts.append((p * wgt).astype(jnp.bfloat16))
    return jnp.concatenate(parts, axis=1)


def hidden_grad_kernel(nblk, inner, n_out, d_ref, z_ref, lse_ref, w_ref, lab_ref, e_ref, *rest):
    lse, wgt = lse_ref[...], w_ref[...]
    lab = lab_ref[...] - lax.broadcasted_iota(jnp.int32, lab_ref.shape, 1)
    acc_s, outs = rest[-1], rest[-1 - n_out:-1]
    acc_s[...] = rest[0][...] if len(rest) > n_out + 1 else jnp.zeros(acc_s.shape, jnp.float32)

    def step(it, carry):
        acc = None
        for k in range(inner):
            j = it * inner + k
            g = grad_block(z_ref[j], lse, wgt, lab, (d_ref[0] * nblk + j) * VB)
            e = e_ref[pl.ds(pl.multiple_of(j * VB, VB), VB), :]
            part = jnp.dot(g, e, preferred_element_type=jnp.float32)
            acc = part if acc is None else acc + part
        acc_s[...] += acc
        return carry

    lax.fori_loop(0, nblk // inner, step, 0)
    if n_out == 1:
        outs[0][...] = acc_s[...]
    else:
        per = pl.num_programs(0) // n_out
        for c in range(n_out):
            @pl.when(pl.program_id(0) // per == c)
            def _():
                outs[c][...] = acc_s[...]


def hidden_grad(dev, z, lse, wgt, lab, e_dev, parity, n_slot, add=None):
    nblk, tokens, _ = z.shape
    hid = e_dev.shape[1]
    tb = 256
    per = tokens // n_slot // tb
    steps = n_slot // 2 * per
    n_out = 1 if add is None else n_slot // 2
    at = lambda i: (2 * (i // per) + parity) * per + i % per
    wide = pl.BlockSpec((tb, 128), lambda i, d: (at(i), 0))
    in_specs = [
        pl.BlockSpec((nblk, tb, VB), lambda i, d: (0, at(i), 0)),
        wide, wide, wide,
        pl.BlockSpec((nblk * VB, hid), lambda i, d: (0, 0), pipeline_mode=pl.Buffered(1)),
    ]
    args = [dev, z, lse, wgt, lab, e_dev]
    row = pl.BlockSpec((tb, hid), lambda i, d: (i, 0))
    if add is None:
        out_specs = [row]
        out_shape = [jax.ShapeDtypeStruct((steps * tb, hid), jnp.float32)]
    else:
        in_specs.append(row)
        args.append(add)
        out_specs = [
            pl.BlockSpec((tb, hid), functools.partial(lambda c, i, d: (jnp.clip(i - c * per, 0, per - 1), 0), c))
            for c in range(n_out)
        ]
        out_shape = [jax.ShapeDtypeStruct((per * tb, hid), jnp.float32)] * n_out
    return pl.pallas_call(
        functools.partial(hidden_grad_kernel, nblk, 19, n_out),
        grid_spec=pltpu.PrefetchScalarGridSpec(
            num_scalar_prefetch=1,
            grid=(steps,),
            in_specs=in_specs,
            out_specs=out_specs,
            scratch_shapes=[pltpu.VMEM((tb, hid), jnp.float32)],
        ),
        out_shape=out_shape,
        compiler_params=pltpu.CompilerParams(vmem_limit_bytes=60 << 20),
        cost_estimate=pl.CostEstimate(flops=tokens * nblk * VB * hid, bytes_accessed=2 * tokens * nblk * VB, transcendentals=0),
        name="hidden_grad",
    )(*args)


def embed_grad_kernel(nblk, off, n_dp, d_ref, z_ref, lse_ref, w_ref, lab_ref, ut_ref, *rest):
    outs, acc_s = rest[:n_dp], rest[n_dp]
    j = pl.program_id(0)
    hid, tokens = ut_ref.shape
    cols = hid // n_dp
    lane = lax.broadcasted_iota(jnp.int32, (256, 128), 1)
    acc = None
    for i in range(tokens // 256):
        sl = slice(i * 256, (i + 1) * 256)
        lse, wgt, lab = lse_ref[sl, :], w_ref[sl, :], lab_ref[sl, :] - lane
        g = jnp.concatenate(
            [grad_block(z_ref[k, sl, :], lse, wgt, lab, (d_ref[0] * nblk + (off + j) * 2 + k) * VB) for k in range(2)],
            axis=1,
        )
        part = jnp.dot(ut_ref[:, sl], g, preferred_element_type=jnp.float32)
        acc = part if acc is None else acc + part
    acc_s[...] = acc
    for r in range(n_dp):
        at = pl.multiple_of((d_ref[0] ^ r) * cols, 8)
        outs[r][...] = acc_s[pl.ds(at, cols), :]


def embed_grad(dev, z, lse, wgt, lab, ut, off, steps, n_dp):
    nblk, tokens, _ = z.shape
    hid = ut.shape[0]
    cols = hid // n_dp
    one = pl.Buffered(1)
    wide = pl.BlockSpec((tokens, 128), lambda j, d: (0, 0), pipeline_mode=one)
    return pl.pallas_call(
        functools.partial(embed_grad_kernel, nblk, off, n_dp),
        grid_spec=pltpu.PrefetchScalarGridSpec(
            num_scalar_prefetch=1,
            grid=(steps,),
            in_specs=[
                pl.BlockSpec((2, tokens, VB), lambda j, d: (off + j, 0, 0)),
                wide, wide, wide,
                pl.BlockSpec((hid, tokens), lambda j, d: (0, 0), pipeline_mode=one),
            ],
            out_specs=[pl.BlockSpec((cols, 2 * VB), lambda j, d: (0, j))] * n_dp,
            scratch_shapes=[pltpu.VMEM((hid, 2 * VB), jnp.float32)],
        ),
        out_shape=[jax.ShapeDtypeStruct((cols, steps * 2 * VB), jnp.float32)] * n_dp,
        compiler_params=pltpu.CompilerParams(vmem_limit_bytes=60 << 20),
        cost_estimate=pl.CostEstimate(flops=2 * tokens * steps * 2 * VB * hid, bytes_accessed=8 * tokens * steps * VB, transcendentals=0),
        name="embed_grad",
    )(dev, z, lse, wgt, lab, ut)


def place_kernel(n_dp, per, off, last, d_ref, *refs):
    pieces, out = refs[:n_dp], refs[-1]
    s, j = pl.program_id(0), pl.program_id(1)
    for r in range(n_dp):
        @pl.when(((s ^ d_ref[0]) == r) & (s * per + off + j <= last))
        def _():
            out[...] = pieces[r][...]


def place(dev, pieces, prev, off, steps, vocab_loc, nblk):
    n_dp, cols = len(pieces), pieces[0].shape[0]
    rows, per = 2 * VB, nblk // 2
    last = (vocab_loc + rows - 1) // rows - 1
    specs = [
        pl.BlockSpec((cols, rows), functools.partial(lambda r, s, j, d: (0, jnp.where((s ^ d[0]) == r, j, 0)), r))
        for r in range(n_dp)
    ]
    args = [dev, *pieces]
    alias = {}
    if prev is not None:
        specs.append(pl.BlockSpec(memory_space=pl.ANY))
        args.append(prev)
        alias = {n_dp + 1: 0}
    return pl.pallas_call(
        functools.partial(place_kernel, n_dp, per, off, last),
        grid_spec=pltpu.PrefetchScalarGridSpec(
            num_scalar_prefetch=1,
            grid=(n_dp, steps),
            in_specs=specs,
            out_specs=pl.BlockSpec((cols, rows), lambda s, j, d: (0, jnp.minimum(s * per + off + j, last))),
        ),
        out_shape=jax.ShapeDtypeStruct((cols, vocab_loc), jnp.float32),
        input_output_aliases=alias,
        cost_estimate=pl.CostEstimate(flops=n_dp * steps * rows * cols, bytes_accessed=8 * n_dp * steps * rows * cols, transcendentals=0),
        name="place",
    )(*args)


def solution(mesh):
    n_dp, n_tp = mesh.shape["dp"], mesh.shape["tp"]

    def swap(x, mask, axis="dp"):
        size = n_dp if axis == "dp" else n_tp
        return lax.ppermute(x, axis, [(i, i ^ mask) for i in range(size)])

    def local_step(hidden, labels, loss_mask, norm_gain, embed_table):
        n_seq, seq_len, hid = hidden.shape
        vocab_loc = embed_table.shape[0]
        tokens = n_seq * seq_len
        unit = 2 * VB * n_dp
        nblk = (vocab_loc + unit - 1) // unit * 2
        me = lax.axis_index("dp").astype(jnp.int32)
        dev = me.reshape(1)
        offset = lax.axis_index("tp").astype(jnp.int32) * vocab_loc
        n_chip = n_dp // 2

        x_full = hidden.reshape(tokens, hid).astype(jnp.float32)
        gain32 = norm_gain.astype(jnp.float32)
        ints = jnp.stack([labels.reshape(tokens), loss_mask.reshape(tokens)]).astype(jnp.float32)
        mine = jnp.concatenate([x_full, jnp.pad(ints, ((0, 6), (0, hid - tokens)))])
        held = [mine] + [swap(mine, 2 * c) for c in range(1, n_chip)]
        prev, stats = None, []
        for g in range(n_chip):
            sib = swap(held[g], 1)
            res = logits_call(
                g, n_chip, vocab_loc, nblk, tokens, dev, held[g], sib, offset.reshape(1), gain32[None, :],
                embed_table if prev is None else e_dev, prev,
            )
            if prev is None:
                e_dev = res[4]
            prev = z, ut, lab = res[:3]
            stats.append(res[3])
        mask_all = jnp.concatenate([st[3] for st in stats]).reshape(n_dp, tokens)
        mask_count = jnp.sum(mask_all)

        stat = jnp.concatenate(stats, axis=1)[:3].reshape(3, n_dp, tokens)
        for axis, mask in (("dp", 1), ("dp", 2), ("dp", 4), ("tp", 1)):
            got = swap(stat, mask, axis)
            if axis == "dp":
                got = jnp.stack([got[:, r ^ mask] for r in range(n_dp)], axis=1)
            top = jnp.maximum(stat[0], got[0])
            stat = jnp.stack([
                top,
                stat[1] * jnp.exp(stat[0] - top) + got[1] * jnp.exp(got[0] - top),
                stat[2] + got[2],
            ])
        log_norm = stat[0] + jnp.log(stat[1])
        wide = lambda a: jnp.broadcast_to(a.reshape(-1)[:, None], (n_dp * tokens, 128))
        lse, wgt = wide(log_norm), wide(mask_all / mask_count)

        def after(x, *deps):
            return lax.optimization_barrier((x, *deps))[0]

        off, out, sent, turn = 0, None, [], dev
        for c, steps in enumerate(CHUNKS):
            pieces = embed_grad(turn, z, lse, wgt, lab, ut, off, steps, n_dp)
            sent.append((off, steps, [pieces[0]] + [swap(pieces[r], r) for r in range(1, n_dp)]))
            turn = after(dev, pieces[0])
            off += steps
            if c == 1:
                odd, = hidden_grad(turn, z, lse, wgt, lab, e_dev, 1, n_dp)
                turn = after(dev, odd)
                got = swap(odd, 1)
            if c == 2:
                even = hidden_grad(turn, z, lse, wgt, lab, e_dev, 0, n_dp, got)
                turn = after(dev, even[0])
        part = even[0]
        for c in range(1, n_chip):
            part = part + swap(even[c], 2 * c)
        grad_norm = part + swap(part, 1, "tp")
        for off, steps, pieces in sent:
            out = place(turn, pieces, out, off, steps, vocab_loc, nblk)
            turn = dev

        inv_rms = lax.rsqrt(jnp.mean(x_full * x_full, axis=-1, keepdims=True) + EPSILON)
        x_hat = x_full * inv_rms
        own = mask_all[0] * (log_norm[0] - stat[2, 0]) * (1.0 / n_tp)
        sums = lax.psum(jnp.concatenate([jnp.sum(grad_norm * x_hat, axis=0) * (1.0 / n_tp), jnp.sum(own)[None]]), ("tp", "dp"))
        grad_gain, loss_value = sums[:hid], sums[hid] / mask_count
        a = grad_norm * gain32
        grad_hidden = inv_rms * (a - x_hat * jnp.mean(a * x_hat, axis=-1, keepdims=True))
        return loss_value, grad_hidden.reshape(n_seq, seq_len, hid), out.T, grad_gain

    return jax.shard_map(
        local_step,
        mesh=mesh,
        in_specs=(P("dp", None, None), P("dp", None), P("dp", None), P(), P("tp", None)),
        out_specs=(P(), P("dp", None, None), P("tp", "dp"), P()),
        check_vma=False,
    )
```

time: 3290 us -> 1180 us (0.36)
  blocking collectives: 2660 us -> 32 us
  Pallas kernels: 0 us -> 614 us
  waiting for transfers between devices: 0.02 us -> 437 us
  matrix products: 413 us -> 0 us
  other arithmetic: 198 us -> 22.6 us
  starting transfers between devices: 0.04 us -> 44.8 us
    reduce_scatter x1 -> x0, blocking collectives: 2630 us -> none  [local_step(): lax.psum_scatter(embed_part, 'dp', scatter_dimension=1, tiled=True)]
    pallas_call x0 -> x14, Pallas kernels: none -> 614 us  [the longest x4 198 us: logits_call(): pl.pallas_call(functools.partial(logit_kernel, vocab_loc, nblk, first), g...]
    ppermute x0 -> x44, waiting for transfers between devices: none -> 437 us  [swap(): return lax.ppermute(x, axis, [(i, i ^ mask) for i in range(size)])]
    dot_general x3 -> x0, matrix products: 413 us -> none  [the longest x1 143 us: local_step(): lax.dot_general(normed, embed_table, ROW_CONTRACT, preferred_element_type...]
    convert_element_type x3 -> x2, other arithmetic: 113 us -> 1.54 us  [the longest x1 1.53 us: local_step(): x_full = hidden.reshape(tokens, hid).astype(jnp.float32)]
    reduce_sum x4 -> x5, other arithmetic: 75.4 us -> 8.11 us  [the longest x3 4.37 us: local_step(): mask_count = jnp.sum(mask_all)]
    ppermute x0 -> x44, starting transfers between devices: none -> 44.8 us  [swap(): return lax.ppermute(x, axis, [(i, i ^ mask) for i in range(size)])]
  transfers between devices with their start and end apart: 1 -> 44, of which waited for: 0 -> 16; matrix products, arithmetic and copies ran while one was open for 4% -> 1% of each run, Pallas kernels for 0% -> 35%
where the time goes in v1:
time: 1180 us; the launch traced here: 1170 us
  Pallas kernels  614 us (52%)
  waiting for transfers between devices  437 us (37%)
  starting transfers between devices  44.8 us (4%)
  blocking collectives  32 us (3%)
  other arithmetic  22.6 us (2%)
  local copies, waits for them, and re-layouts  15 us (1%)
    ppermute x44, waiting for transfers between devices, swap(): return lax.ppermute(x, axis, [(i, i ^ mask) for i in range(size)])  437 us
    pallas_call x4, Pallas kernels, logits_call(): pl.pallas_call(functools.partial(logit_kernel, vocab_loc, nblk, first), g...  198 us
    pallas_call x4, Pallas kernels, embed_grad(): pl.pallas_call(functools.partial(embed_grad_kernel, nblk, off, n_dp), gri...  162 us
    pallas_call x2, Pallas kernels, hidden_grad(): pl.pallas_call(functools.partial(hidden_grad_kernel, nblk, 19, n_out), gr...  160 us
    pallas_call x4, Pallas kernels, place(): pl.pallas_call(functools.partial(place_kernel, n_dp, per, off, last), gri...  93.7 us
    ppermute x44, starting transfers between devices, swap(): return lax.ppermute(x, axis, [(i, i ^ mask) for i in range(size)])  44.8 us
    psum x1, blocking collectives, local_step(): lax.psum(jnp.concatenate([jnp.sum(grad_norm * x_hat, axis=0) * (1.0 / n_t...  32 us
  transfers between devices with their start and end apart: 44, of which 16 were waited for; matrix products, arithmetic and copies ran while one was open for 1% of the time, Pallas kernels for 35%

profile of v1, /device:TPU:0, one launch (start us, length us, event | category | flops | bytes accessed | tf_op | source)
XLA Modules:
  0.0 1171.5 jit_solution(1404477178773133638)
XLA Ops:
  0.7 1.5 bitcast_convert_fusion
  2.5 3.2 collective-permute-start.5
  5.7 1.5 collective-permute-start.3
  7.2 59.7 %collective-permute-done.5.refs_0_ = f32[776,896]{1,0:T(8,128)} collective-permute-done((f32[776,896]{1,0:T(8,128)S(1)}, f32[776,896]{1,0:T(8,128)}, u32[]{:S(2)}, u32[]{:S(2)}) %collective-permute-start.5) | collective-permute-done | bytes 2781216 | tf_op jit(solution)/shard_map/ppermute | solution.py:311
  67.5 59.6 %collective-permute-done.3.refs_0_ = f32[776,896]{1,0:T(8,128)} collective-permute-done((f32[776,896]{1,0:T(8,128)S(1)}, f32[776,896]{1,0:T(8,128)}, u32[]{:S(2)}, u32[]{:S(2)}) %collective-permute-start.3) | collective-permute-done | bytes 2781216 | tf_op jit(solution)/shard_map/ppermute | solution.py:311
  127.2 50.8 %logits.4 = (f32[38,6144,256]{2,1,0:T(8,128)}, bf16[896,6144]{1,0:T(8,128)(2,1)}, s32[6144,128]{1,0:T(8,128)}, f32[8,1536]{1,0:T(8,128)}, bf16[9728,896]{1,0:T(8,128)(2,1)}) custom-call(s32[1]{0:T(128)} %bitcast.d_ref, f32[776,896]{1,0:T(8,128)} %copy-done.1, f32[776,896]{1,0:T(8,128)} %collective-permute-done.2.refs_1_, s32[1]{0:T(128)} %bitcast.2.refs_2_, ...), custom_call_target="tpu_custom_call" | custom-call | flops 26776436736 | bytes 59768832 | tf_op jit(solution)/shard_map/logits/pallas_call | solution.py:117
  179.3 49.0 %logits.5 = (f32[38,6144,256]{2,1,0:T(8,128)}, bf16[896,6144]{1,0:T(8,128)(2,1)}, s32[6144,128]{1,0:T(8,128)}, f32[8,1536]{1,0:T(8,128)}) custom-call(s32[1]{0:T(128)} %bitcast.d_ref, f32[776,896]{1,0:T(8,128)} %collective-permute-done.5.refs_0_, ...), custom_call_target="tpu_custom_call", output_to_operand_aliasing={{0}: (6, {}), {1}: (7, {}), {2}: (8, {})} | custom-call | flops 26776436736 | bytes 59768832 | tf_op jit(solution)/shard_map/logits/pallas_call | solution.py:117
  229.0 49.2 %logits.6 = (f32[38,6144,256]{2,1,0:T(8,128)}, bf16[896,6144]{1,0:T(8,128)(2,1)}, s32[6144,128]{1,0:T(8,128)}, f32[8,1536]{1,0:T(8,128)}) custom-call(s32[1]{0:T(128)} %bitcast.d_ref, f32[776,896]{1,0:T(8,128)} %collective-permute-done.3.refs_0_, ...), custom_call_target="tpu_custom_call", output_to_operand_aliasing={{0}: (6, {}), {1}: (7, {}), {2}: (8, {})} | custom-call | flops 26776436736 | bytes 59768832 | tf_op jit(solution)/shard_map/logits/pallas_call | solution.py:117
  279.1 49.0 %logits.7 = (f32[38,6144,256]{2,1,0:T(8,128)}, bf16[896,6144]{1,0:T(8,128)(2,1)}, s32[6144,128]{1,0:T(8,128)}, f32[8,1536]{1,0:T(8,128)}) custom-call(s32[1]{0:T(128)} %bitcast.d_ref, f32[776,896]{1,0:T(8,128)} %collective-permute-done.refs_0_, ...), custom_call_target="tpu_custom_call", output_to_operand_aliasing={{0}: (6, {}), {1}: (7, {}), {2}: (8, {})} | custom-call | flops 26776436736 | bytes 59768832 | tf_op jit(solution)/shard_map/logits/pallas_call | solution.py:117
  329.2 1.4 slice_reduce_fusion.1
  331.0 1.4 slice_reduce_fusion.3
  332.4 3.2 collective-permute-done.8
  336.4 1.6 collective-permute-start.9
  337.9 1.5 slice_reduce_fusion.5
  342.7 1.6 collective-permute-start.10
  344.4 2.7 collective-permute-done.10
  347.8 2.3 broadcast_in_dim.10.w_ref
  350.0 2.2 broadcast_in_dim.9.lse_ref
  352.2 24.0 %embed_grad.4 = (f32[112,1024]{1,0:T(8,128)}, f32[112,1024]{1,0:T(8,128)}, f32[112,1024]{1,0:T(8,128)}, f32[112,1024]{1,0:T(8,128)}, f32[112,1024]{1,0:T(8,128)}...) custom-call(s32[1]{0:T(128)} %bitcast.d_ref, f32[38,6144,256]{2,1,0:T(8,128)} %get-tuple-element.73.z_ref, ...), custom_call_target="tpu_custom_call" | custom-call | flops 11274289152 | bytes 25165824 | tf_op jit(solution)/shard_map/embed_grad/pallas_call | solution.py:248
  376.2 48.3 %embed_grad.5 = (f32[112,3072]{1,0:T(8,128)}, f32[112,3072]{1,0:T(8,128)}, f32[112,3072]{1,0:T(8,128)}, f32[112,3072]{1,0:T(8,128)}, f32[112,3072]{1,0:T(8,128)}...) custom-call(s32[1]{0:T(128)} %bitcast.d_ref, f32[38,6144,256]{2,1,0:T(8,128)} %get-tuple-element.73.z_ref, ...), custom_call_target="tpu_custom_call" | custom-call | flops 33822867456 | bytes 75497472 | tf_op jit(solution)/shard_map/embed_grad/pallas_call | solution.py:248
  424.4 79.1 %hidden_grad.2 = f32[3072,896]{1,0:T(8,128)} custom-call(s32[1]{0:T(128)} %bitcast.d_ref, f32[38,6144,256]{2,1,0:T(8,128)} %get-tuple-element.73.z_ref, f32[6144,128]{1,0:T(8,128)} %broadcast_in_dim.9.lse_ref, f32[6144,128]{1,0:T(8,128)} %broadcast_in_dim.10.w_ref, s32[6144,128]{1,0:T(8,128)} %get-tuple-element.78.lab_ref, ...), custom_call_target="tpu_custom_call" | custom-call | flops 53552873472 | bytes 119537664 | tf_op jit(solution)/shard_map/hidden_grad/pallas_call | solution.py:204
  504.5 0.9 collective-permute-start.39
  505.4 42.0 %embed_grad.6 = (f32[112,2560]{1,0:T(8,128)}, f32[112,2560]{1,0:T(8,128)}, f32[112,2560]{1,0:T(8,128)}, f32[112,2560]{1,0:T(8,128)}, f32[112,2560]{1,0:T(8,128)}...) custom-call(s32[1]{0:T(128)} %bitcast.d_ref, f32[38,6144,256]{2,1,0:T(8,128)} %get-tuple-element.73.z_ref, ...), custom_call_target="tpu_custom_call" | custom-call | flops 28185722880 | bytes 62914560 | tf_op jit(solution)/shard_map/embed_grad/pallas_call | solution.py:248
  549.9 12.2 %collective-permute-done.40.refs_4_ = f32[112,1024]{1,0:T(8,128)S(1)} collective-permute-done((f32[112,1024]{1,0:T(8,128)S(1)}, f32[112,1024]{1,0:T(8,128)S(1)}, u32[]{:S(2)}, u32[]{:S(2)}) %collective-permute-start.40) | collective-permute-done | bytes 458784 | tf_op jit(solution)/shard_map/ppermute | solution.py:311
  562.2 1.6 collective-permute-start.42
  563.7 5.9 collective-permute-done.41.refs_5_
  569.7 2.4 collective-permute-start.43
  572.1 14.4 %collective-permute-done.42.refs_6_ = f32[112,1024]{1,0:T(8,128)S(1)} collective-permute-done((f32[112,1024]{1,0:T(8,128)S(1)}, f32[112,1024]{1,0:T(8,128)S(1)}, u32[]{:S(2)}, u32[]{:S(2)}) %collective-permute-start.42) | collective-permute-done | bytes 458784 | tf_op jit(solution)/shard_map/ppermute | solution.py:311
  587.2 7.2 collective-permute-done.43.refs_7_
  595.2 1.5 collective-permute-start.26
  596.7 1.5 collective-permute-start.27
  598.2 1.4 collective-permute-start.28
  599.6 19.5 %collective-permute-done.25.refs_3_ = f32[112,2560]{1,0:T(8,128)S(1)} collective-permute-done((f32[112,2560]{1,0:T(8,128)}, f32[112,2560]{1,0:T(8,128)S(1)}, u32[]{:S(2)}, u32[]{:S(2)}) %collective-permute-start.25) | collective-permute-done | bytes 1146912 | tf_op jit(solution)/shard_map/ppermute | solution.py:311
  619.1 2.0 collective-permute-start.30
  621.0 26.4 %collective-permute-done.26.refs_4_ = f32[112,2560]{1,0:T(8,128)S(1)} collective-permute-done((f32[112,2560]{1,0:T(8,128)}, f32[112,2560]{1,0:T(8,128)S(1)}, u32[]{:S(2)}, u32[]{:S(2)}) %collective-permute-start.26) | collective-permute-done | bytes 1146912 | tf_op jit(solution)/shard_map/ppermute | solution.py:311
  647.5 2.0 collective-permute-start.31
  649.5 23.2 %collective-permute-done.27.refs_5_ = f32[112,2560]{1,0:T(8,128)S(1)} collective-permute-done((f32[112,2560]{1,0:T(8,128)}, f32[112,2560]{1,0:T(8,128)S(1)}, u32[]{:S(2)}, u32[]{:S(2)}) %collective-permute-start.27) | collective-permute-done | bytes 1146912 | tf_op jit(solution)/shard_map/ppermute | solution.py:311
  673.8 1.5 collective-permute-start.33
  675.2 1.2 collective-permute-start.29
  676.5 81.2 %hidden_grad.3 = (f32[768,896]{1,0:T(8,128)}, f32[768,896]{1,0:T(8,128)}, f32[768,896]{1,0:T(8,128)}, f32[768,896]{1,0:T(8,128)}) custom-call(s32[1]{0:T(128)} %bitcast.d_ref, f32[38,6144,256]{2,1,0:T(8,128)} %get-tuple-element.73.z_ref, f32[6144,128]{1,0:T(8,128)} %broadcast_in_dim.9.lse_ref, f32[6144,128]{1,0:T(8,128)} %broadcast_in_dim.10.w_ref, ...), custom_call_target="tpu_custom_call" | custom-call | flops 53552873472 | bytes 119537664 | tf_op jit(solution)/shard_map/hidden_grad/pallas_call | solution.py:204
  758.1 1.5 collective-permute-start.35
  759.7 1.1 copy-done.4
  760.7 1.1 collective-permute-start.12
  762.7 1.5 collective-permute-start.14
  764.2 48.2 %embed_grad.7 = (f32[112,3072]{1,0:T(8,128)}, f32[112,3072]{1,0:T(8,128)}, f32[112,3072]{1,0:T(8,128)}, f32[112,3072]{1,0:T(8,128)}, f32[112,3072]{1,0:T(8,128)}...) custom-call(s32[1]{0:T(128)} %bitcast.d_ref, f32[38,6144,256]{2,1,0:T(8,128)} %get-tuple-element.73.z_ref, ...), custom_call_target="tpu_custom_call" | custom-call | flops 33822867456 | bytes 75497472 | tf_op jit(solution)/shard_map/embed_grad/pallas_call | solution.py:248
  812.5 7.5 collective-permute-done.34.refs_5_
  820.0 1.6 collective-permute-start.36
  821.6 28.8 %collective-permute-done.12 = f32[768,896]{1,0:T(8,128)S(1)} collective-permute-done((f32[768,896]{1,0:T(8,128)}, f32[768,896]{1,0:T(8,128)S(1)}, u32[]{:S(2)}, u32[]{:S(2)}) %collective-permute-start.12) | collective-permute-done | bytes 2752544 | tf_op jit(solution)/shard_map/ppermute | solution.py:311
  850.8 115.9 %collective-permute-done.13 = f32[768,896]{1,0:T(8,128)} collective-permute-done((f32[768,896]{1,0:T(8,128)}, f32[768,896]{1,0:T(8,128)}, u32[]{:S(2)}, u32[]{:S(2)}) %collective-permute-start.13) | collective-permute-done | bytes 2752544 | tf_op jit(solution)/shard_map/ppermute | solution.py:311
  966.7 1.2 collective-permute-start.17
  968.3 4.8 add_add_fusion
  973.1 1.7 collective-permute-start.15
  974.8 1.0 collective-permute-start.19
  976.3 23.6 %collective-permute-done.17.refs_2_ = f32[112,3072]{1,0:T(8,128)S(1)} collective-permute-done((f32[112,3072]{1,0:T(8,128)}, f32[112,3072]{1,0:T(8,128)S(1)}, u32[]{:S(2)}, u32[]{:S(2)}) %collective-permute-start.17) | collective-permute-done | bytes 1376288 | tf_op jit(solution)/shard_map/ppermute | solution.py:311
  1000.0 1.5 collective-permute-start.21
  1001.4 26.9 %collective-permute-done.18.refs_3_ = f32[112,3072]{1,0:T(8,128)S(1)} collective-permute-done((f32[112,3072]{1,0:T(8,128)}, f32[112,3072]{1,0:T(8,128)S(1)}, u32[]{:S(2)}, u32[]{:S(2)}) %collective-permute-start.18) | collective-permute-done | bytes 1376288 | tf_op jit(solution)/shard_map/ppermute | solution.py:311
  1028.3 2.4 collective-permute-start.22
  1035.0 10.9 place.4.refs_8_
  1045.8 29.1 %place.5.refs_8_ = f32[112,75968]{1,0:T(8,128)} custom-call(s32[1]{0:T(128)} %bitcast.d_ref, f32[112,3072]{1,0:T(8,128)} %get-tuple-element.82.refs_0_, f32[112,3072]{1,0:T(8,128)} %copy-done.3, f32[112,3072]{1,0:T(8,128)} %copy-done.4, f32[112,3072]{1,0:T(8,128)} %copy-done.5, ...), custom_call_target="tpu_custom_call", output_to_operand_aliasing={{}: (9, {})} | custom-call | flops 2752512 | bytes 22020096 | tf_op jit(solution)/shard_map/place/pallas_call | solution.py:291
  1075.0 24.8 %place.6.refs_8_ = f32[112,75968]{1,0:T(8,128)} custom-call(s32[1]{0:T(128)} %bitcast.d_ref, f32[112,2560]{1,0:T(8,128)} %get-tuple-element.85.refs_0_, f32[112,2560]{1,0:T(8,128)} %copy-done.10, f32[112,2560]{1,0:T(8,128)} %copy-done.11, f32[112,2560]{1,0:T(8,128)} %copy-done.12, f32[112,2560]{1,0:T(8,128)} %copy-done.13, ...), custom_call_target="tpu_custom_call", output_to_operand_aliasing={{}: (9, {})} | custom-call | flops 2293760 | bytes 18350080 | tf_op jit(solution)/shard_map/place/pallas_call | solution.py:291
  1099.8 28.9 %place.7 = f32[112,75968]{1,0:T(8,128)} custom-call(s32[1]{0:T(128)} %bitcast.d_ref, f32[112,3072]{1,0:T(8,128)} %get-tuple-element.92.refs_0_, f32[112,3072]{1,0:T(8,128)} %copy-done.6, f32[112,3072]{1,0:T(8,128)} %copy-done.7, f32[112,3072]{1,0:T(8,128)} %copy-done.8, f32[112,3072]{1,0:T(8,128)} %collective-permute-done.19.refs_4_, ...), custom_call_target="tpu_custom_call", output_to_operand_aliasing={{}: (9, {})} | custom-call | flops 2752512 | bytes 22020096 | tf_op jit(solution)/shard_map/place/pallas_call | solution.py:291
  1128.7 3.1 multiply_reduce_fusion
  1132.5 32.0 %psum.7 = f32[897]{0:T(1024)S(1)} all-reduce(f32[897]{0:T(1024)S(1)} %pad_maximum_fusion.5), channel_id=1, replica_groups=mesh['tp'=2,'dp'=8] {'tp','dp'}, use_global_device_ids=true, to_apply=%region_7.8 | all-reduce | flops 897 | bytes 7176 | tf_op jit(solution)/shard_map/psum | solution.py:385
  1165.7 4.4 subtract_multiply_fusion
  (200 shorter events, 21.3 us)
Async XLA Ops:
  2.2 64.7 %copy-start.36 = (bf16[896]{0:T(1024)(128)(2,1)S(1)}, bf16[896]{0:T(1024)(128)(2,1)}, u32[]{:S(2)}) copy-start(bf16[896]{0:T(1024)(128)(2,1)} %param.8) | copy-start | bytes 5380
  2.4 124.7 %copy-start.1 = (f32[776,896]{1,0:T(8,128)}, f32[776,896]{1,0:T(8,128)S(1)}, u32[]{:S(2)}) copy-start(f32[776,896]{1,0:T(8,128)S(1)} %select_maximum_fusion.refs_0_) | copy-start | bytes 8343556
  2.5 64.5 %collective-permute-start.5 = (f32[776,896]{1,0:T(8,128)S(1)}, f32[776,896]{1,0:T(8,128)}, u32[]{:S(2)}, u32[]{:S(2)}) collective-permute-start(f32[776,896]{1,0:T(8,128)S(1)} %select_maximum_fusion.refs_0_), channel_id=1, source_target_pairs={{0,2},{1,3},{2,0},{3,1},{4,6},{5,7},{6,4},{7,5},{8,10},{9,11},{10,... | collective-permute-start | bytes 8343560 | tf_op jit(solution)/shard_map/ppermute | solution.py:311
  5.7 121.5 %collective-permute-start.3 = (f32[776,896]{1,0:T(8,128)S(1)}, f32[776,896]{1,0:T(8,128)}, u32[]{:S(2)}, u32[]{:S(2)}) collective-permute-start(f32[776,896]{1,0:T(8,128)S(1)} %select_maximum_fusion.refs_0_), channel_id=1, source_target_pairs={{0,4},{1,5},{2,6},{3,7},{4,0},{5,1},{6,2},{7,3},{8,12},{9,13},{10,... | collective-permute-start | bytes 8343560 | tf_op jit(solution)/shard_map/ppermute | solution.py:311
  7.2 119.9 %collective-permute-start.2 = (f32[776,896]{1,0:T(8,128)S(1)}, f32[776,896]{1,0:T(8,128)}, u32[]{:S(2)}, u32[]{:S(2)}) collective-permute-start(f32[776,896]{1,0:T(8,128)S(1)} %select_maximum_fusion.refs_0_), channel_id=1, source_target_pairs={{0,1},{1,0},{2,3},{3,2},{4,5},{5,4},{6,7},{7,6},{8,9},{9,8},{10,11... | collective-permute-start | bytes 8343560 | tf_op jit(solution)/shard_map/ppermute | solution.py:311
  7.2 171.6 %collective-permute-start = (f32[776,896]{1,0:T(8,128)S(1)}, f32[776,896]{1,0:T(8,128)}, u32[]{:S(2)}, u32[]{:S(2)}) collective-permute-start(f32[776,896]{1,0:T(8,128)S(1)} %select_maximum_fusion.refs_0_), channel_id=1, source_target_pairs={{0,6},{1,7},{2,4},{3,5},{4,2},{5,3},{6,0},{7,1},{8,14},{9,15},{10,... | collective-permute-start | bytes 8343560 | tf_op jit(solution)/shard_map/ppermute | solution.py:311
  66.9 112.4 %collective-permute-start.6 = (f32[776,896]{1,0:T(8,128)}, f32[776,896]{1,0:T(8,128)}, u32[]{:S(2)}, u32[]{:S(2)}) collective-permute-start(f32[776,896]{1,0:T(8,128)} %collective-permute-done.5.refs_0_), channel_id=1, source_target_pairs={{0,1},{1,0},{2,3},{3,2},{4,5},{5,4},{6,7},{7,6},{8,9},{9,8},{10,11... | collective-permute-start | bytes 8343560 | tf_op jit(solution)/shard_map/ppermute | solution.py:311
  127.1 101.9 %collective-permute-start.4 = (f32[776,896]{1,0:T(8,128)}, f32[776,896]{1,0:T(8,128)}, u32[]{:S(2)}, u32[]{:S(2)}) collective-permute-start(f32[776,896]{1,0:T(8,128)} %collective-permute-done.3.refs_0_), channel_id=1, source_target_pairs={{0,1},{1,0},{2,3},{3,2},{4,5},{5,4},{6,7},{7,6},{8,9},{9,8},{10,11... | collective-permute-start | bytes 8343560 | tf_op jit(solution)/shard_map/ppermute | solution.py:311
  178.8 100.3 %collective-permute-start.1 = (f32[776,896]{1,0:T(8,128)}, f32[776,896]{1,0:T(8,128)}, u32[]{:S(2)}, u32[]{:S(2)}) collective-permute-start(f32[776,896]{1,0:T(8,128)} %collective-permute-done.refs_0_), channel_id=1, source_target_pairs={{0,1},{1,0},{2,3},{3,2},{4,5},{5,4},{6,7},{7,6},{8,9},{9,8},{10,11... | collective-permute-start | bytes 8343560 | tf_op jit(solution)/shard_map/ppermute | solution.py:311
  329.2 1.5 collective-permute-start.7
  331.0 4.7 collective-permute-start.8
  336.4 5.6 collective-permute-start.9
  342.7 4.4 collective-permute-start.10
  424.4 79.6 %copy-start.46 = (f32[112,1024]{1,0:T(8,128)S(1)}, f32[112,1024]{1,0:T(8,128)}, u32[]{:S(2)}) copy-start(f32[112,1024]{1,0:T(8,128)} %get-tuple-element.116) | copy-start | bytes 1376260
  424.4 80.0 %copy-start.45 = (f32[112,1024]{1,0:T(8,128)S(1)}, f32[112,1024]{1,0:T(8,128)}, u32[]{:S(2)}) copy-start(f32[112,1024]{1,0:T(8,128)} %get-tuple-element.117) | copy-start | bytes 1376260
  503.5 171.7 %collective-permute-start.11 = (f32[3072,896]{1,0:T(8,128)}, f32[3072,896]{1,0:T(8,128)}, u32[]{:S(2)}, u32[]{:S(2)}) collective-permute-start(f32[3072,896]{1,0:T(8,128)} %hidden_grad.2), channel_id=1, source_target_pairs={{0,1},{1,0},{2,3},{3,2},{4,5},{5,4},{6,7},{7,6},{8,9},{9,8},{10,11... | collective-permute-start | bytes 33030152 | tf_op jit(solution)/shard_map/ppermute | solution.py:311
  503.5 44.8 %collective-permute-start.37 = (f32[112,1024]{1,0:T(8,128)}, f32[112,1024]{1,0:T(8,128)S(1)}, u32[]{:S(2)}, u32[]{:S(2)}) collective-permute-start(f32[112,1024]{1,0:T(8,128)} %get-tuple-element.115), channel_id=1, source_target_pairs={{0,1},{1,0},{2,3},{3,2},{4,5},{5,4},{6,7},{7,6},{8,9},{9,8},{10,11... | collective-permute-start | bytes 1376264 | tf_op jit(solution)/shard_map/ppermute | solution.py:311
  504.0 44.7 %collective-permute-start.38 = (f32[112,1024]{1,0:T(8,128)S(1)}, f32[112,1024]{1,0:T(8,128)S(1)}, u32[]{:S(2)}, u32[]{:S(2)}) collective-permute-start(f32[112,1024]{1,0:T(8,128)S(1)} %copy-done.46), channel_id=1, source_target_pairs={{0,2},{1,3},{2,0},{3,1},{4,6},{5,7},{6,4},{7,5},{8,10},{9,11},{10,... | collective-permute-start | bytes 1376264 | tf_op jit(solution)/shard_map/ppermute | solution.py:311
  504.5 57.7 %copy-start.42 = (f32[112,1024]{1,0:T(8,128)S(1)}, f32[112,1024]{1,0:T(8,128)}, u32[]{:S(2)}) copy-start(f32[112,1024]{1,0:T(8,128)} %get-tuple-element.120) | copy-start | bytes 1376260
  504.5 65.2 %copy-start.41 = (f32[112,1024]{1,0:T(8,128)S(1)}, f32[112,1024]{1,0:T(8,128)}, u32[]{:S(2)}) copy-start(f32[112,1024]{1,0:T(8,128)} %get-tuple-element.121) | copy-start | bytes 1376260
  504.5 44.6 %collective-permute-start.39 = (f32[112,1024]{1,0:T(8,128)S(1)}, f32[112,1024]{1,0:T(8,128)S(1)}, u32[]{:S(2)}, u32[]{:S(2)}) collective-permute-start(f32[112,1024]{1,0:T(8,128)S(1)} %copy-done.45), channel_id=1, source_target_pairs={{0,3},{1,2},{2,1},{3,0},{4,7},{5,6},{6,5},{7,4},{8,11},{9,10},{10,... | collective-permute-start | bytes 1376264 | tf_op jit(solution)/shard_map/ppermute | solution.py:311
  547.5 49.2 %collective-permute-start.23 = (f32[112,2560]{1,0:T(8,128)}, f32[112,2560]{1,0:T(8,128)S(1)}, u32[]{:S(2)}, u32[]{:S(2)}) collective-permute-start(f32[112,2560]{1,0:T(8,128)} %get-tuple-element.100), channel_id=1, source_target_pairs={{0,1},{1,0},{2,3},{3,2},{4,5},{5,4},{6,7},{7,6},{8,9},{9,8},{10,11... | collective-permute-start | bytes 3440648 | tf_op jit(solution)/shard_map/ppermute | solution.py:311
  548.3 70.8 %copy-start.20 = (f32[112,1024]{1,0:T(8,128)}, f32[112,1024]{1,0:T(8,128)S(1)}, u32[]{:S(2)}) copy-start(f32[112,1024]{1,0:T(8,128)S(1)} %collective-permute-done.37.refs_1_) | copy-start | bytes 1376260
  548.3 49.9 %collective-permute-start.24 = (f32[112,2560]{1,0:T(8,128)}, f32[112,2560]{1,0:T(8,128)S(1)}, u32[]{:S(2)}, u32[]{:S(2)}) collective-permute-start(f32[112,2560]{1,0:T(8,128)} %get-tuple-element.101), channel_id=1, source_target_pairs={{0,2},{1,3},{2,0},{3,1},{4,6},{5,7},{6,4},{7,5},{8,10},{9,11},{10,... | collective-permute-start | bytes 3440648 | tf_op jit(solution)/shard_map/ppermute | solution.py:311
  548.7 70.3 %copy-start.21 = (f32[112,1024]{1,0:T(8,128)}, f32[112,1024]{1,0:T(8,128)S(1)}, u32[]{:S(2)}) copy-start(f32[112,1024]{1,0:T(8,128)S(1)} %collective-permute-done.38.refs_2_) | copy-start | bytes 1376260
  548.7 13.4 %collective-permute-start.40 = (f32[112,1024]{1,0:T(8,128)S(1)}, f32[112,1024]{1,0:T(8,128)S(1)}, u32[]{:S(2)}, u32[]{:S(2)}) collective-permute-start(f32[112,1024]{1,0:T(8,128)S(1)} %copy-done.44), channel_id=1, source_target_pairs={{0,4},{1,5},{2,6},{3,7},{4,0},{5,1},{6,2},{7,3},{8,12},{9,13},{10,... | collective-permute-start | bytes 1376264 | tf_op jit(solution)/shard_map/ppermute | solution.py:311
  549.1 69.9 %copy-start.22 = (f32[112,1024]{1,0:T(8,128)}, f32[112,1024]{1,0:T(8,128)S(1)}, u32[]{:S(2)}) copy-start(f32[112,1024]{1,0:T(8,128)S(1)} %collective-permute-done.39.refs_3_) | copy-start | bytes 1376260
  549.1 20.5 %collective-permute-start.41 = (f32[112,1024]{1,0:T(8,128)S(1)}, f32[112,1024]{1,0:T(8,128)S(1)}, u32[]{:S(2)}, u32[]{:S(2)}) collective-permute-start(f32[112,1024]{1,0:T(8,128)S(1)} %copy-done.43), channel_id=1, source_target_pairs={{0,5},{1,4},{2,7},{3,6},{4,1},{5,0},{6,3},{7,2},{8,13},{9,12},{10,... | collective-permute-start | bytes 1376264 | tf_op jit(solution)/shard_map/ppermute | solution.py:311
  562.2 24.3 %collective-permute-start.42 = (f32[112,1024]{1,0:T(8,128)S(1)}, f32[112,1024]{1,0:T(8,128)S(1)}, u32[]{:S(2)}, u32[]{:S(2)}) collective-permute-start(f32[112,1024]{1,0:T(8,128)S(1)} %copy-done.42), channel_id=1, source_target_pairs={{0,6},{1,7},{2,4},{3,5},{4,2},{5,3},{6,0},{7,1},{8,14},{9,15},{10,... | collective-permute-start | bytes 1376264 | tf_op jit(solution)/shard_map/ppermute | solution.py:311
  569.7 24.8 %collective-permute-start.43 = (f32[112,1024]{1,0:T(8,128)S(1)}, f32[112,1024]{1,0:T(8,128)S(1)}, u32[]{:S(2)}, u32[]{:S(2)}) collective-permute-start(f32[112,1024]{1,0:T(8,128)S(1)} %copy-done.41), channel_id=1, source_target_pairs={{0,7},{1,6},{2,5},{3,4},{4,3},{5,2},{6,1},{7,0},{8,15},{9,14},{10,... | collective-permute-start | bytes 1376264 | tf_op jit(solution)/shard_map/ppermute | solution.py:311
  587.2 31.8 %collective-permute-start.25 = (f32[112,2560]{1,0:T(8,128)}, f32[112,2560]{1,0:T(8,128)S(1)}, u32[]{:S(2)}, u32[]{:S(2)}) collective-permute-start(f32[112,2560]{1,0:T(8,128)} %get-tuple-element.102), channel_id=1, source_target_pairs={{0,3},{1,2},{2,1},{3,0},{4,7},{5,6},{6,5},{7,4},{8,11},{9,10},{10,... | collective-permute-start | bytes 3440648 | tf_op jit(solution)/shard_map/ppermute | solution.py:311
  595.2 52.3 %collective-permute-start.26 = (f32[112,2560]{1,0:T(8,128)}, f32[112,2560]{1,0:T(8,128)S(1)}, u32[]{:S(2)}, u32[]{:S(2)}) collective-permute-start(f32[112,2560]{1,0:T(8,128)} %get-tuple-element.103), channel_id=1, source_target_pairs={{0,4},{1,5},{2,6},{3,7},{4,0},{5,1},{6,2},{7,3},{8,12},{9,13},{10,... | collective-permute-start | bytes 3440648 | tf_op jit(solution)/shard_map/ppermute | solution.py:311
  596.7 76.0 %copy-start.10 = (f32[112,2560]{1,0:T(8,128)}, f32[112,2560]{1,0:T(8,128)S(1)}, u32[]{:S(2)}) copy-start(f32[112,2560]{1,0:T(8,128)S(1)} %collective-permute-done.23.refs_1_) | copy-start | bytes 3440644
  596.7 76.0 %collective-permute-start.27 = (f32[112,2560]{1,0:T(8,128)}, f32[112,2560]{1,0:T(8,128)S(1)}, u32[]{:S(2)}, u32[]{:S(2)}) collective-permute-start(f32[112,2560]{1,0:T(8,128)} %get-tuple-element.104), channel_id=1, source_target_pairs={{0,5},{1,4},{2,7},{3,6},{4,1},{5,0},{6,3},{7,2},{8,13},{9,12},{10,... | collective-permute-start | bytes 3440648 | tf_op jit(solution)/shard_map/ppermute | solution.py:311
  598.2 74.5 %copy-start.11 = (f32[112,2560]{1,0:T(8,128)}, f32[112,2560]{1,0:T(8,128)S(1)}, u32[]{:S(2)}) copy-start(f32[112,2560]{1,0:T(8,128)S(1)} %collective-permute-done.24.refs_2_) | copy-start | bytes 3440644
  598.2 75.2 %collective-permute-start.28 = (f32[112,2560]{1,0:T(8,128)}, f32[112,2560]{1,0:T(8,128)S(1)}, u32[]{:S(2)}, u32[]{:S(2)}) collective-permute-start(f32[112,2560]{1,0:T(8,128)} %get-tuple-element.105), channel_id=1, source_target_pairs={{0,6},{1,7},{2,4},{3,5},{4,2},{5,3},{6,0},{7,1},{8,14},{9,15},{10,... | collective-permute-start | bytes 3440648 | tf_op jit(solution)/shard_map/ppermute | solution.py:311
  619.1 139.1 %collective-permute-start.30 = (f32[112,3072]{1,0:T(8,128)}, f32[112,3072]{1,0:T(8,128)S(1)}, u32[]{:S(2)}, u32[]{:S(2)}) collective-permute-start(f32[112,3072]{1,0:T(8,128)} %get-tuple-element.107), channel_id=1, source_target_pairs={{0,1},{1,0},{2,3},{3,2},{4,5},{5,4},{6,7},{7,6},{8,9},{9,8},{10,11... | collective-permute-start | bytes 4128776 | tf_op jit(solution)/shard_map/ppermute | solution.py:311
  647.5 112.2 %collective-permute-start.31 = (f32[112,3072]{1,0:T(8,128)}, f32[112,3072]{1,0:T(8,128)S(1)}, u32[]{:S(2)}, u32[]{:S(2)}) collective-permute-start(f32[112,3072]{1,0:T(8,128)} %get-tuple-element.108), channel_id=1, source_target_pairs={{0,2},{1,3},{2,0},{3,1},{4,6},{5,7},{6,4},{7,5},{8,10},{9,11},{10,... | collective-permute-start | bytes 4128776 | tf_op jit(solution)/shard_map/ppermute | solution.py:311
  672.7 89.1 %collective-permute-start.32 = (f32[112,3072]{1,0:T(8,128)}, f32[112,3072]{1,0:T(8,128)S(1)}, u32[]{:S(2)}, u32[]{:S(2)}) collective-permute-start(f32[112,3072]{1,0:T(8,128)} %get-tuple-element.109), channel_id=1, source_target_pairs={{0,3},{1,2},{2,1},{3,0},{4,7},{5,6},{6,5},{7,4},{8,11},{9,10},{10,... | collective-permute-start | bytes 4128776 | tf_op jit(solution)/shard_map/ppermute | solution.py:311
  673.8 89.0 %collective-permute-start.33 = (f32[112,3072]{1,0:T(8,128)}, f32[112,3072]{1,0:T(8,128)}, u32[]{:S(2)}, u32[]{:S(2)}) collective-permute-start(f32[112,3072]{1,0:T(8,128)} %get-tuple-element.110), channel_id=1, source_target_pairs={{0,4},{1,5},{2,6},{3,7},{4,0},{5,1},{6,2},{7,3},{8,12},{9,13},{10,... | collective-permute-start | bytes 4128776 | tf_op jit(solution)/shard_map/ppermute | solution.py:311
  675.2 82.4 %collective-permute-start.29 = (f32[112,2560]{1,0:T(8,128)}, f32[112,2560]{1,0:T(8,128)}, u32[]{:S(2)}, u32[]{:S(2)}) collective-permute-start(f32[112,2560]{1,0:T(8,128)} %get-tuple-element.106), channel_id=1, source_target_pairs={{0,7},{1,6},{2,5},{3,4},{4,3},{5,2},{6,1},{7,0},{8,15},{9,14},{10,... | collective-permute-start | bytes 3440648 | tf_op jit(solution)/shard_map/ppermute | solution.py:311
  757.6 62.3 %collective-permute-start.34 = (f32[112,3072]{1,0:T(8,128)}, f32[112,3072]{1,0:T(8,128)}, u32[]{:S(2)}, u32[]{:S(2)}) collective-permute-start(f32[112,3072]{1,0:T(8,128)} %get-tuple-element.111), channel_id=1, source_target_pairs={{0,5},{1,4},{2,7},{3,6},{4,1},{5,0},{6,3},{7,2},{8,13},{9,12},{10,... | collective-permute-start | bytes 4128776 | tf_op jit(solution)/shard_map/ppermute | solution.py:311
  758.1 215.0 %collective-permute-start.35 = (f32[112,3072]{1,0:T(8,128)}, f32[112,3072]{1,0:T(8,128)}, u32[]{:S(2)}, u32[]{:S(2)}) collective-permute-start(f32[112,3072]{1,0:T(8,128)} %get-tuple-element.112), channel_id=1, source_target_pairs={{0,6},{1,7},{2,4},{3,5},{4,2},{5,3},{6,0},{7,1},{8,14},{9,15},{10,... | collective-permute-start | bytes 4128776 | tf_op jit(solution)/shard_map/ppermute | solution.py:311
  760.7 89.7 %collective-permute-start.12 = (f32[768,896]{1,0:T(8,128)}, f32[768,896]{1,0:T(8,128)S(1)}, u32[]{:S(2)}, u32[]{:S(2)}) collective-permute-start(f32[768,896]{1,0:T(8,128)} %get-tuple-element.88), channel_id=1, source_target_pairs={{0,2},{1,3},{2,0},{3,1},{4,6},{5,7},{6,4},{7,5},{8,10},{9,11},{10,... | collective-permute-start | bytes 8257544 | tf_op jit(solution)/shard_map/ppermute | solution.py:311
  761.9 204.8 %collective-permute-start.13 = (f32[768,896]{1,0:T(8,128)}, f32[768,896]{1,0:T(8,128)}, u32[]{:S(2)}, u32[]{:S(2)}) collective-permute-start(f32[768,896]{1,0:T(8,128)} %get-tuple-element.89), channel_id=1, source_target_pairs={{0,4},{1,5},{2,6},{3,7},{4,0},{5,1},{6,2},{7,3},{8,12},{9,13},{10,... | collective-permute-start | bytes 8257544 | tf_op jit(solution)/shard_map/ppermute | solution.py:311
  762.7 205.2 %collective-permute-start.14 = (f32[768,896]{1,0:T(8,128)}, f32[768,896]{1,0:T(8,128)}, u32[]{:S(2)}, u32[]{:S(2)}) collective-permute-start(f32[768,896]{1,0:T(8,128)} %get-tuple-element.90), channel_id=1, source_target_pairs={{0,6},{1,7},{2,4},{3,5},{4,2},{5,3},{6,0},{7,1},{8,14},{9,15},{10,... | collective-permute-start | bytes 8257544 | tf_op jit(solution)/shard_map/ppermute | solution.py:311
  820.0 154.8 %collective-permute-start.36 = (f32[112,3072]{1,0:T(8,128)}, f32[112,3072]{1,0:T(8,128)S(1)}, u32[]{:S(2)}, u32[]{:S(2)}) collective-permute-start(f32[112,3072]{1,0:T(8,128)} %get-tuple-element.113), channel_id=1, source_target_pairs={{0,7},{1,6},{2,5},{3,4},{4,3},{5,2},{6,1},{7,0},{8,15},{9,14},{10,... | collective-permute-start | bytes 4128776 | tf_op jit(solution)/shard_map/ppermute | solution.py:311
  850.4 117.5 %copy-start.2 = (f32[768,896]{1,0:T(8,128)}, f32[768,896]{1,0:T(8,128)S(1)}, u32[]{:S(2)}) copy-start(f32[768,896]{1,0:T(8,128)S(1)} %collective-permute-done.12) | copy-start | bytes 8257540
  850.4 125.4 %collective-permute-start.16 = (f32[112,3072]{1,0:T(8,128)}, f32[112,3072]{1,0:T(8,128)S(1)}, u32[]{:S(2)}, u32[]{:S(2)}) collective-permute-start(f32[112,3072]{1,0:T(8,128)} %get-tuple-element.93), channel_id=1, source_target_pairs={{0,1},{1,0},{2,3},{3,2},{4,5},{5,4},{6,7},{7,6},{8,9},{9,8},{10,11... | collective-permute-start | bytes 4128776 | tf_op jit(solution)/shard_map/ppermute | solution.py:311
  966.7 33.3 %collective-permute-start.17 = (f32[112,3072]{1,0:T(8,128)}, f32[112,3072]{1,0:T(8,128)S(1)}, u32[]{:S(2)}, u32[]{:S(2)}) collective-permute-start(f32[112,3072]{1,0:T(8,128)} %get-tuple-element.94), channel_id=1, source_target_pairs={{0,2},{1,3},{2,0},{3,1},{4,6},{5,7},{6,4},{7,5},{8,10},{9,11},{10,... | collective-permute-start | bytes 4128776 | tf_op jit(solution)/shard_map/ppermute | solution.py:311
  967.9 62.8 %copy-start.37 = (bf16[896]{0:T(1024)(128)(2,1)S(1)}, bf16[896]{0:T(1024)(128)(2,1)}, u32[]{:S(2)}) copy-start(bf16[896]{0:T(1024)(128)(2,1)} %param.8) | copy-start | bytes 5380
  967.9 62.8 %copy-start = (bf16[3,256,896]{2,1,0:T(8,128)(2,1)S(1)}, bf16[3,256,896]{2,1,0:T(8,128)(2,1)}, u32[]{:S(2)}) copy-start(bf16[3,256,896]{2,1,0:T(8,128)(2,1)} %param.5) | copy-start | bytes 4128772
  967.9 64.0 %copy-start.32 = (f32[1,6144]{1,0:T(1,128)S(1)}, f32[1,6144]{1,0:T(1,128)}, u32[]{:S(2)}) copy-start(f32[1,6144]{1,0:T(1,128)} %copy-done.31) | copy-start | bytes 73732
  967.9 64.0 %copy-start.30 = (f32[1,6144]{1,0:T(1,128)S(1)}, f32[1,6144]{1,0:T(1,128)}, u32[]{:S(2)}) copy-start(f32[1,6144]{1,0:T(1,128)} %copy-done.29) | copy-start | bytes 73732
  968.0 64.8 %copy-start.17 = (f32[3,8,768]{2,1,0:T(8,128)S(1)}, f32[3,8,768]{2,1,0:T(8,128)}, u32[]{:S(2)}) copy-start(f32[3,8,768]{2,1,0:T(8,128)} %copy-done.16) | copy-start | bytes 221188
  968.0 64.8 %copy-start.19 = (f32[3,8,768]{2,1,0:T(8,128)S(1)}, f32[3,8,768]{2,1,0:T(8,128)}, u32[]{:S(2)}) copy-start(f32[3,8,768]{2,1,0:T(8,128)} %copy-done.18) | copy-start | bytes 221188
  968.0 64.8 %copy-start.28 = (f32[1,8,768]{2,1,0:T(8,128)S(1)}, f32[1,8,768]{2,1,0:T(8,128)}, u32[]{:S(2)}) copy-start(f32[1,8,768]{2,1,0:T(8,128)} %copy-done.27) | copy-start | bytes 73732
  968.0 60.3 %collective-permute-start.18 = (f32[112,3072]{1,0:T(8,128)}, f32[112,3072]{1,0:T(8,128)S(1)}, u32[]{:S(2)}, u32[]{:S(2)}) collective-permute-start(f32[112,3072]{1,0:T(8,128)} %get-tuple-element.95), channel_id=1, source_target_pairs={{0,3},{1,2},{2,1},{3,0},{4,7},{5,6},{6,5},{7,4},{8,11},{9,10},{10,... | collective-permute-start | bytes 4128776 | tf_op jit(solution)/shard_map/ppermute | solution.py:311
  973.1 155.5 %collective-permute-start.15 = (f32[768,896]{1,0:T(8,128)S(1)}, f32[768,896]{1,0:T(8,128)}, u32[]{:S(2)}, u32[]{:S(2)}) collective-permute-start(f32[768,896]{1,0:T(8,128)S(1)} %add_add_fusion), channel_id=1, source_target_pairs={{0,8},{8,0},{1,9},{9,1},{2,10},{10,2},{3,11},{11,3},{4,12},{12,4},... | collective-permute-start | bytes 8257544 | tf_op jit(solution)/shard_map/ppermute | solution.py:311
  974.8 56.3 %copy-start.9 = (f32[112,3072]{1,0:T(8,128)}, f32[112,3072]{1,0:T(8,128)S(1)}, u32[]{:S(2)}) copy-start(f32[112,3072]{1,0:T(8,128)S(1)} %collective-permute-done.36.refs_7_) | copy-start | bytes 4128772
  974.8 124.9 %collective-permute-start.19 = (f32[112,3072]{1,0:T(8,128)}, f32[112,3072]{1,0:T(8,128)}, u32[]{:S(2)}, u32[]{:S(2)}) collective-permute-start(f32[112,3072]{1,0:T(8,128)} %get-tuple-element.96), channel_id=1, source_target_pairs={{0,4},{1,5},{2,6},{3,7},{4,0},{5,1},{6,2},{7,3},{8,12},{9,13},{10,... | collective-permute-start | bytes 4128776 | tf_op jit(solution)/shard_map/ppermute | solution.py:311
  975.8 123.9 %collective-permute-start.20 = (f32[112,3072]{1,0:T(8,128)}, f32[112,3072]{1,0:T(8,128)}, u32[]{:S(2)}, u32[]{:S(2)}) collective-permute-start(f32[112,3072]{1,0:T(8,128)} %get-tuple-element.97), channel_id=1, source_target_pairs={{0,5},{1,4},{2,7},{3,6},{4,1},{5,0},{6,3},{7,2},{8,13},{9,12},{10,... | collective-permute-start | bytes 4128776 | tf_op jit(solution)/shard_map/ppermute | solution.py:311
  1000.0 99.8 %collective-permute-start.21 = (f32[112,3072]{1,0:T(8,128)}, f32[112,3072]{1,0:T(8,128)}, u32[]{:S(2)}, u32[]{:S(2)}) collective-permute-start(f32[112,3072]{1,0:T(8,128)} %get-tuple-element.98), channel_id=1, source_target_pairs={{0,6},{1,7},{2,4},{3,5},{4,2},{5,3},{6,0},{7,1},{8,14},{9,15},{10,... | collective-permute-start | bytes 4128776 | tf_op jit(solution)/shard_map/ppermute | solution.py:311
  1028.3 71.5 %collective-permute-start.22 = (f32[112,3072]{1,0:T(8,128)}, f32[112,3072]{1,0:T(8,128)}, u32[]{:S(2)}, u32[]{:S(2)}) collective-permute-start(f32[112,3072]{1,0:T(8,128)} %get-tuple-element.99), channel_id=1, source_target_pairs={{0,7},{1,6},{2,5},{3,4},{4,3},{5,2},{6,1},{7,0},{8,15},{9,14},{10,... | collective-permute-start | bytes 4128776 | tf_op jit(solution)/shard_map/ppermute | solution.py:311
  (27 other events, 453.4 us)

commit v2 on v1

--- a/solution.py
+++ b/solution.py
@@ -13,7 +13,7 @@
 VB = 256
 NT = (((1,), (1,)), ((), ()))
 
-CHUNKS = (2, 6, 5, 6)
+CHUNKS = ((0, 3), (3, 7), (15, 4), (10, 5))
 
 
 def logit_kernel(vocab_loc, nblk, first, d_ref, *refs):
@@ -174,33 +174,24 @@
                 outs[c][...] = acc_s[...]
 
 
-def hidden_grad(dev, z, lse, wgt, lab, e_dev, parity, n_slot, add=None):
-    nblk, tokens, _ = z.shape
+def hidden_grad(dev, z, lse, wgt, lab, e_dev, tb, at, steps, n_out, add=None, add_at=None):
+    nblk, _, _ = z.shape
     hid = e_dev.shape[1]
-    tb = 256
-    per = tokens // n_slot // tb
-    steps = n_slot // 2 * per
-    n_out = 1 if add is None else n_slot // 2
-    at = lambda i: (2 * (i // per) + parity) * per + i % per
-    wide = pl.BlockSpec((tb, 128), lambda i, d: (at(i), 0))
+    per = steps // n_out
+    wide = pl.BlockSpec((tb, 128), lambda i, d: (at(i, d), 0))
     in_specs = [
-        pl.BlockSpec((nblk, tb, VB), lambda i, d: (0, at(i), 0)),
+        pl.BlockSpec((nblk, tb, VB), lambda i, d: (0, at(i, d), 0)),
         wide, wide, wide,
         pl.BlockSpec((nblk * VB, hid), lambda i, d: (0, 0), pipeline_mode=pl.Buffered(1)),
     ]
     args = [dev, z, lse, wgt, lab, e_dev]
-    row = pl.BlockSpec((tb, hid), lambda i, d: (i, 0))
-    if add is None:
-        out_specs = [row]
-        out_shape = [jax.ShapeDtypeStruct((steps * tb, hid), jnp.float32)]
-    else:
-        in_specs.append(row)
+    if add is not None:
+        in_specs.append(pl.BlockSpec((tb, hid), lambda i, d: (add_at(i, d), 0)))
         args.append(add)
-        out_specs = [
-            pl.BlockSpec((tb, hid), functools.partial(lambda c, i, d: (jnp.clip(i - c * per, 0, per - 1), 0), c))
-            for c in range(n_out)
-        ]
-        out_shape = [jax.ShapeDtypeStruct((per * tb, hid), jnp.float32)] * n_out
+    out_specs = [
+        pl.BlockSpec((tb, hid), functools.partial(lambda c, i, d: (jnp.clip(i - c * per, 0, per - 1), 0), c))
+        for c in range(n_out)
+    ]
     return pl.pallas_call(
         functools.partial(hidden_grad_kernel, nblk, 19, n_out),
         grid_spec=pltpu.PrefetchScalarGridSpec(
@@ -210,9 +201,9 @@
             out_specs=out_specs,
             scratch_shapes=[pltpu.VMEM((tb, hid), jnp.float32)],
         ),
-        out_shape=out_shape,
+        out_shape=[jax.ShapeDtypeStruct((per * tb, hid), jnp.float32)] * n_out,
         compiler_params=pltpu.CompilerParams(vmem_limit_bytes=60 << 20),
-        cost_estimate=pl.CostEstimate(flops=tokens * nblk * VB * hid, bytes_accessed=2 * tokens * nblk * VB, transcendentals=0),
+        cost_estimate=pl.CostEstimate(flops=2 * steps * tb * nblk * VB * hid, bytes_accessed=4 * steps * tb * nblk * VB, transcendentals=0),
         name="hidden_grad",
     )(*args)
 
@@ -223,17 +214,24 @@
     hid, tokens = ut_ref.shape
     cols = hid // n_dp
     lane = lax.broadcasted_iota(jnp.int32, (256, 128), 1)
-    acc = None
-    for i in range(tokens // 256):
-        sl = slice(i * 256, (i + 1) * 256)
-        lse, wgt, lab = lse_ref[sl, :], w_ref[sl, :], lab_ref[sl, :] - lane
-        g = jnp.concatenate(
-            [grad_block(z_ref[k, sl, :], lse, wgt, lab, (d_ref[0] * nblk + (off + j) * 2 + k) * VB) for k in range(2)],
-            axis=1,
-        )
-        part = jnp.dot(ut_ref[:, sl], g, preferred_element_type=jnp.float32)
-        acc = part if acc is None else acc + part
-    acc_s[...] = acc
+    group = tokens // 4
+    acc_s[...] = jnp.zeros(acc_s.shape, jnp.float32)
+
+    def step(it, carry):
+        acc = None
+        for i in range(group // 256):
+            sl = pl.ds(pl.multiple_of(it * group + i * 256, 256), 256)
+            lse, wgt, lab = lse_ref[sl, :], w_ref[sl, :], lab_ref[sl, :] - lane
+            g = jnp.concatenate(
+                [grad_block(z_ref[k, sl, :], lse, wgt, lab, (d_ref[0] * nblk + (off + j) * 2 + k) * VB) for k in range(2)],
+                axis=1,
+            )
+            part = jnp.dot(ut_ref[:, sl], g, preferred_element_type=jnp.float32)
+            acc = part if acc is None else acc + part
+        acc_s[...] += acc
+        return carry
+
+    lax.fori_loop(0, 4, step, 0)
     for r in range(n_dp):
         at = pl.multiple_of((d_ref[0] ^ r) * cols, 8)
         outs[r][...] = acc_s[pl.ds(at, cols), :]
@@ -265,6 +263,52 @@
     )(dev, z, lse, wgt, lab, ut)
 
 
+def place_copy_kernel(n_dp, per, off, d_ref, *refs):
+    pieces, out, (buf, in_sem, out_sem) = refs[:n_dp], refs[-4], refs[-3:]
+    width = pieces[0].shape[1]
+    loads = [pltpu.make_async_copy(pieces[r], buf.at[r], in_sem.at[r]) for r in range(n_dp)]
+    stores = []
+    for r in range(n_dp):
+        at = pl.multiple_of(((d_ref[0] ^ r) * per + off) * 2 * VB, 2 * VB)
+        stores.append(pltpu.make_async_copy(buf.at[r], out.at[:, pl.ds(at, width)], out_sem.at[r]))
+    for load in loads:
+        load.start()
+    for load, store in zip(loads, stores):
+        load.wait()
+        store.start()
+    for store in stores:
+        store.wait()
+
+
+def place_copy(dev, pieces, prev, off, steps, vocab_loc, nblk):
+    n_dp, cols = len(pieces), pieces[0].shape[0]
+    width = steps * 2 * VB
+    anywhere = pl.BlockSpec(memory_space=pl.ANY)
+    args = [dev, *pieces]
+    alias = {}
+    if prev is not None:
+        args.append(prev)
+        alias = {n_dp + 1: 0}
+    return pl.pallas_call(
+        functools.partial(place_copy_kernel, n_dp, nblk // 2, off),
+        grid_spec=pltpu.PrefetchScalarGridSpec(
+            num_scalar_prefetch=1,
+            grid=(1,),
+            in_specs=[anywhere] * (len(args) - 1),
+            out_specs=anywhere,
+            scratch_shapes=[
+                pltpu.VMEM((n_dp, cols, width), jnp.float32),
+                pltpu.SemaphoreType.DMA((n_dp,)),
+                pltpu.SemaphoreType.DMA((n_dp,)),
+            ],
+        ),
+        out_shape=jax.ShapeDtypeStruct((cols, vocab_loc), jnp.float32),
+        input_output_aliases=alias,
+        compiler_params=pltpu.CompilerParams(vmem_limit_bytes=40 << 20),
+        cost_estimate=pl.CostEstimate(flops=n_dp * width * cols, bytes_accessed=8 * n_dp * width * cols, transcendentals=0),
+    )(*args)
+
+
 def place_kernel(n_dp, per, off, last, d_ref, *refs):
     pieces, out = refs[:n_dp], refs[-1]
     s, j = pl.program_id(0), pl.program_id(1)
@@ -317,8 +361,9 @@
         unit = 2 * VB * n_dp
         nblk = (vocab_loc + unit - 1) // unit * 2
         me = lax.axis_index("dp").astype(jnp.int32)
-        dev = me.reshape(1)
-        offset = lax.axis_index("tp").astype(jnp.int32) * vocab_loc
+        plane = lax.axis_index("tp").astype(jnp.int32)
+        dev = jnp.stack([me, plane])
+        offset = plane * vocab_loc
         n_chip = n_dp // 2
 
         x_full = hidden.reshape(tokens, hid).astype(jnp.float32)
@@ -358,34 +403,52 @@
         def after(x, *deps):
             return lax.optimization_barrier((x, *deps))[0]
 
-        off, out, sent, turn = 0, None, [], dev
-        for c, steps in enumerate(CHUNKS):
+        half = tokens // 2
+        tb = half // 2
+        odd_at = lambda i, d: (2 * (i // 3) + 1) * 3 + i % 3
+        send_at = lambda i, d: (i // 2) * 8 + (1 - d[1]) * 2 + i % 2
+        send_add = lambda i, d: (i // 2) * 4 + (1 - d[1]) * 2 + i % 2
+        keep_at = lambda i, d: (i // 2) * 8 + d[1] * 2 + i % 2
+        keep_add = lambda i, d: (i // 2) * 4 + d[1] * 2 + i % 2
+        sent, turn = [], dev
+        for c, (off, steps) in enumerate(CHUNKS):
+            if c == len(CHUNKS) - 2:
+                odd, = hidden_grad(turn, z, lse, wgt, lab, e_dev, 256, odd_at, 12, 1)
+                turn = after(dev, odd)
+                got = swap(odd, 1)
+            if c == len(CHUNKS) - 1:
+                away = hidden_grad(turn, z, lse, wgt, lab, e_dev, tb, send_at, 8, n_chip, got, send_add)
+                turn = after(dev, away[0])
+                back = [swap(p, 1, "tp") for p in away]
+                kept = hidden_grad(turn, z, lse, wgt, lab, e_dev, tb, keep_at, 8, n_chip, got, keep_add)
+                turn = after(dev, kept[0])
             pieces = embed_grad(turn, z, lse, wgt, lab, ut, off, steps, n_dp)
             sent.append((off, steps, [pieces[0]] + [swap(pieces[r], r) for r in range(1, n_dp)]))
             turn = after(dev, pieces[0])
-            off += steps
-            if c == 1:
-                odd, = hidden_grad(turn, z, lse, wgt, lab, e_dev, 1, n_dp)
-                turn = after(dev, odd)
-                got = swap(odd, 1)
-            if c == 2:
-                even = hidden_grad(turn, z, lse, wgt, lab, e_dev, 0, n_dp, got)
-                turn = after(dev, even[0])
-        part = even[0]
+        both = [k + b for k, b in zip(kept, back)]
+        grad_norm = both[0]
         for c in range(1, n_chip):
-            part = part + swap(even[c], 2 * c)
-        grad_norm = part + swap(part, 1, "tp")
-        for off, steps, pieces in sent:
-            out = place(turn, pieces, out, off, steps, vocab_loc, nblk)
-            turn = dev
-
-        inv_rms = lax.rsqrt(jnp.mean(x_full * x_full, axis=-1, keepdims=True) + EPSILON)
-        x_hat = x_full * inv_rms
-        own = mask_all[0] * (log_norm[0] - stat[2, 0]) * (1.0 / n_tp)
-        sums = lax.psum(jnp.concatenate([jnp.sum(grad_norm * x_hat, axis=0) * (1.0 / n_tp), jnp.sum(own)[None]]), ("tp", "dp"))
-        grad_gain, loss_value = sums[:hid], sums[hid] / mask_count
+            grad_norm = grad_norm + swap(both[c], 2 * c)
+
+        x_half = lax.dynamic_slice_in_dim(hidden.reshape(tokens, hid), plane * half, half).astype(jnp.float32)
+        inv_rms = lax.rsqrt(jnp.mean(x_half * x_half, axis=-1, keepdims=True) + EPSILON)
+        x_hat = x_half * inv_rms
         a = grad_norm * gain32
-        grad_hidden = inv_rms * (a - x_hat * jnp.mean(a * x_hat, axis=-1, keepdims=True))
+        dh_half = inv_rms * (a - x_hat * jnp.mean(a * x_hat, axis=-1, keepdims=True))
+        dh_other = swap(dh_half, 1, "tp")
+        grad_hidden = jnp.where(plane == 0, jnp.concatenate([dh_half, dh_other]), jnp.concatenate([dh_other, dh_half]))
+        own = jnp.sum(mask_all[0] * (log_norm[0] - stat[2, 0])) * (1.0 / n_tp)
+        sums = jnp.concatenate([jnp.sum(grad_norm * x_hat, axis=0), own[None]])[None]
+        for axis, mask in (("tp", 1), ("dp", 1), ("dp", 2), ("dp", 4)):
+            sums = sums + swap(sums, mask, axis)
+
+        out = None
+        for c, (off, steps, pieces) in enumerate(sent):
+            ragged = n_dp * nblk * VB - (nblk // 2 - off - steps) * 2 * VB > vocab_loc
+            turn = dev if c < len(sent) - 1 else after(dev, grad_hidden, sums)
+            out = (place if ragged else place_copy)(turn, pieces, out, off, steps, vocab_loc, nblk)
+
+        grad_gain, loss_value = sums[0, :hid], sums[0, hid] / mask_count
         return loss_value, grad_hidden.reshape(n_seq, seq_len, hid), out.T, grad_gain
 
     return jax.shard_map(

time: 1180 us -> 1250 us (1.059)
  waiting for transfers between devices: 437 us -> 531 us
  blocking collectives: 32 us -> 0 us
    ppermute x44 -> x52, waiting for transfers between devices: 437 us -> 531 us  [swap(): return lax.ppermute(x, axis, [(i, i ^ mask) for i in range(size)])]
    pallas_call x4 -> x1, Pallas kernels: 93.7 us -> 20.7 us  [place(): pl.pallas_call(functools.partial(place_kernel, n_dp, per, off, last), gri...]
    psum x1 -> x0, blocking collectives: 32 us -> none  [local_step(): lax.psum(jnp.concatenate([jnp.sum(grad_norm * x_hat, axis=0) * (1.0 / n_t...]
    pallas_call x4, Pallas kernels: 162 us -> 187 us  [embed_grad(): pl.pallas_call(functools.partial(embed_grad_kernel, nblk, off, n_dp), gri...]
    pallas_call x0 -> x3, Pallas kernels: none -> 20.8 us  [place_copy(): pl.pallas_call(functools.partial(place_copy_kernel, n_dp, nblk // 2, off)...]
    pallas_call x2 -> x3, Pallas kernels: 160 us -> 174 us  [hidden_grad(): pl.pallas_call(functools.partial(hidden_grad_kernel, nblk, 19, n_out), gr...]
    ppermute x44 -> x52, starting transfers between devices: 44.8 us -> 47.6 us  [swap(): return lax.ppermute(x, axis, [(i, i ^ mask) for i in range(size)])]
  transfers between devices with their start and end apart: 44 -> 52, of which waited for: 16 -> 17; matrix products, arithmetic and copies ran while one was open for 1% -> 2% of each run, Pallas kernels for 35% -> 30%
where the time goes in v2:
time: 1250 us; the launch traced here: 1240 us
  Pallas kernels  603 us (48%)
  waiting for transfers between devices  531 us (42%)
  starting transfers between devices  47.6 us (4%)
  other arithmetic  30.7 us (2%)
  local copies, waits for them, and re-layouts  25.1 us (2%)
    ppermute x52, waiting for transfers between devices, swap(): return lax.ppermute(x, axis, [(i, i ^ mask) for i in range(size)])  531 us
    pallas_call x4, Pallas kernels, logits_call(): pl.pallas_call(functools.partial(logit_kernel, vocab_loc, nblk, first), g...  201 us
    pallas_call x4, Pallas kernels, embed_grad(): pl.pallas_call(functools.partial(embed_grad_kernel, nblk, off, n_dp), gri...  187 us
    pallas_call x3, Pallas kernels, hidden_grad(): pl.pallas_call(functools.partial(hidden_grad_kernel, nblk, 19, n_out), gr...  174 us
    ppermute x52, starting transfers between devices, swap(): return lax.ppermute(x, axis, [(i, i ^ mask) for i in range(size)])  47.6 us
  transfers between devices with their start and end apart: 52, of which 17 were waited for; matrix products, arithmetic and copies ran while one was open for 2% of the time, Pallas kernels for 30%

profile of v2, /device:TPU:0, one launch (start us, length us, event | category | flops | bytes accessed | tf_op | source)
XLA Modules:
  0.0 1243.1 jit_solution(15854666815273434661)
XLA Ops:
  0.7 1.5 bitcast_convert_fusion
  2.5 3.2 collective-permute-start.5
  5.7 1.5 collective-permute-start.3
  7.2 59.7 %collective-permute-done.5.refs_0_ = f32[776,896]{1,0:T(8,128)} collective-permute-done((f32[776,896]{1,0:T(8,128)S(1)}, f32[776,896]{1,0:T(8,128)}, u32[]{:S(2)}, u32[]{:S(2)}) %collective-permute-start.5) | collective-permute-done | bytes 2781216 | tf_op jit(solution)/shard_map/ppermute | solution.py:355
  68.2 59.0 %collective-permute-done.3.refs_0_ = f32[776,896]{1,0:T(8,128)} collective-permute-done((f32[776,896]{1,0:T(8,128)S(1)}, f32[776,896]{1,0:T(8,128)}, u32[]{:S(2)}, u32[]{:S(2)}) %collective-permute-start.3) | collective-permute-done | bytes 2781216 | tf_op jit(solution)/shard_map/ppermute | solution.py:355
  127.2 51.5 %logits.4 = (f32[38,6144,256]{2,1,0:T(8,128)}, bf16[896,6144]{1,0:T(8,128)(2,1)}, s32[6144,128]{1,0:T(8,128)}, f32[8,1536]{1,0:T(8,128)}, bf16[9728,896]{1,0:T(8,128)(2,1)}) custom-call(s32[2]{0:T(128)} %pad_add_fusion.d_ref, f32[776,896]{1,0:T(8,128)} %copy-done.19, f32[776,896]{1,0:T(8,128)} %collective-permute-done.2.refs_1_, s32[1]{0:T(128)} %bitcast.3.refs_2_, ...), custom_call_target="tpu_custom_call" | custom-call | flops 26776436736 | bytes 59768832 | tf_op jit(solution)/shard_map/logits/pallas_call | solution.py:117
  179.9 49.6 %logits.5 = (f32[38,6144,256]{2,1,0:T(8,128)}, bf16[896,6144]{1,0:T(8,128)(2,1)}, s32[6144,128]{1,0:T(8,128)}, f32[8,1536]{1,0:T(8,128)}) custom-call(s32[2]{0:T(128)} %pad_add_fusion.d_ref, f32[776,896]{1,0:T(8,128)} %collective-permute-done.5.refs_0_, ...), custom_call_target="tpu_custom_call", output_to_operand_aliasing={{0}: (6, {}), {1}: (7, {}), {2}: (8, {})} | custom-call | flops 26776436736 | bytes 59768832 | tf_op jit(solution)/shard_map/logits/pallas_call | solution.py:117
  230.4 50.1 %logits.6 = (f32[38,6144,256]{2,1,0:T(8,128)}, bf16[896,6144]{1,0:T(8,128)(2,1)}, s32[6144,128]{1,0:T(8,128)}, f32[8,1536]{1,0:T(8,128)}) custom-call(s32[2]{0:T(128)} %pad_add_fusion.d_ref, f32[776,896]{1,0:T(8,128)} %collective-permute-done.3.refs_0_, ...), custom_call_target="tpu_custom_call", output_to_operand_aliasing={{0}: (6, {}), {1}: (7, {}), {2}: (8, {})} | custom-call | flops 26776436736 | bytes 59768832 | tf_op jit(solution)/shard_map/logits/pallas_call | solution.py:117
  281.2 49.7 %logits.7 = (f32[38,6144,256]{2,1,0:T(8,128)}, bf16[896,6144]{1,0:T(8,128)(2,1)}, s32[6144,128]{1,0:T(8,128)}, f32[8,1536]{1,0:T(8,128)}) custom-call(s32[2]{0:T(128)} %pad_add_fusion.d_ref, f32[776,896]{1,0:T(8,128)} %collective-permute-done.refs_0_, ...), custom_call_target="tpu_custom_call", output_to_operand_aliasing={{0}: (6, {}), {1}: (7, {}), {2}: (8, {})} | custom-call | flops 26776436736 | bytes 59768832 | tf_op jit(solution)/shard_map/logits/pallas_call | solution.py:117
  333.8 1.4 slice_reduce_fusion.4
  335.3 3.2 collective-permute-done.8
  339.2 1.6 collective-permute-start.9
  340.8 1.5 slice_reduce_fusion.6
  345.5 1.6 collective-permute-start.10
  347.2 2.7 collective-permute-done.10
  350.6 2.3 broadcast_in_dim.12.w_ref
  352.9 2.2 broadcast_in_dim.11.lse_ref
  355.0 34.2 %embed_grad.4 = (f32[112,1536]{1,0:T(8,128)}, f32[112,1536]{1,0:T(8,128)}, f32[112,1536]{1,0:T(8,128)}, f32[112,1536]{1,0:T(8,128)}, f32[112,1536]{1,0:T(8,128)}...) custom-call(s32[2]{0:T(128)} %pad_add_fusion.d_ref, f32[38,6144,256]{2,1,0:T(8,128)} %get-tuple-element.78.z_ref, ...), custom_call_target="tpu_custom_call" | custom-call | flops 16911433728 | bytes 37748736 | tf_op jit(solution)/shard_map/embed_grad/pallas_call | solution.py:246
  389.2 62.8 %embed_grad.5 = (f32[112,3584]{1,0:T(8,128)}, f32[112,3584]{1,0:T(8,128)}, f32[112,3584]{1,0:T(8,128)}, f32[112,3584]{1,0:T(8,128)}, f32[112,3584]{1,0:T(8,128)}...) custom-call(s32[2]{0:T(128)} %pad_add_fusion.d_ref, f32[38,6144,256]{2,1,0:T(8,128)} %get-tuple-element.78.z_ref, ...), custom_call_target="tpu_custom_call" | custom-call | flops 39460012032 | bytes 88080384 | tf_op jit(solution)/shard_map/embed_grad/pallas_call | solution.py:246
  452.0 79.3 %hidden_grad.3 = f32[3072,896]{1,0:T(8,128)} custom-call(s32[2]{0:T(128)} %pad_add_fusion.d_ref, f32[38,6144,256]{2,1,0:T(8,128)} %get-tuple-element.78.z_ref, f32[6144,128]{1,0:T(8,128)} %broadcast_in_dim.11.lse_ref, f32[6144,128]{1,0:T(8,128)} %broadcast_in_dim.12.w_ref, s32[6144,128]{1,0:T(8,128)} %get-tuple-element.83.lab_ref, ...), custom_call_target="tpu_custom_call" | custom-call | flops 53552873472 | bytes 119537664 | tf_op jit(solution)/shard_map/hidden_grad/pallas_call | solution.py:195
  533.2 41.1 %embed_grad.6 = (f32[112,2048]{1,0:T(8,128)}, f32[112,2048]{1,0:T(8,128)}, f32[112,2048]{1,0:T(8,128)}, f32[112,2048]{1,0:T(8,128)}, f32[112,2048]{1,0:T(8,128)}...) custom-call(s32[2]{0:T(128)} %pad_add_fusion.d_ref, f32[38,6144,256]{2,1,0:T(8,128)} %get-tuple-element.78.z_ref, ...), custom_call_target="tpu_custom_call" | custom-call | flops 22548578304 | bytes 50331648 | tf_op jit(solution)/shard_map/embed_grad/pallas_call | solution.py:246
  574.4 47.2 %hidden_grad.4 = (f32[384,896]{1,0:T(8,128)}, f32[384,896]{1,0:T(8,128)}, f32[384,896]{1,0:T(8,128)}, f32[384,896]{1,0:T(8,128)}) custom-call(s32[2]{0:T(128)} %pad_add_fusion.d_ref, f32[38,6144,256]{2,1,0:T(8,128)} %get-tuple-element.78.z_ref, f32[6144,128]{1,0:T(8,128)} %broadcast_in_dim.11.lse_ref, f32[6144,128]{1,0:T(8,128)} %broadcast_in_dim.12.w_ref, ...), custom_call_target="tpu_custom_call" | custom-call | flops 26776436736 | bytes 59768832 | tf_op jit(solution)/shard_map/hidden_grad/pallas_call | solution.py:195
  621.6 1.6 collective-permute-start.13
  625.8 30.9 %collective-permute-done.48.refs_4_ = f32[112,1536]{1,0:T(8,128)S(1)} collective-permute-done((f32[112,1536]{1,0:T(8,128)S(1)}, f32[112,1536]{1,0:T(8,128)S(1)}, u32[]{:S(2)}, u32[]{:S(2)}) %collective-permute-start.48) | collective-permute-done | bytes 688160 | tf_op jit(solution)/shard_map/ppermute | solution.py:355
  657.5 27.1 %collective-permute-done.49.refs_5_ = f32[112,1536]{1,0:T(8,128)S(1)} collective-permute-done((f32[112,1536]{1,0:T(8,128)S(1)}, f32[112,1536]{1,0:T(8,128)S(1)}, u32[]{:S(2)}, u32[]{:S(2)}) %collective-permute-start.49) | collective-permute-done | bytes 688160 | tf_op jit(solution)/shard_map/ppermute | solution.py:355
  687.5 1.6 collective-permute-start.12
  689.5 47.3 %hidden_grad.5 = (f32[384,896]{1,0:T(8,128)}, f32[384,896]{1,0:T(8,128)}, f32[384,896]{1,0:T(8,128)}, f32[384,896]{1,0:T(8,128)}) custom-call(s32[2]{0:T(128)} %pad_add_fusion.d_ref, f32[38,6144,256]{2,1,0:T(8,128)} %get-tuple-element.78.z_ref, f32[6144,128]{1,0:T(8,128)} %broadcast_in_dim.11.lse_ref, f32[6144,128]{1,0:T(8,128)} %broadcast_in_dim.12.w_ref, ...), custom_call_target="tpu_custom_call" | custom-call | flops 26776436736 | bytes 59768832 | tf_op jit(solution)/shard_map/hidden_grad/pallas_call | solution.py:195
  736.7 2.7 add.140
  739.4 2.7 add.142
  742.1 1.6 collective-permute-start.14
  743.7 5.4 collective-permute-done.17
  749.4 2.7 add.144
  752.1 2.7 collective-permute-start.18
  756.7 65.3 %collective-permute-done.33.refs_3_ = f32[112,2048]{1,0:T(8,128)} collective-permute-done((f32[112,2048]{1,0:T(8,128)}, f32[112,2048]{1,0:T(8,128)}, u32[]{:S(2)}, u32[]{:S(2)}) %collective-permute-start.33) | collective-permute-done | bytes 917536 | tf_op jit(solution)/shard_map/ppermute | solution.py:355
  822.5 1.6 collective-permute-start.35
  825.0 1.6 collective-permute-start.39
  828.9 5.0 fusion.4
  833.9 11.6 collective-permute-done.34.refs_4_
  845.5 1.6 collective-permute-start.19
  847.1 17.6 %collective-permute-done.35.refs_5_ = f32[112,2048]{1,0:T(8,128)} collective-permute-done((f32[112,2048]{1,0:T(8,128)}, f32[112,2048]{1,0:T(8,128)}, u32[]{:S(2)}, u32[]{:S(2)}) %collective-permute-start.35) | collective-permute-done | bytes 917536 | tf_op jit(solution)/shard_map/ppermute | solution.py:355
  865.8 1.5 collective-permute-start.37
  867.3 50.0 %collective-permute-done.36.refs_6_ = f32[112,2048]{1,0:T(8,128)S(1)} collective-permute-done((f32[112,2048]{1,0:T(8,128)S(1)}, f32[112,2048]{1,0:T(8,128)S(1)}, u32[]{:S(2)}, u32[]{:S(2)}) %collective-permute-start.36) | collective-permute-done | bytes 917536 | tf_op jit(solution)/shard_map/ppermute | solution.py:355
  917.3 1.4 collective-permute-start.41
  918.7 16.9 %collective-permute-done.37.refs_7_ = f32[112,2048]{1,0:T(8,128)S(1)} collective-permute-done((f32[112,2048]{1,0:T(8,128)S(1)}, f32[112,2048]{1,0:T(8,128)S(1)}, u32[]{:S(2)}, u32[]{:S(2)}) %collective-permute-start.37) | collective-permute-done | bytes 917536 | tf_op jit(solution)/shard_map/ppermute | solution.py:355
  935.6 1.8 collective-permute-start.42
  937.4 1.5 collective-permute-start.43
  940.5 48.4 %embed_grad.7 = (f32[112,2560]{1,0:T(8,128)}, f32[112,2560]{1,0:T(8,128)}, f32[112,2560]{1,0:T(8,128)}, f32[112,2560]{1,0:T(8,128)}, f32[112,2560]{1,0:T(8,128)}...) custom-call(s32[2]{0:T(128)} %pad_add_fusion.d_ref, f32[38,6144,256]{2,1,0:T(8,128)} %get-tuple-element.78.z_ref, ...), custom_call_target="tpu_custom_call" | custom-call | flops 28185722880 | bytes 62914560 | tf_op jit(solution)/shard_map/embed_grad/pallas_call | solution.py:246
  988.9 50.7 %collective-permute-done.41.refs_4_ = f32[112,3584]{1,0:T(8,128)} collective-permute-done((f32[112,3584]{1,0:T(8,128)}, f32[112,3584]{1,0:T(8,128)}, u32[]{:S(2)}, u32[]{:S(2)}) %collective-permute-start.41) | collective-permute-done | bytes 1605664 | tf_op jit(solution)/shard_map/ppermute | solution.py:355
  1039.7 34.2 %collective-permute-done.42.refs_5_ = f32[112,3584]{1,0:T(8,128)} collective-permute-done((f32[112,3584]{1,0:T(8,128)}, f32[112,3584]{1,0:T(8,128)}, u32[]{:S(2)}, u32[]{:S(2)}) %collective-permute-start.42) | collective-permute-done | bytes 1605664 | tf_op jit(solution)/shard_map/ppermute | solution.py:355
  1073.9 1.7 collective-permute-start.25
  1075.6 1.5 collective-permute-start.21
  1077.1 3.0 fusion.6
  1080.1 46.0 %collective-permute-done.21 = f32[1,897]{1,0:T(1,128)S(1)} collective-permute-done((f32[1,897]{1,0:T(1,128)S(1)}, f32[1,897]{1,0:T(1,128)S(1)}, u32[]{:S(2)}, u32[]{:S(2)}) %collective-permute-start.21) | collective-permute-done | bytes 3620 | tf_op jit(solution)/shard_map/ppermute | solution.py:355
  1126.0 1.6 collective-permute-start.23
  1127.6 1.7 collective-permute-start.22
  1132.8 2.6 collective-permute-start.29
  1135.5 1.4 collective-permute-start.30
  1142.4 4.4 shard_map.84.refs_8_
  1146.8 9.2 shard_map.85.refs_8_
  1156.0 20.7 %place.1.refs_8_ = f32[112,75968]{1,0:T(8,128)} custom-call(s32[2]{0:T(128)} %pad_add_fusion.d_ref, f32[112,2048]{1,0:T(8,128)} %get-tuple-element.90.refs_0_, f32[112,2048]{1,0:T(8,128)} %collective-permute-done.31.refs_1_, f32[112,2048]{1,0:T(8,128)} %collective-permute-done.32.refs_2_, ...), custom_call_target="tpu_custom_call", output_to_operand_aliasing={{}: (9, {})} | custom-call | flops 1835008 | bytes 14680064 | tf_op jit(solution)/shard_map/place/pallas_call | solution.py:335
  1177.9 30.1 %collective-permute-done.27.refs_4_ = f32[112,2560]{1,0:T(8,128)} collective-permute-done((f32[112,2560]{1,0:T(8,128)}, f32[112,2560]{1,0:T(8,128)}, u32[]{:S(2)}, u32[]{:S(2)}) %collective-permute-start.27) | collective-permute-done | bytes 1146912 | tf_op jit(solution)/shard_map/ppermute | solution.py:355
  1208.0 20.1 %collective-permute-done.28.refs_5_ = f32[112,2560]{1,0:T(8,128)} collective-permute-done((f32[112,2560]{1,0:T(8,128)}, f32[112,2560]{1,0:T(8,128)}, u32[]{:S(2)}, u32[]{:S(2)}) %collective-permute-start.28) | collective-permute-done | bytes 1146912 | tf_op jit(solution)/shard_map/ppermute | solution.py:355
  1229.4 7.2 shard_map.86
  1237.2 4.5 maximum_select_fusion
  (227 shorter events, 37.1 us)
Async XLA Ops:
  2.2 65.3 %copy-start.39 = (bf16[896]{0:T(1024)(128)(2,1)S(1)}, bf16[896]{0:T(1024)(128)(2,1)}, u32[]{:S(2)}) copy-start(bf16[896]{0:T(1024)(128)(2,1)} %param.8) | copy-start | bytes 5380
  2.4 124.7 %copy-start.19 = (f32[776,896]{1,0:T(8,128)}, f32[776,896]{1,0:T(8,128)S(1)}, u32[]{:S(2)}) copy-start(f32[776,896]{1,0:T(8,128)S(1)} %select_maximum_fusion.refs_0_) | copy-start | bytes 8343556
  2.5 64.5 %collective-permute-start.5 = (f32[776,896]{1,0:T(8,128)S(1)}, f32[776,896]{1,0:T(8,128)}, u32[]{:S(2)}, u32[]{:S(2)}) collective-permute-start(f32[776,896]{1,0:T(8,128)S(1)} %select_maximum_fusion.refs_0_), channel_id=1, source_target_pairs={{0,2},{1,3},{2,0},{3,1},{4,6},{5,7},{6,4},{7,5},{8,10},{9,11},{10,... | collective-permute-start | bytes 8343560 | tf_op jit(solution)/shard_map/ppermute | solution.py:355
  5.7 121.5 %collective-permute-start.3 = (f32[776,896]{1,0:T(8,128)S(1)}, f32[776,896]{1,0:T(8,128)}, u32[]{:S(2)}, u32[]{:S(2)}) collective-permute-start(f32[776,896]{1,0:T(8,128)S(1)} %select_maximum_fusion.refs_0_), channel_id=1, source_target_pairs={{0,4},{1,5},{2,6},{3,7},{4,0},{5,1},{6,2},{7,3},{8,12},{9,13},{10,... | collective-permute-start | bytes 8343560 | tf_op jit(solution)/shard_map/ppermute | solution.py:355
  7.2 119.9 %collective-permute-start.2 = (f32[776,896]{1,0:T(8,128)S(1)}, f32[776,896]{1,0:T(8,128)}, u32[]{:S(2)}, u32[]{:S(2)}) collective-permute-start(f32[776,896]{1,0:T(8,128)S(1)} %select_maximum_fusion.refs_0_), channel_id=1, source_target_pairs={{0,1},{1,0},{2,3},{3,2},{4,5},{5,4},{6,7},{7,6},{8,9},{9,8},{10,11... | collective-permute-start | bytes 8343560 | tf_op jit(solution)/shard_map/ppermute | solution.py:355
  7.2 172.2 %collective-permute-start = (f32[776,896]{1,0:T(8,128)S(1)}, f32[776,896]{1,0:T(8,128)}, u32[]{:S(2)}, u32[]{:S(2)}) collective-permute-start(f32[776,896]{1,0:T(8,128)S(1)} %select_maximum_fusion.refs_0_), channel_id=1, source_target_pairs={{0,6},{1,7},{2,4},{3,5},{4,2},{5,3},{6,0},{7,1},{8,14},{9,15},{10,... | collective-permute-start | bytes 8343560 | tf_op jit(solution)/shard_map/ppermute | solution.py:355
  66.9 113.0 %collective-permute-start.6 = (f32[776,896]{1,0:T(8,128)}, f32[776,896]{1,0:T(8,128)}, u32[]{:S(2)}, u32[]{:S(2)}) collective-permute-start(f32[776,896]{1,0:T(8,128)} %collective-permute-done.5.refs_0_), channel_id=1, source_target_pairs={{0,1},{1,0},{2,3},{3,2},{4,5},{5,4},{6,7},{7,6},{8,9},{9,8},{10,11... | collective-permute-start | bytes 8343560 | tf_op jit(solution)/shard_map/ppermute | solution.py:355
  127.1 103.2 %collective-permute-start.4 = (f32[776,896]{1,0:T(8,128)}, f32[776,896]{1,0:T(8,128)}, u32[]{:S(2)}, u32[]{:S(2)}) collective-permute-start(f32[776,896]{1,0:T(8,128)} %collective-permute-done.3.refs_0_), channel_id=1, source_target_pairs={{0,1},{1,0},{2,3},{3,2},{4,5},{5,4},{6,7},{7,6},{8,9},{9,8},{10,11... | collective-permute-start | bytes 8343560 | tf_op jit(solution)/shard_map/ppermute | solution.py:355
  179.4 101.8 %collective-permute-start.1 = (f32[776,896]{1,0:T(8,128)}, f32[776,896]{1,0:T(8,128)}, u32[]{:S(2)}, u32[]{:S(2)}) collective-permute-start(f32[776,896]{1,0:T(8,128)} %collective-permute-done.refs_0_), channel_id=1, source_target_pairs={{0,1},{1,0},{2,3},{3,2},{4,5},{5,4},{6,7},{7,6},{8,9},{9,8},{10,11... | collective-permute-start | bytes 8343560 | tf_op jit(solution)/shard_map/ppermute | solution.py:355
  332.0 1.5 collective-permute-start.7
  333.8 4.7 collective-permute-start.8
  339.2 5.6 collective-permute-start.9
  345.5 4.4 collective-permute-start.10
  531.3 43.0 %collective-permute-start.11 = (f32[3072,896]{1,0:T(8,128)}, f32[3072,896]{1,0:T(8,128)}, u32[]{:S(2)}, u32[]{:S(2)}) collective-permute-start(f32[3072,896]{1,0:T(8,128)} %hidden_grad.3), channel_id=1, source_target_pairs={{0,1},{1,0},{2,3},{3,2},{4,5},{5,4},{6,7},{7,6},{8,9},{9,8},{10,11... | collective-permute-start | bytes 33030152 | tf_op jit(solution)/shard_map/ppermute | solution.py:355
  531.3 92.3 %collective-permute-start.45 = (f32[112,1536]{1,0:T(8,128)}, f32[112,1536]{1,0:T(8,128)}, u32[]{:S(2)}, u32[]{:S(2)}) collective-permute-start(f32[112,1536]{1,0:T(8,128)} %get-tuple-element.125), channel_id=1, source_target_pairs={{0,1},{1,0},{2,3},{3,2},{4,5},{5,4},{6,7},{7,6},{8,9},{9,8},{10,11... | collective-permute-start | bytes 2064392 | tf_op jit(solution)/shard_map/ppermute | solution.py:355
  531.8 92.3 %collective-permute-start.46 = (f32[112,1536]{1,0:T(8,128)}, f32[112,1536]{1,0:T(8,128)}, u32[]{:S(2)}, u32[]{:S(2)}) collective-permute-start(f32[112,1536]{1,0:T(8,128)} %get-tuple-element.126), channel_id=1, source_target_pairs={{0,2},{1,3},{2,0},{3,1},{4,6},{5,7},{6,4},{7,5},{8,10},{9,11},{10,... | collective-permute-start | bytes 2064392 | tf_op jit(solution)/shard_map/ppermute | solution.py:355
  532.3 92.9 %collective-permute-start.47 = (f32[112,1536]{1,0:T(8,128)}, f32[112,1536]{1,0:T(8,128)}, u32[]{:S(2)}, u32[]{:S(2)}) collective-permute-start(f32[112,1536]{1,0:T(8,128)} %get-tuple-element.127), channel_id=1, source_target_pairs={{0,3},{1,2},{2,1},{3,0},{4,7},{5,6},{6,5},{7,4},{8,11},{9,10},{10,... | collective-permute-start | bytes 2064392 | tf_op jit(solution)/shard_map/ppermute | solution.py:355
  574.3 49.3 %copy-start.48 = (f32[112,1536]{1,0:T(8,128)S(1)}, f32[112,1536]{1,0:T(8,128)}, u32[]{:S(2)}) copy-start(f32[112,1536]{1,0:T(8,128)} %get-tuple-element.128) | copy-start | bytes 2064388
  574.3 49.8 %copy-start.47 = (f32[112,1536]{1,0:T(8,128)S(1)}, f32[112,1536]{1,0:T(8,128)}, u32[]{:S(2)}) copy-start(f32[112,1536]{1,0:T(8,128)} %get-tuple-element.129) | copy-start | bytes 2064388
  574.3 50.9 %copy-start.46 = (f32[112,1536]{1,0:T(8,128)S(1)}, f32[112,1536]{1,0:T(8,128)}, u32[]{:S(2)}) copy-start(f32[112,1536]{1,0:T(8,128)} %get-tuple-element.130) | copy-start | bytes 2064388
  574.3 83.2 %copy-start.45 = (f32[112,1536]{1,0:T(8,128)S(1)}, f32[112,1536]{1,0:T(8,128)}, u32[]{:S(2)}) copy-start(f32[112,1536]{1,0:T(8,128)} %get-tuple-element.131) | copy-start | bytes 2064388
  621.6 65.9 %collective-permute-start.13 = (f32[384,896]{1,0:T(8,128)}, f32[384,896]{1,0:T(8,128)S(1)}, u32[]{:S(2)}, u32[]{:S(2)}) collective-permute-start(f32[384,896]{1,0:T(8,128)} %get-tuple-element.96), channel_id=1, source_target_pairs={{0,8},{8,0},{1,9},{9,1},{2,10},{10,2},{3,11},{11,3},{4,12},{12,4},... | collective-permute-start | bytes 4128776 | tf_op jit(solution)/shard_map/ppermute | solution.py:355
  623.1 65.9 %collective-permute-start.15 = (f32[384,896]{1,0:T(8,128)}, f32[384,896]{1,0:T(8,128)}, u32[]{:S(2)}, u32[]{:S(2)}) collective-permute-start(f32[384,896]{1,0:T(8,128)} %get-tuple-element.98), channel_id=1, source_target_pairs={{0,8},{8,0},{1,9},{9,1},{2,10},{10,2},{3,11},{11,3},{4,12},{12,4},... | collective-permute-start | bytes 4128776 | tf_op jit(solution)/shard_map/ppermute | solution.py:355
  623.6 33.1 %collective-permute-start.48 = (f32[112,1536]{1,0:T(8,128)S(1)}, f32[112,1536]{1,0:T(8,128)S(1)}, u32[]{:S(2)}, u32[]{:S(2)}) collective-permute-start(f32[112,1536]{1,0:T(8,128)S(1)} %copy-done.48), channel_id=1, source_target_pairs={{0,4},{1,5},{2,6},{3,7},{4,0},{5,1},{6,2},{7,3},{8,12},{9,13},{10,... | collective-permute-start | bytes 2064392 | tf_op jit(solution)/shard_map/ppermute | solution.py:355
  624.1 60.6 %collective-permute-start.49 = (f32[112,1536]{1,0:T(8,128)S(1)}, f32[112,1536]{1,0:T(8,128)S(1)}, u32[]{:S(2)}, u32[]{:S(2)}) collective-permute-start(f32[112,1536]{1,0:T(8,128)S(1)} %copy-done.47), channel_id=1, source_target_pairs={{0,5},{1,4},{2,7},{3,6},{4,1},{5,0},{6,3},{7,2},{8,13},{9,12},{10,... | collective-permute-start | bytes 2064392 | tf_op jit(solution)/shard_map/ppermute | solution.py:355
  625.2 60.9 %collective-permute-start.50 = (f32[112,1536]{1,0:T(8,128)S(1)}, f32[112,1536]{1,0:T(8,128)S(1)}, u32[]{:S(2)}, u32[]{:S(2)}) collective-permute-start(f32[112,1536]{1,0:T(8,128)S(1)} %copy-done.46), channel_id=1, source_target_pairs={{0,6},{1,7},{2,4},{3,5},{4,2},{5,3},{6,0},{7,1},{8,14},{9,15},{10,... | collective-permute-start | bytes 2064392 | tf_op jit(solution)/shard_map/ppermute | solution.py:355
  657.5 84.6 %collective-permute-start.51 = (f32[112,1536]{1,0:T(8,128)S(1)}, f32[112,1536]{1,0:T(8,128)S(1)}, u32[]{:S(2)}, u32[]{:S(2)}) collective-permute-start(f32[112,1536]{1,0:T(8,128)S(1)} %copy-done.45), channel_id=1, source_target_pairs={{0,7},{1,6},{2,5},{3,4},{4,3},{5,2},{6,1},{7,0},{8,15},{9,14},{10,... | collective-permute-start | bytes 2064392 | tf_op jit(solution)/shard_map/ppermute | solution.py:355
  685.5 66.6 %collective-permute-start.31 = (f32[112,2048]{1,0:T(8,128)}, f32[112,2048]{1,0:T(8,128)}, u32[]{:S(2)}, u32[]{:S(2)}) collective-permute-start(f32[112,2048]{1,0:T(8,128)} %get-tuple-element.111), channel_id=1, source_target_pairs={{0,1},{1,0},{2,3},{3,2},{4,5},{5,4},{6,7},{7,6},{8,9},{9,8},{10,11... | collective-permute-start | bytes 2752520 | tf_op jit(solution)/shard_map/ppermute | solution.py:355
  687.0 67.8 %collective-permute-start.32 = (f32[112,2048]{1,0:T(8,128)}, f32[112,2048]{1,0:T(8,128)}, u32[]{:S(2)}, u32[]{:S(2)}) collective-permute-start(f32[112,2048]{1,0:T(8,128)} %get-tuple-element.112), channel_id=1, source_target_pairs={{0,2},{1,3},{2,0},{3,1},{4,6},{5,7},{6,4},{7,5},{8,10},{9,11},{10,... | collective-permute-start | bytes 2752520 | tf_op jit(solution)/shard_map/ppermute | solution.py:355
  687.5 135.0 %collective-permute-start.12 = (f32[384,896]{1,0:T(8,128)}, f32[384,896]{1,0:T(8,128)S(1)}, u32[]{:S(2)}, u32[]{:S(2)}) collective-permute-start(f32[384,896]{1,0:T(8,128)} %get-tuple-element.92), channel_id=1, source_target_pairs={{0,8},{8,0},{1,9},{9,1},{2,10},{10,2},{3,11},{11,3},{4,12},{12,4},... | collective-permute-start | bytes 4128776 | tf_op jit(solution)/shard_map/ppermute | solution.py:355
  689.1 60.0 %collective-permute-start.17 = (f32[384,896]{1,0:T(8,128)}, f32[384,896]{1,0:T(8,128)}, u32[]{:S(2)}, u32[]{:S(2)}) collective-permute-start(f32[384,896]{1,0:T(8,128)} %get-tuple-element.100), channel_id=1, source_target_pairs={{0,8},{8,0},{1,9},{9,1},{2,10},{10,2},{3,11},{11,3},{4,12},{12,4},... | collective-permute-start | bytes 4128776 | tf_op jit(solution)/shard_map/ppermute | solution.py:355
  742.1 82.8 %collective-permute-start.14 = (f32[384,896]{1,0:T(8,128)}, f32[384,896]{1,0:T(8,128)}, u32[]{:S(2)}, u32[]{:S(2)}) collective-permute-start(f32[384,896]{1,0:T(8,128)} %add.140), channel_id=1, source_target_pairs={{0,2},{1,3},{2,0},{3,1},{4,6},{5,7},{6,4},{7,5},{8,10},{9,11},{10,... | collective-permute-start | bytes 4128776 | tf_op jit(solution)/shard_map/ppermute | solution.py:355
  749.1 76.0 %collective-permute-start.16 = (f32[384,896]{1,0:T(8,128)}, f32[384,896]{1,0:T(8,128)}, u32[]{:S(2)}, u32[]{:S(2)}) collective-permute-start(f32[384,896]{1,0:T(8,128)} %add.142), channel_id=1, source_target_pairs={{0,4},{1,5},{2,6},{3,7},{4,0},{5,1},{6,2},{7,3},{8,12},{9,13},{10,... | collective-permute-start | bytes 4128776 | tf_op jit(solution)/shard_map/ppermute | solution.py:355
  752.1 74.5 %collective-permute-start.18 = (f32[384,896]{1,0:T(8,128)}, f32[384,896]{1,0:T(8,128)}, u32[]{:S(2)}, u32[]{:S(2)}) collective-permute-start(f32[384,896]{1,0:T(8,128)} %add.144), channel_id=1, source_target_pairs={{0,6},{1,7},{2,4},{3,5},{4,2},{5,3},{6,0},{7,1},{8,14},{9,15},{10,... | collective-permute-start | bytes 4128776 | tf_op jit(solution)/shard_map/ppermute | solution.py:355
  754.8 67.1 %collective-permute-start.33 = (f32[112,2048]{1,0:T(8,128)}, f32[112,2048]{1,0:T(8,128)}, u32[]{:S(2)}, u32[]{:S(2)}) collective-permute-start(f32[112,2048]{1,0:T(8,128)} %get-tuple-element.113), channel_id=1, source_target_pairs={{0,3},{1,2},{2,1},{3,0},{4,7},{5,6},{6,5},{7,4},{8,11},{9,10},{10,... | collective-permute-start | bytes 2752520 | tf_op jit(solution)/shard_map/ppermute | solution.py:355
  822.0 23.5 %collective-permute-start.34 = (f32[112,2048]{1,0:T(8,128)}, f32[112,2048]{1,0:T(8,128)}, u32[]{:S(2)}, u32[]{:S(2)}) collective-permute-start(f32[112,2048]{1,0:T(8,128)} %get-tuple-element.114), channel_id=1, source_target_pairs={{0,4},{1,5},{2,6},{3,7},{4,0},{5,1},{6,2},{7,3},{8,12},{9,13},{10,... | collective-permute-start | bytes 2752520 | tf_op jit(solution)/shard_map/ppermute | solution.py:355
  822.5 42.2 %collective-permute-start.35 = (f32[112,2048]{1,0:T(8,128)}, f32[112,2048]{1,0:T(8,128)}, u32[]{:S(2)}, u32[]{:S(2)}) collective-permute-start(f32[112,2048]{1,0:T(8,128)} %get-tuple-element.115), channel_id=1, source_target_pairs={{0,5},{1,4},{2,7},{3,6},{4,1},{5,0},{6,3},{7,2},{8,13},{9,12},{10,... | collective-permute-start | bytes 2752520 | tf_op jit(solution)/shard_map/ppermute | solution.py:355
  824.9 112.5 %collective-permute-start.38 = (f32[112,3584]{1,0:T(8,128)}, f32[112,3584]{1,0:T(8,128)S(1)}, u32[]{:S(2)}, u32[]{:S(2)}) collective-permute-start(f32[112,3584]{1,0:T(8,128)} %get-tuple-element.118), channel_id=1, source_target_pairs={{0,1},{1,0},{2,3},{3,2},{4,5},{5,4},{6,7},{7,6},{8,9},{9,8},{10,11... | collective-permute-start | bytes 4816904 | tf_op jit(solution)/shard_map/ppermute | solution.py:355
  825.0 113.9 %collective-permute-start.39 = (f32[112,3584]{1,0:T(8,128)}, f32[112,3584]{1,0:T(8,128)S(1)}, u32[]{:S(2)}, u32[]{:S(2)}) collective-permute-start(f32[112,3584]{1,0:T(8,128)} %get-tuple-element.119), channel_id=1, source_target_pairs={{0,2},{1,3},{2,0},{3,1},{4,6},{5,7},{6,4},{7,5},{8,10},{9,11},{10,... | collective-permute-start | bytes 4816904 | tf_op jit(solution)/shard_map/ppermute | solution.py:355
  826.6 113.3 %collective-permute-start.40 = (f32[112,3584]{1,0:T(8,128)}, f32[112,3584]{1,0:T(8,128)}, u32[]{:S(2)}, u32[]{:S(2)}) collective-permute-start(f32[112,3584]{1,0:T(8,128)} %get-tuple-element.120), channel_id=1, source_target_pairs={{0,3},{1,2},{2,1},{3,0},{4,7},{5,6},{6,5},{7,4},{8,11},{9,10},{10,... | collective-permute-start | bytes 4816904 | tf_op jit(solution)/shard_map/ppermute | solution.py:355
  828.9 36.9 %copy-start.43 = (f32[112,2048]{1,0:T(8,128)S(1)}, f32[112,2048]{1,0:T(8,128)}, u32[]{:S(2)}) copy-start(f32[112,2048]{1,0:T(8,128)} %get-tuple-element.117) | copy-start | bytes 2752516
  845.5 20.3 %collective-permute-start.19 = (f32[1,897]{1,0:T(1,128)S(1)}, f32[1,897]{1,0:T(1,128)S(1)}, u32[]{:S(2)}, u32[]{:S(2)}) collective-permute-start(f32[1,897]{1,0:T(1,128)S(1)} %bitcast.92), channel_id=1, source_target_pairs={{0,8},{8,0},{1,9},{9,1},{2,10},{10,2},{3,11},{11,3},{4,12},{12,4},... | collective-permute-start | bytes 10772 | tf_op jit(solution)/shard_map/ppermute | solution.py:355
  864.7 52.6 %collective-permute-start.36 = (f32[112,2048]{1,0:T(8,128)S(1)}, f32[112,2048]{1,0:T(8,128)S(1)}, u32[]{:S(2)}, u32[]{:S(2)}) collective-permute-start(f32[112,2048]{1,0:T(8,128)S(1)} %copy-done.44), channel_id=1, source_target_pairs={{0,6},{1,7},{2,4},{3,5},{4,2},{5,3},{6,0},{7,1},{8,14},{9,15},{10,... | collective-permute-start | bytes 2752520 | tf_op jit(solution)/shard_map/ppermute | solution.py:355
  865.8 69.8 %collective-permute-start.37 = (f32[112,2048]{1,0:T(8,128)S(1)}, f32[112,2048]{1,0:T(8,128)S(1)}, u32[]{:S(2)}, u32[]{:S(2)}) collective-permute-start(f32[112,2048]{1,0:T(8,128)S(1)} %copy-done.43), channel_id=1, source_target_pairs={{0,7},{1,6},{2,5},{3,4},{4,3},{5,2},{6,1},{7,0},{8,15},{9,14},{10,... | collective-permute-start | bytes 2752520 | tf_op jit(solution)/shard_map/ppermute | solution.py:355
  917.3 122.4 %collective-permute-start.41 = (f32[112,3584]{1,0:T(8,128)}, f32[112,3584]{1,0:T(8,128)}, u32[]{:S(2)}, u32[]{:S(2)}) collective-permute-start(f32[112,3584]{1,0:T(8,128)} %get-tuple-element.121), channel_id=1, source_target_pairs={{0,4},{1,5},{2,6},{3,7},{4,0},{5,1},{6,2},{7,3},{8,12},{9,13},{10,... | collective-permute-start | bytes 4816904 | tf_op jit(solution)/shard_map/ppermute | solution.py:355
  935.6 138.3 %collective-permute-start.42 = (f32[112,3584]{1,0:T(8,128)}, f32[112,3584]{1,0:T(8,128)}, u32[]{:S(2)}, u32[]{:S(2)}) collective-permute-start(f32[112,3584]{1,0:T(8,128)} %get-tuple-element.122), channel_id=1, source_target_pairs={{0,5},{1,4},{2,7},{3,6},{4,1},{5,0},{6,3},{7,2},{8,13},{9,12},{10,... | collective-permute-start | bytes 4816904 | tf_op jit(solution)/shard_map/ppermute | solution.py:355
  937.4 138.2 %collective-permute-start.43 = (f32[112,3584]{1,0:T(8,128)}, f32[112,3584]{1,0:T(8,128)}, u32[]{:S(2)}, u32[]{:S(2)}) collective-permute-start(f32[112,3584]{1,0:T(8,128)} %get-tuple-element.123), channel_id=1, source_target_pairs={{0,6},{1,7},{2,4},{3,5},{4,2},{5,3},{6,0},{7,1},{8,14},{9,15},{10,... | collective-permute-start | bytes 4816904 | tf_op jit(solution)/shard_map/ppermute | solution.py:355
  938.9 188.7 %collective-permute-start.44 = (f32[112,3584]{1,0:T(8,128)}, f32[112,3584]{1,0:T(8,128)}, u32[]{:S(2)}, u32[]{:S(2)}) collective-permute-start(f32[112,3584]{1,0:T(8,128)} %get-tuple-element.124), channel_id=1, source_target_pairs={{0,7},{1,6},{2,5},{3,4},{4,3},{5,2},{6,1},{7,0},{8,15},{9,14},{10,... | collective-permute-start | bytes 4816904 | tf_op jit(solution)/shard_map/ppermute | solution.py:355
  939.9 135.7 %collective-permute-start.20 = (f32[1,897]{1,0:T(1,128)S(1)}, f32[1,897]{1,0:T(1,128)S(1)}, u32[]{:S(2)}, u32[]{:S(2)}) collective-permute-start(f32[1,897]{1,0:T(1,128)S(1)} %add.155), channel_id=1, source_target_pairs={{0,1},{1,0},{2,3},{3,2},{4,5},{5,4},{6,7},{7,6},{8,9},{9,8},{10,11... | collective-permute-start | bytes 10772 | tf_op jit(solution)/shard_map/ppermute | solution.py:355
  1039.7 89.7 %collective-permute-start.24 = (f32[112,2560]{1,0:T(8,128)}, f32[112,2560]{1,0:T(8,128)S(1)}, u32[]{:S(2)}, u32[]{:S(2)}) collective-permute-start(f32[112,2560]{1,0:T(8,128)} %get-tuple-element.104), channel_id=1, source_target_pairs={{0,1},{1,0},{2,3},{3,2},{4,5},{5,4},{6,7},{7,6},{8,9},{9,8},{10,11... | collective-permute-start | bytes 3440648 | tf_op jit(solution)/shard_map/ppermute | solution.py:355
  1073.9 56.8 %collective-permute-start.25 = (f32[112,2560]{1,0:T(8,128)}, f32[112,2560]{1,0:T(8,128)S(1)}, u32[]{:S(2)}, u32[]{:S(2)}) collective-permute-start(f32[112,2560]{1,0:T(8,128)} %get-tuple-element.105), channel_id=1, source_target_pairs={{0,2},{1,3},{2,0},{3,1},{4,6},{5,7},{6,4},{7,5},{8,10},{9,11},{10,... | collective-permute-start | bytes 3440648 | tf_op jit(solution)/shard_map/ppermute | solution.py:355
  1075.6 56.2 %collective-permute-start.26 = (f32[112,2560]{1,0:T(8,128)}, f32[112,2560]{1,0:T(8,128)S(1)}, u32[]{:S(2)}, u32[]{:S(2)}) collective-permute-start(f32[112,2560]{1,0:T(8,128)} %get-tuple-element.106), channel_id=1, source_target_pairs={{0,3},{1,2},{2,1},{3,0},{4,7},{5,6},{6,5},{7,4},{8,11},{9,10},{10,... | collective-permute-start | bytes 3440648 | tf_op jit(solution)/shard_map/ppermute | solution.py:355
  1075.6 50.4 %collective-permute-start.21 = (f32[1,897]{1,0:T(1,128)S(1)}, f32[1,897]{1,0:T(1,128)S(1)}, u32[]{:S(2)}, u32[]{:S(2)}) collective-permute-start(f32[1,897]{1,0:T(1,128)S(1)} %add.156), channel_id=1, source_target_pairs={{0,2},{1,3},{2,0},{3,1},{4,6},{5,7},{6,4},{7,5},{8,10},{9,11},{10,... | collective-permute-start | bytes 10772 | tf_op jit(solution)/shard_map/ppermute | solution.py:355
  1077.1 59.8 %copy-start.17 = (s32[2]{0:T(128)S(1)}, s32[2]{0:T(128)}, u32[]{:S(2)}) copy-start(s32[2]{0:T(128)} %pad_add_fusion.d_ref) | copy-start | bytes 28
  1126.0 111.1 %collective-permute-start.23 = (f32[384,896]{1,0:T(8,128)}, f32[384,896]{1,0:T(8,128)}, u32[]{:S(2)}, u32[]{:S(2)}) collective-permute-start(f32[384,896]{1,0:T(8,128)} %fusion.6), channel_id=1, source_target_pairs={{0,8},{8,0},{1,9},{9,1},{2,10},{10,2},{3,11},{11,3},{4,12},{12,4},... | collective-permute-start | bytes 4128776 | tf_op jit(solution)/shard_map/ppermute | solution.py:355
  1127.6 7.8 collective-permute-start.22
  1130.4 77.6 %collective-permute-start.27 = (f32[112,2560]{1,0:T(8,128)}, f32[112,2560]{1,0:T(8,128)}, u32[]{:S(2)}, u32[]{:S(2)}) collective-permute-start(f32[112,2560]{1,0:T(8,128)} %get-tuple-element.107), channel_id=1, source_target_pairs={{0,4},{1,5},{2,6},{3,7},{4,0},{5,1},{6,2},{7,3},{8,12},{9,13},{10,... | collective-permute-start | bytes 3440648 | tf_op jit(solution)/shard_map/ppermute | solution.py:355
  1131.7 96.4 %collective-permute-start.28 = (f32[112,2560]{1,0:T(8,128)}, f32[112,2560]{1,0:T(8,128)}, u32[]{:S(2)}, u32[]{:S(2)}) collective-permute-start(f32[112,2560]{1,0:T(8,128)} %get-tuple-element.108), channel_id=1, source_target_pairs={{0,5},{1,4},{2,7},{3,6},{4,1},{5,0},{6,3},{7,2},{8,13},{9,12},{10,... | collective-permute-start | bytes 3440648 | tf_op jit(solution)/shard_map/ppermute | solution.py:355
  1132.8 95.3 %collective-permute-start.29 = (f32[112,2560]{1,0:T(8,128)}, f32[112,2560]{1,0:T(8,128)}, u32[]{:S(2)}, u32[]{:S(2)}) collective-permute-start(f32[112,2560]{1,0:T(8,128)} %get-tuple-element.109), channel_id=1, source_target_pairs={{0,6},{1,7},{2,4},{3,5},{4,2},{5,3},{6,0},{7,1},{8,14},{9,15},{10,... | collective-permute-start | bytes 3440648 | tf_op jit(solution)/shard_map/ppermute | solution.py:355
  1135.5 92.6 %collective-permute-start.30 = (f32[112,2560]{1,0:T(8,128)}, f32[112,2560]{1,0:T(8,128)}, u32[]{:S(2)}, u32[]{:S(2)}) collective-permute-start(f32[112,2560]{1,0:T(8,128)} %get-tuple-element.110), channel_id=1, source_target_pairs={{0,7},{1,6},{2,5},{3,4},{4,3},{5,2},{6,1},{7,0},{8,15},{9,14},{10,... | collective-permute-start | bytes 3440648 | tf_op jit(solution)/shard_map/ppermute | solution.py:355
  1156.0 72.1 %copy-start.1 = (f32[112,2560]{1,0:T(8,128)S(1)}, f32[112,2560]{1,0:T(8,128)}, u32[]{:S(2)}) copy-start(f32[112,2560]{1,0:T(8,128)} %get-tuple-element.103.refs_0_) | copy-start | bytes 3440644
  1156.0 72.1 %copy-start.3 = (f32[112,2560]{1,0:T(8,128)S(1)}, f32[112,2560]{1,0:T(8,128)}, u32[]{:S(2)}) copy-start(f32[112,2560]{1,0:T(8,128)} %copy-done.2) | copy-start | bytes 3440644
  1156.0 72.1 %copy-start.5 = (f32[112,2560]{1,0:T(8,128)S(1)}, f32[112,2560]{1,0:T(8,128)}, u32[]{:S(2)}) copy-start(f32[112,2560]{1,0:T(8,128)} %copy-done.4) | copy-start | bytes 3440644
  1156.0 72.1 %copy-start.18 = (s32[2]{0:T(128)S(1)}, s32[2]{0:T(128)}, u32[]{:S(2)}) copy-start(s32[2]{0:T(128)} %pad_add_fusion.d_ref) | copy-start | bytes 28
  (37 other events, 223.4 us)

commit v3 on v2

--- a/solution.py
+++ b/solution.py
@@ -13,7 +13,7 @@
 VB = 256
 NT = (((1,), (1,)), ((), ()))
 
-CHUNKS = ((0, 3), (3, 7), (15, 4), (10, 5))
+CHUNKS = ((0, 4), (4, 7), (13, 6), (11, 2))
 
 
 def logit_kernel(vocab_loc, nblk, first, d_ref, *refs):
@@ -146,60 +146,79 @@
     return jnp.concatenate(parts, axis=1)
 
 
-def hidden_grad_kernel(nblk, inner, n_out, d_ref, z_ref, lse_ref, w_ref, lab_ref, e_ref, *rest):
+def hidden_grad_kernel(nblk, inner, n_out, d_ref, z_ref, lse_ref, w_ref, lab_ref, e_hbm, *rest):
+    acc_s, e_ref, sem = rest[-3:]
+    rest = rest[:-3]
     lse, wgt = lse_ref[...], w_ref[...]
     lab = lab_ref[...] - lax.broadcasted_iota(jnp.int32, lab_ref.shape, 1)
-    acc_s, outs = rest[-1], rest[-1 - n_out:-1]
-    acc_s[...] = rest[0][...] if len(rest) > n_out + 1 else jnp.zeros(acc_s.shape, jnp.float32)
-
-    def step(it, carry):
-        acc = None
-        for k in range(inner):
-            j = it * inner + k
-            g = grad_block(z_ref[j], lse, wgt, lab, (d_ref[0] * nblk + j) * VB)
-            e = e_ref[pl.ds(pl.multiple_of(j * VB, VB), VB), :]
-            part = jnp.dot(g, e, preferred_element_type=jnp.float32)
-            acc = part if acc is None else acc + part
-        acc_s[...] += acc
-        return carry
-
-    lax.fori_loop(0, nblk // inner, step, 0)
-    if n_out == 1:
-        outs[0][...] = acc_s[...]
-    else:
-        per = pl.num_programs(0) // n_out
-        for c in range(n_out):
-            @pl.when(pl.program_id(0) // per == c)
-            def _():
-                outs[c][...] = acc_s[...]
+    outs = rest[-n_out:]
+    i, it = pl.program_id(0), pl.program_id(1)
+    rows = inner * VB
+
+    def copy_of(k):
+        sl = pl.ds(pl.multiple_of(k * rows, rows), rows)
+        return pltpu.make_async_copy(e_hbm.at[sl, :], e_ref.at[sl, :], sem.at[k])
+
+    @pl.when((i == 0) & (it == 0))
+    def _():
+        for k in range(nblk // inner):
+            copy_of(k).start()
+
+    @pl.when(i == 0)
+    def _():
+        copy_of(it).wait()
+
+    @pl.when(it == 0)
+    def _():
+        acc_s[...] = rest[0][...] if len(rest) > n_out else jnp.zeros(acc_s.shape, jnp.float32)
+
+    acc = None
+    for k in range(inner):
+        j = it * inner + k
+        g = grad_block(z_ref[k], lse, wgt, lab, (d_ref[0] * nblk + j) * VB)
+        e = e_ref[pl.ds(pl.multiple_of(j * VB, VB), VB), :]
+        part = jnp.dot(g, e, preferred_element_type=jnp.float32)
+        acc = part if acc is None else acc + part
+    acc_s[...] += acc
+
+    per = pl.num_programs(0) // n_out
+    for c in range(n_out):
+        @pl.when((it == nblk // inner - 1) & (i // per == c))
+        def _():
+            outs[c][...] = acc_s[...]
 
 
 def hidden_grad(dev, z, lse, wgt, lab, e_dev, tb, at, steps, n_out, add=None, add_at=None):
     nblk, _, _ = z.shape
     hid = e_dev.shape[1]
     per = steps // n_out
-    wide = pl.BlockSpec((tb, 128), lambda i, d: (at(i, d), 0))
+    inner = nblk // 2
+    wide = pl.BlockSpec((tb, 128), lambda i, t, d: (at(i, d), 0))
     in_specs = [
-        pl.BlockSpec((nblk, tb, VB), lambda i, d: (0, at(i, d), 0)),
+        pl.BlockSpec((inner, tb, VB), lambda i, t, d: (t, at(i, d), 0)),
         wide, wide, wide,
-        pl.BlockSpec((nblk * VB, hid), lambda i, d: (0, 0), pipeline_mode=pl.Buffered(1)),
+        pl.BlockSpec(memory_space=pl.ANY),
     ]
     args = [dev, z, lse, wgt, lab, e_dev]
     if add is not None:
-        in_specs.append(pl.BlockSpec((tb, hid), lambda i, d: (add_at(i, d), 0)))
+        in_specs.append(pl.BlockSpec((tb, hid), lambda i, t, d: (add_at(i, d), 0)))
         args.append(add)
     out_specs = [
-        pl.BlockSpec((tb, hid), functools.partial(lambda c, i, d: (jnp.clip(i - c * per, 0, per - 1), 0), c))
+        pl.BlockSpec((tb, hid), functools.partial(lambda c, i, t, d: (jnp.clip(i - c * per, 0, per - 1), 0), c))
         for c in range(n_out)
     ]
     return pl.pallas_call(
-        functools.partial(hidden_grad_kernel, nblk, 19, n_out),
+        functools.partial(hidden_grad_kernel, nblk, inner, n_out),
         grid_spec=pltpu.PrefetchScalarGridSpec(
             num_scalar_prefetch=1,
-            grid=(steps,),
+            grid=(steps, 2),
             in_specs=in_specs,
             out_specs=out_specs,
-            scratch_shapes=[pltpu.VMEM((tb, hid), jnp.float32)],
+            scratch_shapes=[
+                pltpu.VMEM((tb, hid), jnp.float32),
+                pltpu.VMEM((nblk * VB, hid), jnp.bfloat16),
+                pltpu.SemaphoreType.DMA((2,)),
+            ],
         ),
         out_shape=[jax.ShapeDtypeStruct((per * tb, hid), jnp.float32)] * n_out,
         compiler_params=pltpu.CompilerParams(vmem_limit_bytes=60 << 20),
@@ -208,53 +227,80 @@
     )(*args)
 
 
-def embed_grad_kernel(nblk, off, n_dp, d_ref, z_ref, lse_ref, w_ref, lab_ref, ut_ref, *rest):
-    outs, acc_s = rest[:n_dp], rest[n_dp]
-    j = pl.program_id(0)
+def embed_grad_kernel(nblk, off, n_dp, d_ref, z_ref, *rest):
+    hbm, outs, acc_s, held, sem = rest[:4], rest[4:4 + n_dp], rest[4 + n_dp], rest[5 + n_dp:9 + n_dp], rest[9 + n_dp]
+    lse_ref, w_ref, lab_ref, ut_ref = held
+    j, it = pl.program_id(0), pl.program_id(1)
     hid, tokens = ut_ref.shape
     cols = hid // n_dp
     lane = lax.broadcasted_iota(jnp.int32, (256, 128), 1)
-    group = tokens // 4
-    acc_s[...] = jnp.zeros(acc_s.shape, jnp.float32)
-
-    def step(it, carry):
-        acc = None
-        for i in range(group // 256):
-            sl = pl.ds(pl.multiple_of(it * group + i * 256, 256), 256)
-            lse, wgt, lab = lse_ref[sl, :], w_ref[sl, :], lab_ref[sl, :] - lane
-            g = jnp.concatenate(
-                [grad_block(z_ref[k, sl, :], lse, wgt, lab, (d_ref[0] * nblk + (off + j) * 2 + k) * VB) for k in range(2)],
-                axis=1,
-            )
-            part = jnp.dot(ut_ref[:, sl], g, preferred_element_type=jnp.float32)
-            acc = part if acc is None else acc + part
-        acc_s[...] += acc
-        return carry
-
-    lax.fori_loop(0, 4, step, 0)
-    for r in range(n_dp):
-        at = pl.multiple_of((d_ref[0] ^ r) * cols, 8)
-        outs[r][...] = acc_s[pl.ds(at, cols), :]
+    n_group = tokens // z_ref.shape[1]
+    group = tokens // n_group
+
+    def copies(it):
+        sl = pl.ds(pl.multiple_of(it * group, group), group)
+        for k, (src, dst) in enumerate(zip(hbm, held)):
+            at = (slice(None), sl) if k == 3 else (sl, slice(None))
+            yield pltpu.make_async_copy(src.at[at], dst.at[at], sem.at[it, k])
+
+    @pl.when((j == 0) & (it == 0))
+    def _():
+        for g in range(n_group):
+            for copy in copies(g):
+                copy.start()
+
+    @pl.when(j == 0)
+    def _():
+        for copy in copies(it):
+            copy.wait()
+
+    @pl.when(it == 0)
+    def _():
+        acc_s[...] = jnp.zeros(acc_s.shape, jnp.float32)
+
+    acc = None
+    for i in range(group // 256):
+        sl = pl.ds(pl.multiple_of(it * group + i * 256, 256), 256)
+        lse, wgt, lab = lse_ref[sl, :], w_ref[sl, :], lab_ref[sl, :] - lane
+        g = jnp.concatenate(
+            [
+                grad_block(z_ref[k, i * 256:(i + 1) * 256, :], lse, wgt, lab, (d_ref[0] * nblk + (off + j) * 2 + k) * VB)
+                for k in range(2)
+            ],
+            axis=1,
+        )
+        part = jnp.dot(ut_ref[:, sl], g, preferred_element_type=jnp.float32)
+        acc = part if acc is None else acc + part
+    acc_s[...] += acc
+
+    @pl.when(it == n_group - 1)
+    def _():
+        for r in range(n_dp):
+            at = pl.multiple_of((d_ref[0] ^ r) * cols, 8)
+            outs[r][...] = acc_s[pl.ds(at, cols), :]
 
 
 def embed_grad(dev, z, lse, wgt, lab, ut, off, steps, n_dp):
     nblk, tokens, _ = z.shape
     hid = ut.shape[0]
     cols = hid // n_dp
-    one = pl.Buffered(1)
-    wide = pl.BlockSpec((tokens, 128), lambda j, d: (0, 0), pipeline_mode=one)
     return pl.pallas_call(
         functools.partial(embed_grad_kernel, nblk, off, n_dp),
         grid_spec=pltpu.PrefetchScalarGridSpec(
             num_scalar_prefetch=1,
-            grid=(steps,),
+            grid=(steps, 2),
             in_specs=[
-                pl.BlockSpec((2, tokens, VB), lambda j, d: (off + j, 0, 0)),
-                wide, wide, wide,
-                pl.BlockSpec((hid, tokens), lambda j, d: (0, 0), pipeline_mode=one),
+                pl.BlockSpec((2, tokens // 2, VB), lambda j, t, d: (off + j, t, 0)),
+            ] + [pl.BlockSpec(memory_space=pl.ANY)] * 4,
+            out_specs=[pl.BlockSpec((cols, 2 * VB), lambda j, t, d: (0, j))] * n_dp,
+            scratch_shapes=[
+                pltpu.VMEM((hid, 2 * VB), jnp.float32),
+                pltpu.VMEM((tokens, 128), jnp.float32),
+                pltpu.VMEM((tokens, 128), jnp.float32),
+                pltpu.VMEM((tokens, 128), jnp.int32),
+                pltpu.VMEM((hid, tokens), jnp.bfloat16),
+                pltpu.SemaphoreType.DMA((2, 4)),
             ],
-            out_specs=[pl.BlockSpec((cols, 2 * VB), lambda j, d: (0, j))] * n_dp,
-            scratch_shapes=[pltpu.VMEM((hid, 2 * VB), jnp.float32)],
         ),
         out_shape=[jax.ShapeDtypeStruct((cols, steps * 2 * VB), jnp.float32)] * n_dp,
         compiler_params=pltpu.CompilerParams(vmem_limit_bytes=60 << 20),

time: 1250 us -> 1120 us (0.90)
  waiting for transfers between devices: 531 us -> 415 us
  Pallas kernels: 603 us -> 589 us
    ppermute x52, waiting for transfers between devices: 531 us -> 415 us  [swap(): return lax.ppermute(x, axis, [(i, i ^ mask) for i in range(size)])]
    pallas_call x4, Pallas kernels: 187 us -> 168 us  [embed_grad(): pl.pallas_call(functools.partial(embed_grad_kernel, nblk, off, n_dp), gri...]
  transfers between devices with their start and end apart: 52 -> 52, of which waited for: 17 -> 17; matrix products, arithmetic and copies ran while one was open for 2% -> 2% of each run, Pallas kernels for 30% -> 33%
where the time goes in v3:
time: 1120 us; the launch traced here: 1110 us
  Pallas kernels  589 us (53%)
  waiting for transfers between devices  415 us (37%)
  starting transfers between devices  47.5 us (4%)
  other arithmetic  28.5 us (3%)
  local copies, waits for them, and re-layouts  20.8 us (2%)
    ppermute x52, waiting for transfers between devices, swap(): return lax.ppermute(x, axis, [(i, i ^ mask) for i in range(size)])  415 us
    pallas_call x4, Pallas kernels, logits_call(): pl.pallas_call(functools.partial(logit_kernel, vocab_loc, nblk, first), g...  201 us
    pallas_call x3, Pallas kernels, hidden_grad(): pl.pallas_call(functools.partial(hidden_grad_kernel, nblk, inner, n_out),...  172 us
    pallas_call x4, Pallas kernels, embed_grad(): pl.pallas_call(functools.partial(embed_grad_kernel, nblk, off, n_dp), gri...  168 us
    ppermute x52, starting transfers between devices, swap(): return lax.ppermute(x, axis, [(i, i ^ mask) for i in range(size)])  47.5 us
    pallas_call x1, Pallas kernels, place(): pl.pallas_call(functools.partial(place_kernel, n_dp, per, off, last), gri...  29.7 us
  transfers between devices with their start and end apart: 52, of which 17 were waited for; matrix products, arithmetic and copies ran while one was open for 2% of the time, Pallas kernels for 33%

profile of v3, /device:TPU:0, one launch (start us, length us, event | category | flops | bytes accessed | tf_op | source)
XLA Modules:
  0.0 1107.5 jit_solution(6547267724345359524)
XLA Ops:
  0.7 1.5 bitcast_convert_fusion
  2.5 3.2 collective-permute-start.5
  5.7 1.5 collective-permute-start.3
  7.2 59.7 %collective-permute-done.5.refs_0_ = f32[776,896]{1,0:T(8,128)} collective-permute-done((f32[776,896]{1,0:T(8,128)S(1)}, f32[776,896]{1,0:T(8,128)}, u32[]{:S(2)}, u32[]{:S(2)}) %collective-permute-start.5) | collective-permute-done | bytes 2781216 | tf_op jit(solution)/shard_map/ppermute | solution.py:401
  68.2 59.0 %collective-permute-done.3.refs_0_ = f32[776,896]{1,0:T(8,128)} collective-permute-done((f32[776,896]{1,0:T(8,128)S(1)}, f32[776,896]{1,0:T(8,128)}, u32[]{:S(2)}, u32[]{:S(2)}) %collective-permute-start.3) | collective-permute-done | bytes 2781216 | tf_op jit(solution)/shard_map/ppermute | solution.py:401
  127.2 51.5 %logits.4 = (f32[38,6144,256]{2,1,0:T(8,128)}, bf16[896,6144]{1,0:T(8,128)(2,1)}, s32[6144,128]{1,0:T(8,128)}, f32[8,1536]{1,0:T(8,128)}, bf16[9728,896]{1,0:T(8,128)(2,1)}) custom-call(s32[2]{0:T(128)} %pad_add_fusion.d_ref, f32[776,896]{1,0:T(8,128)} %copy-done.19, f32[776,896]{1,0:T(8,128)} %collective-permute-done.2.refs_1_, s32[1]{0:T(128)} %bitcast.3.refs_2_, ...), custom_call_target="tpu_custom_call" | custom-call | flops 26776436736 | bytes 59768832 | tf_op jit(solution)/shard_map/logits/pallas_call | solution.py:117
  179.9 49.6 %logits.5 = (f32[38,6144,256]{2,1,0:T(8,128)}, bf16[896,6144]{1,0:T(8,128)(2,1)}, s32[6144,128]{1,0:T(8,128)}, f32[8,1536]{1,0:T(8,128)}) custom-call(s32[2]{0:T(128)} %pad_add_fusion.d_ref, f32[776,896]{1,0:T(8,128)} %collective-permute-done.5.refs_0_, ...), custom_call_target="tpu_custom_call", output_to_operand_aliasing={{0}: (6, {}), {1}: (7, {}), {2}: (8, {})} | custom-call | flops 26776436736 | bytes 59768832 | tf_op jit(solution)/shard_map/logits/pallas_call | solution.py:117
  230.4 49.9 %logits.6 = (f32[38,6144,256]{2,1,0:T(8,128)}, bf16[896,6144]{1,0:T(8,128)(2,1)}, s32[6144,128]{1,0:T(8,128)}, f32[8,1536]{1,0:T(8,128)}) custom-call(s32[2]{0:T(128)} %pad_add_fusion.d_ref, f32[776,896]{1,0:T(8,128)} %collective-permute-done.3.refs_0_, ...), custom_call_target="tpu_custom_call", output_to_operand_aliasing={{0}: (6, {}), {1}: (7, {}), {2}: (8, {})} | custom-call | flops 26776436736 | bytes 59768832 | tf_op jit(solution)/shard_map/logits/pallas_call | solution.py:117
  281.1 49.7 %logits.7 = (f32[38,6144,256]{2,1,0:T(8,128)}, bf16[896,6144]{1,0:T(8,128)(2,1)}, s32[6144,128]{1,0:T(8,128)}, f32[8,1536]{1,0:T(8,128)}) custom-call(s32[2]{0:T(128)} %pad_add_fusion.d_ref, f32[776,896]{1,0:T(8,128)} %collective-permute-done.refs_0_, ...), custom_call_target="tpu_custom_call", output_to_operand_aliasing={{0}: (6, {}), {1}: (7, {}), {2}: (8, {})} | custom-call | flops 26776436736 | bytes 59768832 | tf_op jit(solution)/shard_map/logits/pallas_call | solution.py:117
  331.9 1.4 slice_reduce_fusion.2
  333.7 1.4 slice_reduce_fusion.4
  335.1 3.2 collective-permute-done.8
  339.0 1.6 collective-permute-start.9
  340.6 1.5 slice_reduce_fusion.6
  345.2 1.6 collective-permute-start.10
  346.8 2.7 collective-permute-done.10
  350.3 2.2 broadcast_in_dim.12.rest_1_.w_ref
  352.5 2.2 broadcast_in_dim.11.rest_0_.lse_ref
  354.7 36.9 %embed_grad.4 = (f32[112,2048]{1,0:T(8,128)}, f32[112,2048]{1,0:T(8,128)}, f32[112,2048]{1,0:T(8,128)}, f32[112,2048]{1,0:T(8,128)}, f32[112,2048]{1,0:T(8,128)}...) custom-call(s32[2]{0:T(128)} %pad_add_fusion.d_ref, f32[38,6144,256]{2,1,0:T(8,128)} %get-tuple-element.78.z_ref, ...), custom_call_target="tpu_custom_call" | custom-call | flops 22548578304 | bytes 50331648 | tf_op jit(solution)/shard_map/embed_grad/pallas_call | solution.py:287
  391.6 57.0 %embed_grad.5 = (f32[112,3584]{1,0:T(8,128)}, f32[112,3584]{1,0:T(8,128)}, f32[112,3584]{1,0:T(8,128)}, f32[112,3584]{1,0:T(8,128)}, f32[112,3584]{1,0:T(8,128)}...) custom-call(s32[2]{0:T(128)} %pad_add_fusion.d_ref, f32[38,6144,256]{2,1,0:T(8,128)} %get-tuple-element.78.z_ref, ...), custom_call_target="tpu_custom_call" | custom-call | flops 39460012032 | bytes 88080384 | tf_op jit(solution)/shard_map/embed_grad/pallas_call | solution.py:287
  448.7 78.8 %hidden_grad.3 = f32[3072,896]{1,0:T(8,128)} custom-call(s32[2]{0:T(128)} %pad_add_fusion.d_ref, f32[38,6144,256]{2,1,0:T(8,128)} %get-tuple-element.78.z_ref, f32[6144,128]{1,0:T(8,128)} %broadcast_in_dim.11.rest_0_.lse_ref, f32[6144,128]{1,0:T(8,128)} %broadcast_in_dim.12.rest_1_.w_ref, s32[6144,128]{1,0:T(8,128)} %get-tuple-element.83.rest_2_.lab_ref, ...), custom_call_target="tpu_custom_call" | custom-call | flops 53552873472 | bytes 119537664 | tf_op jit(solution)/shard_map/hidden_grad/pallas_call | solution.py:210
  529.9 50.8 %embed_grad.6 = (f32[112,3072]{1,0:T(8,128)}, f32[112,3072]{1,0:T(8,128)}, f32[112,3072]{1,0:T(8,128)}, f32[112,3072]{1,0:T(8,128)}, f32[112,3072]{1,0:T(8,128)}...) custom-call(s32[2]{0:T(128)} %pad_add_fusion.d_ref, f32[38,6144,256]{2,1,0:T(8,128)} %get-tuple-element.78.z_ref, ...), custom_call_target="tpu_custom_call" | custom-call | flops 33822867456 | bytes 75497472 | tf_op jit(solution)/shard_map/embed_grad/pallas_call | solution.py:287
  580.7 1.6 collective-permute-start.49
  582.8 1.9 collective-permute-start.51
  584.7 46.7 %hidden_grad.4 = (f32[384,896]{1,0:T(8,128)}, f32[384,896]{1,0:T(8,128)}, f32[384,896]{1,0:T(8,128)}, f32[384,896]{1,0:T(8,128)}) custom-call(s32[2]{0:T(128)} %pad_add_fusion.d_ref, f32[38,6144,256]{2,1,0:T(8,128)} %get-tuple-element.78.z_ref, f32[6144,128]{1,0:T(8,128)} %broadcast_in_dim.11.rest_0_.lse_ref, f32[6144,128]{1,0:T(8,128)} %broadcast_in_dim.12.rest_1_.w_ref, ...), custom_call_target="tpu_custom_call" | custom-call | flops 26776436736 | bytes 59768832 | tf_op jit(solution)/shard_map/hidden_grad/pallas_call | solution.py:210
  632.7 9.6 collective-permute-done.49.refs_5_
  643.4 1.5 collective-permute-start.34
  644.9 1.6 collective-permute-start.13
  646.5 19.0 %collective-permute-done.32.refs_2_ = f32[112,3072]{1,0:T(8,128)} collective-permute-done((f32[112,3072]{1,0:T(8,128)}, f32[112,3072]{1,0:T(8,128)}, u32[]{:S(2)}, u32[]{:S(2)}) %collective-permute-start.32) | collective-permute-done | bytes 1376288 | tf_op jit(solution)/shard_map/ppermute | solution.py:401
  665.9 27.3 %collective-permute-done.33.refs_3_ = f32[112,3072]{1,0:T(8,128)} collective-permute-done((f32[112,3072]{1,0:T(8,128)}, f32[112,3072]{1,0:T(8,128)}, u32[]{:S(2)}, u32[]{:S(2)}) %collective-permute-start.33) | collective-permute-done | bytes 1376288 | tf_op jit(solution)/shard_map/ppermute | solution.py:401
  693.2 1.6 collective-permute-start.12
  695.2 1.6 collective-permute-start.17
  696.8 46.7 %hidden_grad.5 = (f32[384,896]{1,0:T(8,128)}, f32[384,896]{1,0:T(8,128)}, f32[384,896]{1,0:T(8,128)}, f32[384,896]{1,0:T(8,128)}) custom-call(s32[2]{0:T(128)} %pad_add_fusion.d_ref, f32[38,6144,256]{2,1,0:T(8,128)} %get-tuple-element.78.z_ref, f32[6144,128]{1,0:T(8,128)} %broadcast_in_dim.11.rest_0_.lse_ref, f32[6144,128]{1,0:T(8,128)} %broadcast_in_dim.12.rest_1_.w_ref, ...), custom_call_target="tpu_custom_call" | custom-call | flops 26776436736 | bytes 59768832 | tf_op jit(solution)/shard_map/hidden_grad/pallas_call | solution.py:210
  743.5 3.1 add.140
  746.5 8.5 collective-permute-done.15
  755.1 2.2 collective-permute-start.14
  757.3 2.7 add.142
  760.0 24.6 %collective-permute-done.17 = f32[384,896]{1,0:T(8,128)} collective-permute-done((f32[384,896]{1,0:T(8,128)}, f32[384,896]{1,0:T(8,128)}, u32[]{:S(2)}, u32[]{:S(2)}) %collective-permute-start.17) | collective-permute-done | bytes 1376288 | tf_op jit(solution)/shard_map/ppermute | solution.py:401
  785.2 2.7 add.144
  787.9 3.1 collective-permute-start.18
  791.6 1.6 collective-permute-start.37
  794.8 52.5 %collective-permute-done.16 = f32[384,896]{1,0:T(8,128)} collective-permute-done((f32[384,896]{1,0:T(8,128)}, f32[384,896]{1,0:T(8,128)}, u32[]{:S(2)}, u32[]{:S(2)}) %collective-permute-start.16) | collective-permute-done | bytes 1376288 | tf_op jit(solution)/shard_map/ppermute | solution.py:401
  851.1 3.9 fusion.4
  855.0 30.8 %collective-permute-done.37.refs_7_ = f32[112,3072]{1,0:T(8,128)} collective-permute-done((f32[112,3072]{1,0:T(8,128)}, f32[112,3072]{1,0:T(8,128)}, u32[]{:S(2)}, u32[]{:S(2)}) %collective-permute-start.37) | collective-permute-done | bytes 1376288 | tf_op jit(solution)/shard_map/ppermute | solution.py:401
  885.8 1.6 collective-permute-start.19
  889.4 1.5 collective-permute-start.43
  893.4 1.4 fusion.6
  894.8 25.4 %collective-permute-done.40.refs_3_ = f32[112,3584]{1,0:T(8,128)} collective-permute-done((f32[112,3584]{1,0:T(8,128)}, f32[112,3584]{1,0:T(8,128)}, u32[]{:S(2)}, u32[]{:S(2)}) %collective-permute-start.40) | collective-permute-done | bytes 1605664 | tf_op jit(solution)/shard_map/ppermute | solution.py:401
  920.2 1.6 collective-permute-start.23
  922.3 23.4 %embed_grad.7 = (f32[112,1024]{1,0:T(8,128)}, f32[112,1024]{1,0:T(8,128)}, f32[112,1024]{1,0:T(8,128)}, f32[112,1024]{1,0:T(8,128)}, f32[112,1024]{1,0:T(8,128)}...) custom-call(s32[2]{0:T(128)} %pad_add_fusion.d_ref, f32[38,6144,256]{2,1,0:T(8,128)} %get-tuple-element.78.z_ref, ...), custom_call_target="tpu_custom_call" | custom-call | flops 11274289152 | bytes 25165824 | tf_op jit(solution)/shard_map/embed_grad/pallas_call | solution.py:287
  945.6 73.3 %collective-permute-done.42.refs_5_ = f32[112,3584]{1,0:T(8,128)} collective-permute-done((f32[112,3584]{1,0:T(8,128)}, f32[112,3584]{1,0:T(8,128)}, u32[]{:S(2)}, u32[]{:S(2)}) %collective-permute-start.42) | collective-permute-done | bytes 1605664 | tf_op jit(solution)/shard_map/ppermute | solution.py:401
  1019.3 1.5 collective-permute-start.26
  1021.9 1.7 collective-permute-start.27
  1023.6 8.9 collective-permute-done.25.refs_2_
  1033.3 8.1 collective-permute-done.26.refs_3_
  1042.2 2.9 collective-permute-start.30
  1045.2 1.2 copy-done.1
  1046.3 1.2 copy-done.3
  1049.9 1.2 copy-done.9
  1051.1 5.0 shard_map.84.refs_8_
  1056.1 9.2 shard_map.85.refs_8_
  1065.4 29.7 %place.1.refs_8_ = f32[112,75968]{1,0:T(8,128)} custom-call(s32[2]{0:T(128)} %pad_add_fusion.d_ref, f32[112,3072]{1,0:T(8,128)} %get-tuple-element.90.refs_0_, f32[112,3072]{1,0:T(8,128)} %collective-permute-done.31.refs_1_, f32[112,3072]{1,0:T(8,128)} %collective-permute-done.32.refs_2_, ...), custom_call_target="tpu_custom_call", output_to_operand_aliasing={{}: (9, {})} | custom-call | flops 2752512 | bytes 22020096 | tf_op jit(solution)/shard_map/place/pallas_call | solution.py:381
  1096.3 4.7 shard_map.86
  1101.6 4.5 maximum_select_fusion
  (217 shorter events, 31.4 us)
Async XLA Ops:
  2.2 65.3 %copy-start.38 = (bf16[896]{0:T(1024)(128)(2,1)S(1)}, bf16[896]{0:T(1024)(128)(2,1)}, u32[]{:S(2)}) copy-start(bf16[896]{0:T(1024)(128)(2,1)} %param.8) | copy-start | bytes 5380
  2.4 124.7 %copy-start.19 = (f32[776,896]{1,0:T(8,128)}, f32[776,896]{1,0:T(8,128)S(1)}, u32[]{:S(2)}) copy-start(f32[776,896]{1,0:T(8,128)S(1)} %select_maximum_fusion.refs_0_) | copy-start | bytes 8343556
  2.5 64.5 %collective-permute-start.5 = (f32[776,896]{1,0:T(8,128)S(1)}, f32[776,896]{1,0:T(8,128)}, u32[]{:S(2)}, u32[]{:S(2)}) collective-permute-start(f32[776,896]{1,0:T(8,128)S(1)} %select_maximum_fusion.refs_0_), channel_id=1, source_target_pairs={{0,2},{1,3},{2,0},{3,1},{4,6},{5,7},{6,4},{7,5},{8,10},{9,11},{10,... | collective-permute-start | bytes 8343560 | tf_op jit(solution)/shard_map/ppermute | solution.py:401
  5.7 121.5 %collective-permute-start.3 = (f32[776,896]{1,0:T(8,128)S(1)}, f32[776,896]{1,0:T(8,128)}, u32[]{:S(2)}, u32[]{:S(2)}) collective-permute-start(f32[776,896]{1,0:T(8,128)S(1)} %select_maximum_fusion.refs_0_), channel_id=1, source_target_pairs={{0,4},{1,5},{2,6},{3,7},{4,0},{5,1},{6,2},{7,3},{8,12},{9,13},{10,... | collective-permute-start | bytes 8343560 | tf_op jit(solution)/shard_map/ppermute | solution.py:401
  7.2 119.9 %collective-permute-start.2 = (f32[776,896]{1,0:T(8,128)S(1)}, f32[776,896]{1,0:T(8,128)}, u32[]{:S(2)}, u32[]{:S(2)}) collective-permute-start(f32[776,896]{1,0:T(8,128)S(1)} %select_maximum_fusion.refs_0_), channel_id=1, source_target_pairs={{0,1},{1,0},{2,3},{3,2},{4,5},{5,4},{6,7},{7,6},{8,9},{9,8},{10,11... | collective-permute-start | bytes 8343560 | tf_op jit(solution)/shard_map/ppermute | solution.py:401
  7.2 172.2 %collective-permute-start = (f32[776,896]{1,0:T(8,128)S(1)}, f32[776,896]{1,0:T(8,128)}, u32[]{:S(2)}, u32[]{:S(2)}) collective-permute-start(f32[776,896]{1,0:T(8,128)S(1)} %select_maximum_fusion.refs_0_), channel_id=1, source_target_pairs={{0,6},{1,7},{2,4},{3,5},{4,2},{5,3},{6,0},{7,1},{8,14},{9,15},{10,... | collective-permute-start | bytes 8343560 | tf_op jit(solution)/shard_map/ppermute | solution.py:401
  66.9 113.0 %collective-permute-start.6 = (f32[776,896]{1,0:T(8,128)}, f32[776,896]{1,0:T(8,128)}, u32[]{:S(2)}, u32[]{:S(2)}) collective-permute-start(f32[776,896]{1,0:T(8,128)} %collective-permute-done.5.refs_0_), channel_id=1, source_target_pairs={{0,1},{1,0},{2,3},{3,2},{4,5},{5,4},{6,7},{7,6},{8,9},{9,8},{10,11... | collective-permute-start | bytes 8343560 | tf_op jit(solution)/shard_map/ppermute | solution.py:401
  127.1 103.2 %collective-permute-start.4 = (f32[776,896]{1,0:T(8,128)}, f32[776,896]{1,0:T(8,128)}, u32[]{:S(2)}, u32[]{:S(2)}) collective-permute-start(f32[776,896]{1,0:T(8,128)} %collective-permute-done.3.refs_0_), channel_id=1, source_target_pairs={{0,1},{1,0},{2,3},{3,2},{4,5},{5,4},{6,7},{7,6},{8,9},{9,8},{10,11... | collective-permute-start | bytes 8343560 | tf_op jit(solution)/shard_map/ppermute | solution.py:401
  179.5 101.6 %collective-permute-start.1 = (f32[776,896]{1,0:T(8,128)}, f32[776,896]{1,0:T(8,128)}, u32[]{:S(2)}, u32[]{:S(2)}) collective-permute-start(f32[776,896]{1,0:T(8,128)} %collective-permute-done.refs_0_), channel_id=1, source_target_pairs={{0,1},{1,0},{2,3},{3,2},{4,5},{5,4},{6,7},{7,6},{8,9},{9,8},{10,11... | collective-permute-start | bytes 8343560 | tf_op jit(solution)/shard_map/ppermute | solution.py:401
  331.8 1.6 collective-permute-start.7
  333.6 4.7 collective-permute-start.8
  339.0 5.5 collective-permute-start.9
  345.2 4.4 collective-permute-start.10
  448.7 78.8 %copy-start.43 = (f32[112,2048]{1,0:T(8,128)S(1)}, f32[112,2048]{1,0:T(8,128)}, u32[]{:S(2)}) copy-start(f32[112,2048]{1,0:T(8,128)} %get-tuple-element.125) | copy-start | bytes 2752516
  448.7 79.3 %copy-start.42 = (f32[112,2048]{1,0:T(8,128)S(1)}, f32[112,2048]{1,0:T(8,128)}, u32[]{:S(2)}) copy-start(f32[112,2048]{1,0:T(8,128)} %get-tuple-element.126) | copy-start | bytes 2752516
  527.5 55.3 %collective-permute-start.11 = (f32[3072,896]{1,0:T(8,128)}, f32[3072,896]{1,0:T(8,128)}, u32[]{:S(2)}, u32[]{:S(2)}) collective-permute-start(f32[3072,896]{1,0:T(8,128)} %hidden_grad.3), channel_id=1, source_target_pairs={{0,1},{1,0},{2,3},{3,2},{4,5},{5,4},{6,7},{7,6},{8,9},{9,8},{10,11... | collective-permute-start | bytes 33030152 | tf_op jit(solution)/shard_map/ppermute | solution.py:401
  527.5 53.2 %collective-permute-start.45 = (f32[112,2048]{1,0:T(8,128)S(1)}, f32[112,2048]{1,0:T(8,128)S(1)}, u32[]{:S(2)}, u32[]{:S(2)}) collective-permute-start(f32[112,2048]{1,0:T(8,128)S(1)} %copy-done.43), channel_id=1, source_target_pairs={{0,1},{1,0},{2,3},{3,2},{4,5},{5,4},{6,7},{7,6},{8,9},{9,8},{10,11... | collective-permute-start | bytes 2752520 | tf_op jit(solution)/shard_map/ppermute | solution.py:401
  528.0 54.3 %collective-permute-start.46 = (f32[112,2048]{1,0:T(8,128)S(1)}, f32[112,2048]{1,0:T(8,128)S(1)}, u32[]{:S(2)}, u32[]{:S(2)}) collective-permute-start(f32[112,2048]{1,0:T(8,128)S(1)} %copy-done.42), channel_id=1, source_target_pairs={{0,2},{1,3},{2,0},{3,1},{4,6},{5,7},{6,4},{7,5},{8,10},{9,11},{10,... | collective-permute-start | bytes 2752520 | tf_op jit(solution)/shard_map/ppermute | solution.py:401
  528.5 102.8 %collective-permute-start.47 = (f32[112,2048]{1,0:T(8,128)}, f32[112,2048]{1,0:T(8,128)}, u32[]{:S(2)}, u32[]{:S(2)}) collective-permute-start(f32[112,2048]{1,0:T(8,128)} %get-tuple-element.127), channel_id=1, source_target_pairs={{0,3},{1,2},{2,1},{3,0},{4,7},{5,6},{6,5},{7,4},{8,11},{9,10},{10,... | collective-permute-start | bytes 2752520 | tf_op jit(solution)/shard_map/ppermute | solution.py:401
  529.4 102.7 %collective-permute-start.48 = (f32[112,2048]{1,0:T(8,128)}, f32[112,2048]{1,0:T(8,128)}, u32[]{:S(2)}, u32[]{:S(2)}) collective-permute-start(f32[112,2048]{1,0:T(8,128)} %get-tuple-element.128), channel_id=1, source_target_pairs={{0,4},{1,5},{2,6},{3,7},{4,0},{5,1},{6,2},{7,3},{8,12},{9,13},{10,... | collective-permute-start | bytes 2752520 | tf_op jit(solution)/shard_map/ppermute | solution.py:401
  580.7 50.7 %copy-start.2 = (f32[112,2048]{1,0:T(8,128)}, f32[112,2048]{1,0:T(8,128)S(1)}, u32[]{:S(2)}) copy-start(f32[112,2048]{1,0:T(8,128)S(1)} %collective-permute-done.45.refs_1_) | copy-start | bytes 2752516
  580.7 61.6 %collective-permute-start.49 = (f32[112,2048]{1,0:T(8,128)}, f32[112,2048]{1,0:T(8,128)S(1)}, u32[]{:S(2)}, u32[]{:S(2)}) collective-permute-start(f32[112,2048]{1,0:T(8,128)} %get-tuple-element.129), channel_id=1, source_target_pairs={{0,5},{1,4},{2,7},{3,6},{4,1},{5,0},{6,3},{7,2},{8,13},{9,12},{10,... | collective-permute-start | bytes 2752520 | tf_op jit(solution)/shard_map/ppermute | solution.py:401
  582.4 49.0 %copy-start.4 = (f32[112,2048]{1,0:T(8,128)}, f32[112,2048]{1,0:T(8,128)S(1)}, u32[]{:S(2)}) copy-start(f32[112,2048]{1,0:T(8,128)S(1)} %collective-permute-done.46.refs_2_) | copy-start | bytes 2752516
  582.4 61.0 %collective-permute-start.50 = (f32[112,2048]{1,0:T(8,128)}, f32[112,2048]{1,0:T(8,128)S(1)}, u32[]{:S(2)}, u32[]{:S(2)}) collective-permute-start(f32[112,2048]{1,0:T(8,128)} %get-tuple-element.130), channel_id=1, source_target_pairs={{0,6},{1,7},{2,4},{3,5},{4,2},{5,3},{6,0},{7,1},{8,14},{9,15},{10,... | collective-permute-start | bytes 2752520 | tf_op jit(solution)/shard_map/ppermute | solution.py:401
  582.8 62.2 %collective-permute-start.51 = (f32[112,2048]{1,0:T(8,128)}, f32[112,2048]{1,0:T(8,128)}, u32[]{:S(2)}, u32[]{:S(2)}) collective-permute-start(f32[112,2048]{1,0:T(8,128)} %get-tuple-element.131), channel_id=1, source_target_pairs={{0,7},{1,6},{2,5},{3,4},{4,3},{5,2},{6,1},{7,0},{8,15},{9,14},{10,... | collective-permute-start | bytes 2752520 | tf_op jit(solution)/shard_map/ppermute | solution.py:401
  631.4 15.1 %collective-permute-start.31 = (f32[112,3072]{1,0:T(8,128)}, f32[112,3072]{1,0:T(8,128)}, u32[]{:S(2)}, u32[]{:S(2)}) collective-permute-start(f32[112,3072]{1,0:T(8,128)} %get-tuple-element.111), channel_id=1, source_target_pairs={{0,1},{1,0},{2,3},{3,2},{4,5},{5,4},{6,7},{7,6},{8,9},{9,8},{10,11... | collective-permute-start | bytes 4128776 | tf_op jit(solution)/shard_map/ppermute | solution.py:401
  632.2 33.4 %collective-permute-start.32 = (f32[112,3072]{1,0:T(8,128)}, f32[112,3072]{1,0:T(8,128)}, u32[]{:S(2)}, u32[]{:S(2)}) collective-permute-start(f32[112,3072]{1,0:T(8,128)} %get-tuple-element.112), channel_id=1, source_target_pairs={{0,2},{1,3},{2,0},{3,1},{4,6},{5,7},{6,4},{7,5},{8,10},{9,11},{10,... | collective-permute-start | bytes 4128776 | tf_op jit(solution)/shard_map/ppermute | solution.py:401
  642.3 101.2 %copy-start.6 = (f32[112,2048]{1,0:T(8,128)}, f32[112,2048]{1,0:T(8,128)S(1)}, u32[]{:S(2)}) copy-start(f32[112,2048]{1,0:T(8,128)S(1)} %collective-permute-done.49.refs_5_) | copy-start | bytes 2752516
  642.3 50.9 %collective-permute-start.33 = (f32[112,3072]{1,0:T(8,128)}, f32[112,3072]{1,0:T(8,128)}, u32[]{:S(2)}, u32[]{:S(2)}) collective-permute-start(f32[112,3072]{1,0:T(8,128)} %get-tuple-element.113), channel_id=1, source_target_pairs={{0,3},{1,2},{2,1},{3,0},{4,7},{5,6},{6,5},{7,4},{8,11},{9,10},{10,... | collective-permute-start | bytes 4128776 | tf_op jit(solution)/shard_map/ppermute | solution.py:401
  643.4 100.1 %copy-start.8 = (f32[112,2048]{1,0:T(8,128)}, f32[112,2048]{1,0:T(8,128)S(1)}, u32[]{:S(2)}) copy-start(f32[112,2048]{1,0:T(8,128)S(1)} %collective-permute-done.50.refs_6_) | copy-start | bytes 2752516
  643.4 51.4 %collective-permute-start.34 = (f32[112,3072]{1,0:T(8,128)}, f32[112,3072]{1,0:T(8,128)}, u32[]{:S(2)}, u32[]{:S(2)}) collective-permute-start(f32[112,3072]{1,0:T(8,128)} %get-tuple-element.114), channel_id=1, source_target_pairs={{0,4},{1,5},{2,6},{3,7},{4,0},{5,1},{6,2},{7,3},{8,12},{9,13},{10,... | collective-permute-start | bytes 4128776 | tf_op jit(solution)/shard_map/ppermute | solution.py:401
  644.9 50.3 %collective-permute-start.13 = (f32[384,896]{1,0:T(8,128)}, f32[384,896]{1,0:T(8,128)}, u32[]{:S(2)}, u32[]{:S(2)}) collective-permute-start(f32[384,896]{1,0:T(8,128)} %get-tuple-element.96), channel_id=1, source_target_pairs={{0,8},{8,0},{1,9},{9,1},{2,10},{10,2},{3,11},{11,3},{4,12},{12,4},... | collective-permute-start | bytes 4128776 | tf_op jit(solution)/shard_map/ppermute | solution.py:401
  646.5 141.4 %collective-permute-start.35 = (f32[112,3072]{1,0:T(8,128)}, f32[112,3072]{1,0:T(8,128)S(1)}, u32[]{:S(2)}, u32[]{:S(2)}) collective-permute-start(f32[112,3072]{1,0:T(8,128)} %get-tuple-element.115), channel_id=1, source_target_pairs={{0,5},{1,4},{2,7},{3,6},{4,1},{5,0},{6,3},{7,2},{8,13},{9,12},{10,... | collective-permute-start | bytes 4128776 | tf_op jit(solution)/shard_map/ppermute | solution.py:401
  665.5 125.7 %collective-permute-start.36 = (f32[112,3072]{1,0:T(8,128)}, f32[112,3072]{1,0:T(8,128)}, u32[]{:S(2)}, u32[]{:S(2)}) collective-permute-start(f32[112,3072]{1,0:T(8,128)} %get-tuple-element.116), channel_id=1, source_target_pairs={{0,6},{1,7},{2,4},{3,5},{4,2},{5,3},{6,0},{7,1},{8,14},{9,15},{10,... | collective-permute-start | bytes 4128776 | tf_op jit(solution)/shard_map/ppermute | solution.py:401
  693.2 98.1 %collective-permute-start.12 = (f32[384,896]{1,0:T(8,128)}, f32[384,896]{1,0:T(8,128)}, u32[]{:S(2)}, u32[]{:S(2)}) collective-permute-start(f32[384,896]{1,0:T(8,128)} %get-tuple-element.92), channel_id=1, source_target_pairs={{0,8},{8,0},{1,9},{9,1},{2,10},{10,2},{3,11},{11,3},{4,12},{12,4},... | collective-permute-start | bytes 4128776 | tf_op jit(solution)/shard_map/ppermute | solution.py:401
  694.7 60.3 %collective-permute-start.15 = (f32[384,896]{1,0:T(8,128)}, f32[384,896]{1,0:T(8,128)}, u32[]{:S(2)}, u32[]{:S(2)}) collective-permute-start(f32[384,896]{1,0:T(8,128)} %get-tuple-element.98), channel_id=1, source_target_pairs={{0,8},{8,0},{1,9},{9,1},{2,10},{10,2},{3,11},{11,3},{4,12},{12,4},... | collective-permute-start | bytes 4128776 | tf_op jit(solution)/shard_map/ppermute | solution.py:401
  695.2 89.3 %collective-permute-start.17 = (f32[384,896]{1,0:T(8,128)}, f32[384,896]{1,0:T(8,128)}, u32[]{:S(2)}, u32[]{:S(2)}) collective-permute-start(f32[384,896]{1,0:T(8,128)} %get-tuple-element.100), channel_id=1, source_target_pairs={{0,8},{8,0},{1,9},{9,1},{2,10},{10,2},{3,11},{11,3},{4,12},{12,4},... | collective-permute-start | bytes 4128776 | tf_op jit(solution)/shard_map/ppermute | solution.py:401
  755.1 36.5 %collective-permute-start.14 = (f32[384,896]{1,0:T(8,128)}, f32[384,896]{1,0:T(8,128)}, u32[]{:S(2)}, u32[]{:S(2)}) collective-permute-start(f32[384,896]{1,0:T(8,128)} %add.140), channel_id=1, source_target_pairs={{0,2},{1,3},{2,0},{3,1},{4,6},{5,7},{6,4},{7,5},{8,10},{9,11},{10,... | collective-permute-start | bytes 4128776 | tf_op jit(solution)/shard_map/ppermute | solution.py:401
  784.6 62.7 %collective-permute-start.16 = (f32[384,896]{1,0:T(8,128)}, f32[384,896]{1,0:T(8,128)}, u32[]{:S(2)}, u32[]{:S(2)}) collective-permute-start(f32[384,896]{1,0:T(8,128)} %add.142), channel_id=1, source_target_pairs={{0,4},{1,5},{2,6},{3,7},{4,0},{5,1},{6,2},{7,3},{8,12},{9,13},{10,... | collective-permute-start | bytes 4128776 | tf_op jit(solution)/shard_map/ppermute | solution.py:401
  787.9 60.0 %collective-permute-start.18 = (f32[384,896]{1,0:T(8,128)}, f32[384,896]{1,0:T(8,128)}, u32[]{:S(2)}, u32[]{:S(2)}) collective-permute-start(f32[384,896]{1,0:T(8,128)} %add.144), channel_id=1, source_target_pairs={{0,6},{1,7},{2,4},{3,5},{4,2},{5,3},{6,0},{7,1},{8,14},{9,15},{10,... | collective-permute-start | bytes 4128776 | tf_op jit(solution)/shard_map/ppermute | solution.py:401
  791.2 96.2 %collective-permute-start.38 = (f32[112,3584]{1,0:T(8,128)}, f32[112,3584]{1,0:T(8,128)S(1)}, u32[]{:S(2)}, u32[]{:S(2)}) collective-permute-start(f32[112,3584]{1,0:T(8,128)} %get-tuple-element.118), channel_id=1, source_target_pairs={{0,1},{1,0},{2,3},{3,2},{4,5},{5,4},{6,7},{7,6},{8,9},{9,8},{10,11... | collective-permute-start | bytes 4816904 | tf_op jit(solution)/shard_map/ppermute | solution.py:401
  791.3 99.6 %collective-permute-start.39 = (f32[112,3584]{1,0:T(8,128)}, f32[112,3584]{1,0:T(8,128)S(1)}, u32[]{:S(2)}, u32[]{:S(2)}) collective-permute-start(f32[112,3584]{1,0:T(8,128)} %get-tuple-element.119), channel_id=1, source_target_pairs={{0,2},{1,3},{2,0},{3,1},{4,6},{5,7},{6,4},{7,5},{8,10},{9,11},{10,... | collective-permute-start | bytes 4816904 | tf_op jit(solution)/shard_map/ppermute | solution.py:401
  791.6 94.2 %collective-permute-start.37 = (f32[112,3072]{1,0:T(8,128)}, f32[112,3072]{1,0:T(8,128)}, u32[]{:S(2)}, u32[]{:S(2)}) collective-permute-start(f32[112,3072]{1,0:T(8,128)} %get-tuple-element.117), channel_id=1, source_target_pairs={{0,7},{1,6},{2,5},{3,4},{4,3},{5,2},{6,1},{7,0},{8,15},{9,14},{10,... | collective-permute-start | bytes 4128776 | tf_op jit(solution)/shard_map/ppermute | solution.py:401
  847.3 72.9 %collective-permute-start.40 = (f32[112,3584]{1,0:T(8,128)}, f32[112,3584]{1,0:T(8,128)}, u32[]{:S(2)}, u32[]{:S(2)}) collective-permute-start(f32[112,3584]{1,0:T(8,128)} %get-tuple-element.120), channel_id=1, source_target_pairs={{0,3},{1,2},{2,1},{3,0},{4,7},{5,6},{6,5},{7,4},{8,11},{9,10},{10,... | collective-permute-start | bytes 4816904 | tf_op jit(solution)/shard_map/ppermute | solution.py:401
  847.9 73.9 %collective-permute-start.41 = (f32[112,3584]{1,0:T(8,128)}, f32[112,3584]{1,0:T(8,128)}, u32[]{:S(2)}, u32[]{:S(2)}) collective-permute-start(f32[112,3584]{1,0:T(8,128)} %get-tuple-element.121), channel_id=1, source_target_pairs={{0,4},{1,5},{2,6},{3,7},{4,0},{5,1},{6,2},{7,3},{8,12},{9,13},{10,... | collective-permute-start | bytes 4816904 | tf_op jit(solution)/shard_map/ppermute | solution.py:401
  851.1 42.3 %copy-start.21 = (bf16[3,256,896]{2,1,0:T(8,128)(2,1)S(1)}, bf16[3,256,896]{2,1,0:T(8,128)(2,1)}, u32[]{:S(2)}) copy-start(bf16[3,256,896]{2,1,0:T(8,128)(2,1)} %param.5) | copy-start | bytes 4128772
  885.8 3.6 collective-permute-start.19
  887.4 131.5 %collective-permute-start.42 = (f32[112,3584]{1,0:T(8,128)}, f32[112,3584]{1,0:T(8,128)}, u32[]{:S(2)}, u32[]{:S(2)}) collective-permute-start(f32[112,3584]{1,0:T(8,128)} %get-tuple-element.122), channel_id=1, source_target_pairs={{0,5},{1,4},{2,7},{3,6},{4,1},{5,0},{6,3},{7,2},{8,13},{9,12},{10,... | collective-permute-start | bytes 4816904 | tf_op jit(solution)/shard_map/ppermute | solution.py:401
  889.4 129.5 %collective-permute-start.43 = (f32[112,3584]{1,0:T(8,128)}, f32[112,3584]{1,0:T(8,128)}, u32[]{:S(2)}, u32[]{:S(2)}) collective-permute-start(f32[112,3584]{1,0:T(8,128)} %get-tuple-element.123), channel_id=1, source_target_pairs={{0,6},{1,7},{2,4},{3,5},{4,2},{5,3},{6,0},{7,1},{8,14},{9,15},{10,... | collective-permute-start | bytes 4816904 | tf_op jit(solution)/shard_map/ppermute | solution.py:401
  890.9 1.6 collective-permute-start.20
  892.5 128.3 %collective-permute-start.44 = (f32[112,3584]{1,0:T(8,128)}, f32[112,3584]{1,0:T(8,128)}, u32[]{:S(2)}, u32[]{:S(2)}) collective-permute-start(f32[112,3584]{1,0:T(8,128)} %get-tuple-element.124), channel_id=1, source_target_pairs={{0,7},{1,6},{2,5},{3,4},{4,3},{5,2},{6,1},{7,0},{8,15},{9,14},{10,... | collective-permute-start | bytes 4816904 | tf_op jit(solution)/shard_map/ppermute | solution.py:401
  894.8 150.3 %copy-start.17 = (s32[2]{0:T(128)S(1)}, s32[2]{0:T(128)}, u32[]{:S(2)}) copy-start(s32[2]{0:T(128)} %pad_add_fusion.d_ref) | copy-start | bytes 28
  920.2 181.4 %collective-permute-start.23 = (f32[384,896]{1,0:T(8,128)}, f32[384,896]{1,0:T(8,128)}, u32[]{:S(2)}, u32[]{:S(2)}) collective-permute-start(f32[384,896]{1,0:T(8,128)} %fusion.6), channel_id=1, source_target_pairs={{0,8},{8,0},{1,9},{9,1},{2,10},{10,2},{3,11},{11,3},{4,12},{12,4},... | collective-permute-start | bytes 4128776 | tf_op jit(solution)/shard_map/ppermute | solution.py:401
  921.8 97.5 %collective-permute-start.21 = (f32[1,897]{1,0:T(1,128)S(1)}, f32[1,897]{1,0:T(1,128)S(1)}, u32[]{:S(2)}, u32[]{:S(2)}) collective-permute-start(f32[1,897]{1,0:T(1,128)S(1)} %add.156), channel_id=1, source_target_pairs={{0,2},{1,3},{2,0},{3,1},{4,6},{5,7},{6,4},{7,5},{8,10},{9,11},{10,... | collective-permute-start | bytes 10772 | tf_op jit(solution)/shard_map/ppermute | solution.py:401
  1018.9 2.2 collective-permute-start.24
  1018.9 13.6 %collective-permute-start.25 = (f32[112,1024]{1,0:T(8,128)}, f32[112,1024]{1,0:T(8,128)S(1)}, u32[]{:S(2)}, u32[]{:S(2)}) collective-permute-start(f32[112,1024]{1,0:T(8,128)} %get-tuple-element.105), channel_id=1, source_target_pairs={{0,2},{1,3},{2,0},{3,1},{4,6},{5,7},{6,4},{7,5},{8,10},{9,11},{10,... | collective-permute-start | bytes 1376264 | tf_op jit(solution)/shard_map/ppermute | solution.py:401
  1019.3 22.1 %collective-permute-start.26 = (f32[112,1024]{1,0:T(8,128)}, f32[112,1024]{1,0:T(8,128)S(1)}, u32[]{:S(2)}, u32[]{:S(2)}) collective-permute-start(f32[112,1024]{1,0:T(8,128)} %get-tuple-element.106), channel_id=1, source_target_pairs={{0,3},{1,2},{2,1},{3,0},{4,7},{5,6},{6,5},{7,4},{8,11},{9,10},{10,... | collective-permute-start | bytes 1376264 | tf_op jit(solution)/shard_map/ppermute | solution.py:401
  1020.8 21.4 %collective-permute-start.22 = (f32[1,897]{1,0:T(1,128)S(1)}, f32[1,897]{1,0:T(1,128)S(1)}, u32[]{:S(2)}, u32[]{:S(2)}) collective-permute-start(f32[1,897]{1,0:T(1,128)S(1)} %add.157), channel_id=1, source_target_pairs={{0,4},{1,5},{2,6},{3,7},{4,0},{5,1},{6,2},{7,3},{8,12},{9,13},{10,... | collective-permute-start | bytes 10772 | tf_op jit(solution)/shard_map/ppermute | solution.py:401
  1021.9 74.4 %collective-permute-start.27 = (f32[112,1024]{1,0:T(8,128)}, f32[112,1024]{1,0:T(8,128)}, u32[]{:S(2)}, u32[]{:S(2)}) collective-permute-start(f32[112,1024]{1,0:T(8,128)} %get-tuple-element.107), channel_id=1, source_target_pairs={{0,4},{1,5},{2,6},{3,7},{4,0},{5,1},{6,2},{7,3},{8,12},{9,13},{10,... | collective-permute-start | bytes 1376264 | tf_op jit(solution)/shard_map/ppermute | solution.py:401
  1033.3 63.0 %collective-permute-start.28 = (f32[112,1024]{1,0:T(8,128)}, f32[112,1024]{1,0:T(8,128)}, u32[]{:S(2)}, u32[]{:S(2)}) collective-permute-start(f32[112,1024]{1,0:T(8,128)} %get-tuple-element.108), channel_id=1, source_target_pairs={{0,5},{1,4},{2,7},{3,6},{4,1},{5,0},{6,3},{7,2},{8,13},{9,12},{10,... | collective-permute-start | bytes 1376264 | tf_op jit(solution)/shard_map/ppermute | solution.py:401
  1042.2 54.1 %collective-permute-start.29 = (f32[112,1024]{1,0:T(8,128)}, f32[112,1024]{1,0:T(8,128)}, u32[]{:S(2)}, u32[]{:S(2)}) collective-permute-start(f32[112,1024]{1,0:T(8,128)} %get-tuple-element.109), channel_id=1, source_target_pairs={{0,6},{1,7},{2,4},{3,5},{4,2},{5,3},{6,0},{7,1},{8,14},{9,15},{10,... | collective-permute-start | bytes 1376264 | tf_op jit(solution)/shard_map/ppermute | solution.py:401
  1042.2 54.1 %collective-permute-start.30 = (f32[112,1024]{1,0:T(8,128)}, f32[112,1024]{1,0:T(8,128)}, u32[]{:S(2)}, u32[]{:S(2)}) collective-permute-start(f32[112,1024]{1,0:T(8,128)} %get-tuple-element.110), channel_id=1, source_target_pairs={{0,7},{1,6},{2,5},{3,4},{4,3},{5,2},{6,1},{7,0},{8,15},{9,14},{10,... | collective-permute-start | bytes 1376264 | tf_op jit(solution)/shard_map/ppermute | solution.py:401
  1065.3 31.0 %copy-start.10 = (f32[112,1024]{1,0:T(8,128)S(1)}, f32[112,1024]{1,0:T(8,128)}, u32[]{:S(2)}) copy-start(f32[112,1024]{1,0:T(8,128)} %get-tuple-element.103.refs_0_) | copy-start | bytes 1376260
  1065.3 31.0 %copy-start.12 = (f32[112,1024]{1,0:T(8,128)S(1)}, f32[112,1024]{1,0:T(8,128)}, u32[]{:S(2)}) copy-start(f32[112,1024]{1,0:T(8,128)} %copy-done.11) | copy-start | bytes 1376260
  (32 other events, 284.3 us)

commit v4 on v3

--- a/solution.py
+++ b/solution.py
@@ -13,7 +13,7 @@
 VB = 256
 NT = (((1,), (1,)), ((), ()))
 
-CHUNKS = ((0, 4), (4, 7), (13, 6), (11, 2))
+CHUNKS = ((0, 3), (3, 7), (13, 6), (10, 3))
 
 
 def logit_kernel(vocab_loc, nblk, first, d_ref, *refs):
@@ -485,14 +485,13 @@
         grad_hidden = jnp.where(plane == 0, jnp.concatenate([dh_half, dh_other]), jnp.concatenate([dh_other, dh_half]))
         own = jnp.sum(mask_all[0] * (log_norm[0] - stat[2, 0])) * (1.0 / n_tp)
         sums = jnp.concatenate([jnp.sum(grad_norm * x_hat, axis=0), own[None]])[None]
-        for axis, mask in (("tp", 1), ("dp", 1), ("dp", 2), ("dp", 4)):
+        for axis, mask in (("dp", 1), ("dp", 2), ("dp", 4), ("tp", 1)):
             sums = sums + swap(sums, mask, axis)
 
         out = None
-        for c, (off, steps, pieces) in enumerate(sent):
+        for off, steps, pieces in sent:
             ragged = n_dp * nblk * VB - (nblk // 2 - off - steps) * 2 * VB > vocab_loc
-            turn = dev if c < len(sent) - 1 else after(dev, grad_hidden, sums)
-            out = (place if ragged else place_copy)(turn, pieces, out, off, steps, vocab_loc, nblk)
+            out = (place if ragged else place_copy)(dev, pieces, out, off, steps, vocab_loc, nblk)
 
         grad_gain, loss_value = sums[0, :hid], sums[0, hid] / mask_count
         return loss_value, grad_hidden.reshape(n_seq, seq_len, hid), out.T, grad_gain

time: 1120 us -> 1180 us (1.054)
  starting transfers between devices: 47.5 us -> 103 us
    ppermute x52, starting transfers between devices: 47.5 us -> 103 us  [swap(): return lax.ppermute(x, axis, [(i, i ^ mask) for i in range(size)])]
  transfers between devices with their start and end apart: 52 -> 52, of which waited for: 17 -> 16; matrix products, arithmetic and copies ran while one was open for 2% -> 3% of each run, Pallas kernels for 33% -> 32%
where the time goes in v4:
time: 1180 us; the launch traced here: 1170 us
  Pallas kernels  590 us (50%)
  waiting for transfers between devices  413 us (35%)
  starting transfers between devices  103 us (9%)
  other arithmetic  30.9 us (3%)
  local copies, waits for them, and re-layouts  22.1 us (2%)
    ppermute x52, waiting for transfers between devices, swap(): return lax.ppermute(x, axis, [(i, i ^ mask) for i in range(size)])  413 us
    pallas_call x4, Pallas kernels, logits_call(): pl.pallas_call(functools.partial(logit_kernel, vocab_loc, nblk, first), g...  201 us
    pallas_call x3, Pallas kernels, hidden_grad(): pl.pallas_call(functools.partial(hidden_grad_kernel, nblk, inner, n_out),...  172 us
    pallas_call x4, Pallas kernels, embed_grad(): pl.pallas_call(functools.partial(embed_grad_kernel, nblk, off, n_dp), gri...  168 us
    ppermute x52, starting transfers between devices, swap(): return lax.ppermute(x, axis, [(i, i ^ mask) for i in range(size)])  103 us
    pallas_call x1, Pallas kernels, place(): pl.pallas_call(functools.partial(place_kernel, n_dp, per, off, last), gri...  29.8 us
  transfers between devices with their start and end apart: 52, of which 16 were waited for; matrix products, arithmetic and copies ran while one was open for 3% of the time, Pallas kernels for 32%

profile of v4, /device:TPU:0, one launch (start us, length us, event | category | flops | bytes accessed | tf_op | source)
XLA Modules:
  0.0 1166.1 jit_solution(6647573370722180399)
XLA Ops:
  0.7 1.5 bitcast_convert_fusion
  2.5 3.2 collective-permute-start.5
  5.7 1.5 collective-permute-start.3
  7.2 59.7 %collective-permute-done.5.refs_0_ = f32[776,896]{1,0:T(8,128)} collective-permute-done((f32[776,896]{1,0:T(8,128)S(1)}, f32[776,896]{1,0:T(8,128)}, u32[]{:S(2)}, u32[]{:S(2)}) %collective-permute-start.5) | collective-permute-done | bytes 2781216 | tf_op jit(solution)/shard_map/ppermute | solution.py:401
  68.1 59.0 %collective-permute-done.3.refs_0_ = f32[776,896]{1,0:T(8,128)} collective-permute-done((f32[776,896]{1,0:T(8,128)S(1)}, f32[776,896]{1,0:T(8,128)}, u32[]{:S(2)}, u32[]{:S(2)}) %collective-permute-start.3) | collective-permute-done | bytes 2781216 | tf_op jit(solution)/shard_map/ppermute | solution.py:401
  127.2 51.5 %logits.4 = (f32[38,6144,256]{2,1,0:T(8,128)}, bf16[896,6144]{1,0:T(8,128)(2,1)}, s32[6144,128]{1,0:T(8,128)}, f32[8,1536]{1,0:T(8,128)}, bf16[9728,896]{1,0:T(8,128)(2,1)}) custom-call(s32[2]{0:T(128)} %pad_add_fusion.d_ref, f32[776,896]{1,0:T(8,128)} %copy-done.19, f32[776,896]{1,0:T(8,128)} %collective-permute-done.2.refs_1_, s32[1]{0:T(128)} %bitcast.3.refs_2_, ...), custom_call_target="tpu_custom_call" | custom-call | flops 26776436736 | bytes 59768832 | tf_op jit(solution)/shard_map/logits/pallas_call | solution.py:117
  179.9 49.8 %logits.5 = (f32[38,6144,256]{2,1,0:T(8,128)}, bf16[896,6144]{1,0:T(8,128)(2,1)}, s32[6144,128]{1,0:T(8,128)}, f32[8,1536]{1,0:T(8,128)}) custom-call(s32[2]{0:T(128)} %pad_add_fusion.d_ref, f32[776,896]{1,0:T(8,128)} %collective-permute-done.5.refs_0_, ...), custom_call_target="tpu_custom_call", output_to_operand_aliasing={{0}: (6, {}), {1}: (7, {}), {2}: (8, {})} | custom-call | flops 26776436736 | bytes 59768832 | tf_op jit(solution)/shard_map/logits/pallas_call | solution.py:117
  230.5 49.9 %logits.6 = (f32[38,6144,256]{2,1,0:T(8,128)}, bf16[896,6144]{1,0:T(8,128)(2,1)}, s32[6144,128]{1,0:T(8,128)}, f32[8,1536]{1,0:T(8,128)}) custom-call(s32[2]{0:T(128)} %pad_add_fusion.d_ref, f32[776,896]{1,0:T(8,128)} %collective-permute-done.3.refs_0_, ...), custom_call_target="tpu_custom_call", output_to_operand_aliasing={{0}: (6, {}), {1}: (7, {}), {2}: (8, {})} | custom-call | flops 26776436736 | bytes 59768832 | tf_op jit(solution)/shard_map/logits/pallas_call | solution.py:117
  281.2 49.7 %logits.7 = (f32[38,6144,256]{2,1,0:T(8,128)}, bf16[896,6144]{1,0:T(8,128)(2,1)}, s32[6144,128]{1,0:T(8,128)}, f32[8,1536]{1,0:T(8,128)}) custom-call(s32[2]{0:T(128)} %pad_add_fusion.d_ref, f32[776,896]{1,0:T(8,128)} %collective-permute-done.refs_0_, ...), custom_call_target="tpu_custom_call", output_to_operand_aliasing={{0}: (6, {}), {1}: (7, {}), {2}: (8, {})} | custom-call | flops 26776436736 | bytes 59768832 | tf_op jit(solution)/shard_map/logits/pallas_call | solution.py:117
  332.0 1.4 slice_reduce_fusion.2
  333.8 1.4 slice_reduce_fusion.4
  335.2 3.2 collective-permute-done.8
  339.2 1.6 collective-permute-start.9
  340.7 1.5 slice_reduce_fusion.6
  345.4 1.6 collective-permute-start.10
  347.0 2.7 collective-permute-done.10
  350.5 2.2 broadcast_in_dim.12.rest_1_.w_ref
  352.7 2.2 broadcast_in_dim.11.rest_0_.lse_ref
  354.9 30.2 %embed_grad.4 = (f32[112,1536]{1,0:T(8,128)}, f32[112,1536]{1,0:T(8,128)}, f32[112,1536]{1,0:T(8,128)}, f32[112,1536]{1,0:T(8,128)}, f32[112,1536]{1,0:T(8,128)}...) custom-call(s32[2]{0:T(128)} %pad_add_fusion.d_ref, f32[38,6144,256]{2,1,0:T(8,128)} %get-tuple-element.77.z_ref, ...), custom_call_target="tpu_custom_call" | custom-call | flops 16911433728 | bytes 37748736 | tf_op jit(solution)/shard_map/embed_grad/pallas_call | solution.py:287
  385.1 57.0 %embed_grad.5 = (f32[112,3584]{1,0:T(8,128)}, f32[112,3584]{1,0:T(8,128)}, f32[112,3584]{1,0:T(8,128)}, f32[112,3584]{1,0:T(8,128)}, f32[112,3584]{1,0:T(8,128)}...) custom-call(s32[2]{0:T(128)} %pad_add_fusion.d_ref, f32[38,6144,256]{2,1,0:T(8,128)} %get-tuple-element.77.z_ref, ...), custom_call_target="tpu_custom_call" | custom-call | flops 39460012032 | bytes 88080384 | tf_op jit(solution)/shard_map/embed_grad/pallas_call | solution.py:287
  442.1 78.6 %hidden_grad.3 = f32[3072,896]{1,0:T(8,128)} custom-call(s32[2]{0:T(128)} %pad_add_fusion.d_ref, f32[38,6144,256]{2,1,0:T(8,128)} %get-tuple-element.77.z_ref, f32[6144,128]{1,0:T(8,128)} %broadcast_in_dim.11.rest_0_.lse_ref, f32[6144,128]{1,0:T(8,128)} %broadcast_in_dim.12.rest_1_.w_ref, s32[6144,128]{1,0:T(8,128)} %get-tuple-element.82.rest_2_.lab_ref, ...), custom_call_target="tpu_custom_call" | custom-call | flops 53552873472 | bytes 119537664 | tf_op jit(solution)/shard_map/hidden_grad/pallas_call | solution.py:210
  523.1 50.7 %embed_grad.6 = (f32[112,3072]{1,0:T(8,128)}, f32[112,3072]{1,0:T(8,128)}, f32[112,3072]{1,0:T(8,128)}, f32[112,3072]{1,0:T(8,128)}, f32[112,3072]{1,0:T(8,128)}...) custom-call(s32[2]{0:T(128)} %pad_add_fusion.d_ref, f32[38,6144,256]{2,1,0:T(8,128)} %get-tuple-element.77.z_ref, ...), custom_call_target="tpu_custom_call" | custom-call | flops 33822867456 | bytes 75497472 | tf_op jit(solution)/shard_map/embed_grad/pallas_call | solution.py:287
  573.9 1.7 collective-permute-start.49
  575.5 46.7 %hidden_grad.4 = (f32[384,896]{1,0:T(8,128)}, f32[384,896]{1,0:T(8,128)}, f32[384,896]{1,0:T(8,128)}, f32[384,896]{1,0:T(8,128)}) custom-call(s32[2]{0:T(128)} %pad_add_fusion.d_ref, f32[38,6144,256]{2,1,0:T(8,128)} %get-tuple-element.77.z_ref, f32[6144,128]{1,0:T(8,128)} %broadcast_in_dim.11.rest_0_.lse_ref, f32[6144,128]{1,0:T(8,128)} %broadcast_in_dim.12.rest_1_.w_ref, ...), custom_call_target="tpu_custom_call" | custom-call | flops 26776436736 | bytes 59768832 | tf_op jit(solution)/shard_map/hidden_grad/pallas_call | solution.py:210
  622.4 1.6 collective-permute-start.13
  625.0 1.5 collective-permute-start.51
  626.5 17.1 %collective-permute-done.50.refs_6_ = f32[112,1536]{1,0:T(8,128)S(1)} collective-permute-done((f32[112,1536]{1,0:T(8,128)S(1)}, f32[112,1536]{1,0:T(8,128)S(1)}, u32[]{:S(2)}, u32[]{:S(2)}) %collective-permute-start.50) | collective-permute-done | bytes 688160 | tf_op jit(solution)/shard_map/ppermute | solution.py:401
  645.1 11.1 collective-permute-done.51.refs_7_
  657.0 2.3 collective-permute-start.33
  659.8 1.6 collective-permute-start.12
  661.4 23.8 %collective-permute-done.15 = f32[384,896]{1,0:T(8,128)} collective-permute-done((f32[384,896]{1,0:T(8,128)}, f32[384,896]{1,0:T(8,128)}, u32[]{:S(2)}, u32[]{:S(2)}) %collective-permute-start.15) | collective-permute-done | bytes 1376288 | tf_op jit(solution)/shard_map/ppermute | solution.py:401
  685.2 1.6 collective-permute-start.17
  686.8 46.6 %hidden_grad.5 = (f32[384,896]{1,0:T(8,128)}, f32[384,896]{1,0:T(8,128)}, f32[384,896]{1,0:T(8,128)}, f32[384,896]{1,0:T(8,128)}) custom-call(s32[2]{0:T(128)} %pad_add_fusion.d_ref, f32[38,6144,256]{2,1,0:T(8,128)} %get-tuple-element.77.z_ref, f32[6144,128]{1,0:T(8,128)} %broadcast_in_dim.11.rest_0_.lse_ref, f32[6144,128]{1,0:T(8,128)} %broadcast_in_dim.12.rest_1_.w_ref, ...), custom_call_target="tpu_custom_call" | custom-call | flops 26776436736 | bytes 59768832 | tf_op jit(solution)/shard_map/hidden_grad/pallas_call | solution.py:210
  733.4 3.1 add.140
  736.6 2.7 add.142
  739.9 3.8 collective-permute-done.17
  744.3 2.7 add.144
  747.0 1.4 collective-permute-start.18
  748.7 1.6 collective-permute-start.39
  750.2 22.4 %collective-permute-done.14 = f32[384,896]{1,0:T(8,128)} collective-permute-done((f32[384,896]{1,0:T(8,128)}, f32[384,896]{1,0:T(8,128)}, u32[]{:S(2)}, u32[]{:S(2)}) %collective-permute-start.14) | collective-permute-done | bytes 1376288 | tf_op jit(solution)/shard_map/ppermute | solution.py:401
  772.6 33.9 %collective-permute-done.16 = f32[384,896]{1,0:T(8,128)} collective-permute-done((f32[384,896]{1,0:T(8,128)}, f32[384,896]{1,0:T(8,128)}, u32[]{:S(2)}, u32[]{:S(2)}) %collective-permute-start.16) | collective-permute-done | bytes 1376288 | tf_op jit(solution)/shard_map/ppermute | solution.py:401
  811.5 4.8 fusion.4
  816.3 18.3 %collective-permute-done.35.refs_5_ = f32[112,3072]{1,0:T(8,128)} collective-permute-done((f32[112,3072]{1,0:T(8,128)}, f32[112,3072]{1,0:T(8,128)}, u32[]{:S(2)}, u32[]{:S(2)}) %collective-permute-start.35) | collective-permute-done | bytes 1376288 | tf_op jit(solution)/shard_map/ppermute | solution.py:401
  834.6 58.8 %collective-permute-start.19 = (f32[1,897]{1,0:T(1,128)S(1)}, f32[1,897]{1,0:T(1,128)S(1)}, u32[]{:S(2)}, u32[]{:S(2)}) collective-permute-start(f32[1,897]{1,0:T(1,128)S(1)} %bitcast.92), channel_id=1, source_target_pairs={{0,1},{1,0},{2,3},{3,2},{4,5},{5,4},{6,7},{7,6},{8,9},{9,8},{10,11... | collective-permute-start | bytes 10772 | tf_op jit(solution)/shard_map/ppermute | solution.py:401
  893.7 1.6 collective-permute-start.42
  895.3 1.4 collective-permute-start.43
  897.9 30.2 %embed_grad.7 = (f32[112,1536]{1,0:T(8,128)}, f32[112,1536]{1,0:T(8,128)}, f32[112,1536]{1,0:T(8,128)}, f32[112,1536]{1,0:T(8,128)}, f32[112,1536]{1,0:T(8,128)}...) custom-call(s32[2]{0:T(128)} %pad_add_fusion.d_ref, f32[38,6144,256]{2,1,0:T(8,128)} %get-tuple-element.77.z_ref, ...), custom_call_target="tpu_custom_call" | custom-call | flops 16911433728 | bytes 37748736 | tf_op jit(solution)/shard_map/embed_grad/pallas_call | solution.py:287
  928.1 2.9 collective-permute-done.40.refs_3_
  931.4 69.1 %collective-permute-done.41.refs_4_ = f32[112,3584]{1,0:T(8,128)} collective-permute-done((f32[112,3584]{1,0:T(8,128)}, f32[112,3584]{1,0:T(8,128)}, u32[]{:S(2)}, u32[]{:S(2)}) %collective-permute-start.41) | collective-permute-done | bytes 1605664 | tf_op jit(solution)/shard_map/ppermute | solution.py:401
  1000.6 1.6 collective-permute-start.25
  1002.2 31.8 %collective-permute-done.42.refs_5_ = f32[112,3584]{1,0:T(8,128)} collective-permute-done((f32[112,3584]{1,0:T(8,128)}, f32[112,3584]{1,0:T(8,128)}, u32[]{:S(2)}, u32[]{:S(2)}) %collective-permute-start.42) | collective-permute-done | bytes 1605664 | tf_op jit(solution)/shard_map/ppermute | solution.py:401
  1033.9 1.6 collective-permute-start.26
  1035.9 3.0 fusion.6
  1038.9 13.1 %collective-permute-done.20 = f32[1,897]{1,0:T(1,128)S(1)} collective-permute-done((f32[1,897]{1,0:T(1,128)S(1)}, f32[1,897]{1,0:T(1,128)S(1)}, u32[]{:S(2)}, u32[]{:S(2)}) %collective-permute-start.20) | collective-permute-done | bytes 3620 | tf_op jit(solution)/shard_map/ppermute | solution.py:401
  1052.0 1.4 collective-permute-start.23
  1054.7 1.6 collective-permute-start.27
  1058.1 1.7 collective-permute-start.29
  1061.1 41.4 %collective-permute-done.27.refs_4_ = f32[112,1536]{1,0:T(8,128)S(1)} collective-permute-done((f32[112,1536]{1,0:T(8,128)S(1)}, f32[112,1536]{1,0:T(8,128)S(1)}, u32[]{:S(2)}, u32[]{:S(2)}) %collective-permute-start.27) | collective-permute-done | bytes 688160 | tf_op jit(solution)/shard_map/ppermute | solution.py:401
  1103.4 1.4 collective-permute-start.22
  1109.2 4.3 shard_map.84.refs_8_
  1113.6 9.2 shard_map.85.refs_8_
  1122.9 29.8 %place.1.refs_8_ = f32[112,75968]{1,0:T(8,128)} custom-call(s32[2]{0:T(128)} %pad_add_fusion.d_ref, f32[112,3072]{1,0:T(8,128)} %get-tuple-element.89.refs_0_, f32[112,3072]{1,0:T(8,128)} %collective-permute-done.31.refs_1_, f32[112,3072]{1,0:T(8,128)} %copy-done.21, f32[112,3072]{1,0:T(8,128)} %copy-done.22, ...), custom_call_target="tpu_custom_call", output_to_operand_aliasing={{}: (9, {})} | custom-call | flops 2752512 | bytes 22020096 | tf_op jit(solution)/shard_map/place/pallas_call | solution.py:381
  1152.7 5.8 shard_map.86
  1160.3 4.5 maximum_select_fusion
  (221 shorter events, 33.3 us)
Async XLA Ops:
  2.2 65.3 %copy-start.38 = (bf16[896]{0:T(1024)(128)(2,1)S(1)}, bf16[896]{0:T(1024)(128)(2,1)}, u32[]{:S(2)}) copy-start(bf16[896]{0:T(1024)(128)(2,1)} %param.8) | copy-start | bytes 5380
  2.4 124.7 %copy-start.19 = (f32[776,896]{1,0:T(8,128)}, f32[776,896]{1,0:T(8,128)S(1)}, u32[]{:S(2)}) copy-start(f32[776,896]{1,0:T(8,128)S(1)} %select_maximum_fusion.refs_0_) | copy-start | bytes 8343556
  2.5 64.5 %collective-permute-start.5 = (f32[776,896]{1,0:T(8,128)S(1)}, f32[776,896]{1,0:T(8,128)}, u32[]{:S(2)}, u32[]{:S(2)}) collective-permute-start(f32[776,896]{1,0:T(8,128)S(1)} %select_maximum_fusion.refs_0_), channel_id=1, source_target_pairs={{0,2},{1,3},{2,0},{3,1},{4,6},{5,7},{6,4},{7,5},{8,10},{9,11},{10,... | collective-permute-start | bytes 8343560 | tf_op jit(solution)/shard_map/ppermute | solution.py:401
  5.7 121.5 %collective-permute-start.3 = (f32[776,896]{1,0:T(8,128)S(1)}, f32[776,896]{1,0:T(8,128)}, u32[]{:S(2)}, u32[]{:S(2)}) collective-permute-start(f32[776,896]{1,0:T(8,128)S(1)} %select_maximum_fusion.refs_0_), channel_id=1, source_target_pairs={{0,4},{1,5},{2,6},{3,7},{4,0},{5,1},{6,2},{7,3},{8,12},{9,13},{10,... | collective-permute-start | bytes 8343560 | tf_op jit(solution)/shard_map/ppermute | solution.py:401
  7.2 119.9 %collective-permute-start.2 = (f32[776,896]{1,0:T(8,128)S(1)}, f32[776,896]{1,0:T(8,128)}, u32[]{:S(2)}, u32[]{:S(2)}) collective-permute-start(f32[776,896]{1,0:T(8,128)S(1)} %select_maximum_fusion.refs_0_), channel_id=1, source_target_pairs={{0,1},{1,0},{2,3},{3,2},{4,5},{5,4},{6,7},{7,6},{8,9},{9,8},{10,11... | collective-permute-start | bytes 8343560 | tf_op jit(solution)/shard_map/ppermute | solution.py:401
  7.2 172.2 %collective-permute-start = (f32[776,896]{1,0:T(8,128)S(1)}, f32[776,896]{1,0:T(8,128)}, u32[]{:S(2)}, u32[]{:S(2)}) collective-permute-start(f32[776,896]{1,0:T(8,128)S(1)} %select_maximum_fusion.refs_0_), channel_id=1, source_target_pairs={{0,6},{1,7},{2,4},{3,5},{4,2},{5,3},{6,0},{7,1},{8,14},{9,15},{10,... | collective-permute-start | bytes 8343560 | tf_op jit(solution)/shard_map/ppermute | solution.py:401
  66.9 113.0 %collective-permute-start.6 = (f32[776,896]{1,0:T(8,128)}, f32[776,896]{1,0:T(8,128)}, u32[]{:S(2)}, u32[]{:S(2)}) collective-permute-start(f32[776,896]{1,0:T(8,128)} %collective-permute-done.5.refs_0_), channel_id=1, source_target_pairs={{0,1},{1,0},{2,3},{3,2},{4,5},{5,4},{6,7},{7,6},{8,9},{9,8},{10,11... | collective-permute-start | bytes 8343560 | tf_op jit(solution)/shard_map/ppermute | solution.py:401
  127.1 103.4 %collective-permute-start.4 = (f32[776,896]{1,0:T(8,128)}, f32[776,896]{1,0:T(8,128)}, u32[]{:S(2)}, u32[]{:S(2)}) collective-permute-start(f32[776,896]{1,0:T(8,128)} %collective-permute-done.3.refs_0_), channel_id=1, source_target_pairs={{0,1},{1,0},{2,3},{3,2},{4,5},{5,4},{6,7},{7,6},{8,9},{9,8},{10,11... | collective-permute-start | bytes 8343560 | tf_op jit(solution)/shard_map/ppermute | solution.py:401
  179.5 101.7 %collective-permute-start.1 = (f32[776,896]{1,0:T(8,128)}, f32[776,896]{1,0:T(8,128)}, u32[]{:S(2)}, u32[]{:S(2)}) collective-permute-start(f32[776,896]{1,0:T(8,128)} %collective-permute-done.refs_0_), channel_id=1, source_target_pairs={{0,1},{1,0},{2,3},{3,2},{4,5},{5,4},{6,7},{7,6},{8,9},{9,8},{10,11... | collective-permute-start | bytes 8343560 | tf_op jit(solution)/shard_map/ppermute | solution.py:401
  331.9 1.6 collective-permute-start.7
  333.7 4.7 collective-permute-start.8
  339.2 5.5 collective-permute-start.9
  345.4 4.4 collective-permute-start.10
  520.7 53.1 %collective-permute-start.11 = (f32[3072,896]{1,0:T(8,128)}, f32[3072,896]{1,0:T(8,128)}, u32[]{:S(2)}, u32[]{:S(2)}) collective-permute-start(f32[3072,896]{1,0:T(8,128)} %hidden_grad.3), channel_id=1, source_target_pairs={{0,1},{1,0},{2,3},{3,2},{4,5},{5,4},{6,7},{7,6},{8,9},{9,8},{10,11... | collective-permute-start | bytes 33030152 | tf_op jit(solution)/shard_map/ppermute | solution.py:401
  520.8 101.4 %collective-permute-start.45 = (f32[112,1536]{1,0:T(8,128)}, f32[112,1536]{1,0:T(8,128)}, u32[]{:S(2)}, u32[]{:S(2)}) collective-permute-start(f32[112,1536]{1,0:T(8,128)} %get-tuple-element.123), channel_id=1, source_target_pairs={{0,1},{1,0},{2,3},{3,2},{4,5},{5,4},{6,7},{7,6},{8,9},{9,8},{10,11... | collective-permute-start | bytes 2064392 | tf_op jit(solution)/shard_map/ppermute | solution.py:401
  521.3 101.1 %collective-permute-start.46 = (f32[112,1536]{1,0:T(8,128)}, f32[112,1536]{1,0:T(8,128)}, u32[]{:S(2)}, u32[]{:S(2)}) collective-permute-start(f32[112,1536]{1,0:T(8,128)} %get-tuple-element.124), channel_id=1, source_target_pairs={{0,2},{1,3},{2,0},{3,1},{4,6},{5,7},{6,4},{7,5},{8,10},{9,11},{10,... | collective-permute-start | bytes 2064392 | tf_op jit(solution)/shard_map/ppermute | solution.py:401
  521.8 102.1 %collective-permute-start.47 = (f32[112,1536]{1,0:T(8,128)}, f32[112,1536]{1,0:T(8,128)}, u32[]{:S(2)}, u32[]{:S(2)}) collective-permute-start(f32[112,1536]{1,0:T(8,128)} %get-tuple-element.125), channel_id=1, source_target_pairs={{0,3},{1,2},{2,1},{3,0},{4,7},{5,6},{6,5},{7,4},{8,11},{9,10},{10,... | collective-permute-start | bytes 2064392 | tf_op jit(solution)/shard_map/ppermute | solution.py:401
  522.7 51.2 %copy-start.45 = (f32[112,1536]{1,0:T(8,128)S(1)}, f32[112,1536]{1,0:T(8,128)}, u32[]{:S(2)}) copy-start(f32[112,1536]{1,0:T(8,128)} %get-tuple-element.127) | copy-start | bytes 2064388
  522.7 101.7 %collective-permute-start.48 = (f32[112,1536]{1,0:T(8,128)}, f32[112,1536]{1,0:T(8,128)}, u32[]{:S(2)}, u32[]{:S(2)}) collective-permute-start(f32[112,1536]{1,0:T(8,128)} %get-tuple-element.126), channel_id=1, source_target_pairs={{0,4},{1,5},{2,6},{3,7},{4,0},{5,1},{6,2},{7,3},{8,12},{9,13},{10,... | collective-permute-start | bytes 2064392 | tf_op jit(solution)/shard_map/ppermute | solution.py:401
  573.9 50.5 %copy-start.44 = (f32[112,1536]{1,0:T(8,128)S(1)}, f32[112,1536]{1,0:T(8,128)}, u32[]{:S(2)}) copy-start(f32[112,1536]{1,0:T(8,128)} %get-tuple-element.128) | copy-start | bytes 2064388
  573.9 51.2 %copy-start.43 = (f32[112,1536]{1,0:T(8,128)S(1)}, f32[112,1536]{1,0:T(8,128)}, u32[]{:S(2)}) copy-start(f32[112,1536]{1,0:T(8,128)} %get-tuple-element.129) | copy-start | bytes 2064388
  573.9 51.2 %collective-permute-start.49 = (f32[112,1536]{1,0:T(8,128)S(1)}, f32[112,1536]{1,0:T(8,128)S(1)}, u32[]{:S(2)}, u32[]{:S(2)}) collective-permute-start(f32[112,1536]{1,0:T(8,128)S(1)} %copy-done.45), channel_id=1, source_target_pairs={{0,5},{1,4},{2,7},{3,6},{4,1},{5,0},{6,3},{7,2},{8,13},{9,12},{10,... | collective-permute-start | bytes 2064392 | tf_op jit(solution)/shard_map/ppermute | solution.py:401
  622.2 37.0 %collective-permute-start.31 = (f32[112,3072]{1,0:T(8,128)}, f32[112,3072]{1,0:T(8,128)}, u32[]{:S(2)}, u32[]{:S(2)}) collective-permute-start(f32[112,3072]{1,0:T(8,128)} %get-tuple-element.109), channel_id=1, source_target_pairs={{0,1},{1,0},{2,3},{3,2},{4,5},{5,4},{6,7},{7,6},{8,9},{9,8},{10,11... | collective-permute-start | bytes 4128776 | tf_op jit(solution)/shard_map/ppermute | solution.py:401
  622.4 37.5 %collective-permute-start.13 = (f32[384,896]{1,0:T(8,128)}, f32[384,896]{1,0:T(8,128)}, u32[]{:S(2)}, u32[]{:S(2)}) collective-permute-start(f32[384,896]{1,0:T(8,128)} %get-tuple-element.95), channel_id=1, source_target_pairs={{0,8},{8,0},{1,9},{9,1},{2,10},{10,2},{3,11},{11,3},{4,12},{12,4},... | collective-permute-start | bytes 4128776 | tf_op jit(solution)/shard_map/ppermute | solution.py:401
  623.9 61.3 %collective-permute-start.15 = (f32[384,896]{1,0:T(8,128)}, f32[384,896]{1,0:T(8,128)}, u32[]{:S(2)}, u32[]{:S(2)}) collective-permute-start(f32[384,896]{1,0:T(8,128)} %get-tuple-element.97), channel_id=1, source_target_pairs={{0,8},{8,0},{1,9},{9,1},{2,10},{10,2},{3,11},{11,3},{4,12},{12,4},... | collective-permute-start | bytes 4128776 | tf_op jit(solution)/shard_map/ppermute | solution.py:401
  624.4 19.2 %collective-permute-start.50 = (f32[112,1536]{1,0:T(8,128)S(1)}, f32[112,1536]{1,0:T(8,128)S(1)}, u32[]{:S(2)}, u32[]{:S(2)}) collective-permute-start(f32[112,1536]{1,0:T(8,128)S(1)} %copy-done.44), channel_id=1, source_target_pairs={{0,6},{1,7},{2,4},{3,5},{4,2},{5,3},{6,0},{7,1},{8,14},{9,15},{10,... | collective-permute-start | bytes 2064392 | tf_op jit(solution)/shard_map/ppermute | solution.py:401
  625.0 108.4 %copy-start.2 = (f32[112,1536]{1,0:T(8,128)}, f32[112,1536]{1,0:T(8,128)S(1)}, u32[]{:S(2)}) copy-start(f32[112,1536]{1,0:T(8,128)S(1)} %collective-permute-done.49.refs_5_) | copy-start | bytes 2064388
  625.0 31.1 %collective-permute-start.51 = (f32[112,1536]{1,0:T(8,128)S(1)}, f32[112,1536]{1,0:T(8,128)S(1)}, u32[]{:S(2)}, u32[]{:S(2)}) collective-permute-start(f32[112,1536]{1,0:T(8,128)S(1)} %copy-done.43), channel_id=1, source_target_pairs={{0,7},{1,6},{2,5},{3,4},{4,3},{5,2},{6,1},{7,0},{8,15},{9,14},{10,... | collective-permute-start | bytes 2064392 | tf_op jit(solution)/shard_map/ppermute | solution.py:401
  644.4 94.8 %collective-permute-start.32 = (f32[112,3072]{1,0:T(8,128)}, f32[112,3072]{1,0:T(8,128)S(1)}, u32[]{:S(2)}, u32[]{:S(2)}) collective-permute-start(f32[112,3072]{1,0:T(8,128)} %get-tuple-element.110), channel_id=1, source_target_pairs={{0,2},{1,3},{2,0},{3,1},{4,6},{5,7},{6,4},{7,5},{8,10},{9,11},{10,... | collective-permute-start | bytes 4128776 | tf_op jit(solution)/shard_map/ppermute | solution.py:401
  657.0 90.0 %collective-permute-start.33 = (f32[112,3072]{1,0:T(8,128)}, f32[112,3072]{1,0:T(8,128)S(1)}, u32[]{:S(2)}, u32[]{:S(2)}) collective-permute-start(f32[112,3072]{1,0:T(8,128)} %get-tuple-element.111), channel_id=1, source_target_pairs={{0,3},{1,2},{2,1},{3,0},{4,7},{5,6},{6,5},{7,4},{8,11},{9,10},{10,... | collective-permute-start | bytes 4128776 | tf_op jit(solution)/shard_map/ppermute | solution.py:401
  659.3 89.3 %collective-permute-start.34 = (f32[112,3072]{1,0:T(8,128)}, f32[112,3072]{1,0:T(8,128)}, u32[]{:S(2)}, u32[]{:S(2)}) collective-permute-start(f32[112,3072]{1,0:T(8,128)} %get-tuple-element.112), channel_id=1, source_target_pairs={{0,4},{1,5},{2,6},{3,7},{4,0},{5,1},{6,2},{7,3},{8,12},{9,13},{10,... | collective-permute-start | bytes 4128776 | tf_op jit(solution)/shard_map/ppermute | solution.py:401
  659.8 88.8 %collective-permute-start.12 = (f32[384,896]{1,0:T(8,128)}, f32[384,896]{1,0:T(8,128)}, u32[]{:S(2)}, u32[]{:S(2)}) collective-permute-start(f32[384,896]{1,0:T(8,128)} %get-tuple-element.91), channel_id=1, source_target_pairs={{0,8},{8,0},{1,9},{9,1},{2,10},{10,2},{3,11},{11,3},{4,12},{12,4},... | collective-permute-start | bytes 4128776 | tf_op jit(solution)/shard_map/ppermute | solution.py:401
  685.2 58.4 %collective-permute-start.17 = (f32[384,896]{1,0:T(8,128)}, f32[384,896]{1,0:T(8,128)}, u32[]{:S(2)}, u32[]{:S(2)}) collective-permute-start(f32[384,896]{1,0:T(8,128)} %get-tuple-element.99), channel_id=1, source_target_pairs={{0,8},{8,0},{1,9},{9,1},{2,10},{10,2},{3,11},{11,3},{4,12},{12,4},... | collective-permute-start | bytes 4128776 | tf_op jit(solution)/shard_map/ppermute | solution.py:401
  739.3 33.4 %collective-permute-start.14 = (f32[384,896]{1,0:T(8,128)}, f32[384,896]{1,0:T(8,128)}, u32[]{:S(2)}, u32[]{:S(2)}) collective-permute-start(f32[384,896]{1,0:T(8,128)} %add.140), channel_id=1, source_target_pairs={{0,2},{1,3},{2,0},{3,1},{4,6},{5,7},{6,4},{7,5},{8,10},{9,11},{10,... | collective-permute-start | bytes 4128776 | tf_op jit(solution)/shard_map/ppermute | solution.py:401
  743.7 62.9 %collective-permute-start.16 = (f32[384,896]{1,0:T(8,128)}, f32[384,896]{1,0:T(8,128)}, u32[]{:S(2)}, u32[]{:S(2)}) collective-permute-start(f32[384,896]{1,0:T(8,128)} %add.142), channel_id=1, source_target_pairs={{0,4},{1,5},{2,6},{3,7},{4,0},{5,1},{6,2},{7,3},{8,12},{9,13},{10,... | collective-permute-start | bytes 4128776 | tf_op jit(solution)/shard_map/ppermute | solution.py:401
  744.3 63.5 %copy-start.34 = (f32[1,6144]{1,0:T(1,128)S(1)}, f32[1,6144]{1,0:T(1,128)}, u32[]{:S(2)}) copy-start(f32[1,6144]{1,0:T(1,128)} %copy-done.33) | copy-start | bytes 73732
  744.3 63.5 %copy-start.32 = (f32[1,6144]{1,0:T(1,128)S(1)}, f32[1,6144]{1,0:T(1,128)}, u32[]{:S(2)}) copy-start(f32[1,6144]{1,0:T(1,128)} %copy-done.31) | copy-start | bytes 73732
  744.3 64.3 %copy-start.26 = (f32[3,8,768]{2,1,0:T(8,128)S(1)}, f32[3,8,768]{2,1,0:T(8,128)}, u32[]{:S(2)}) copy-start(f32[3,8,768]{2,1,0:T(8,128)} %copy-done.25) | copy-start | bytes 221188
  744.3 64.3 %copy-start.28 = (f32[3,8,768]{2,1,0:T(8,128)S(1)}, f32[3,8,768]{2,1,0:T(8,128)}, u32[]{:S(2)}) copy-start(f32[3,8,768]{2,1,0:T(8,128)} %copy-done.27) | copy-start | bytes 221188
  744.3 64.3 %copy-start.30 = (f32[1,8,768]{2,1,0:T(8,128)S(1)}, f32[1,8,768]{2,1,0:T(8,128)}, u32[]{:S(2)}) copy-start(f32[1,8,768]{2,1,0:T(8,128)} %copy-done.29) | copy-start | bytes 73732
  747.0 60.0 %collective-permute-start.18 = (f32[384,896]{1,0:T(8,128)}, f32[384,896]{1,0:T(8,128)}, u32[]{:S(2)}, u32[]{:S(2)}) collective-permute-start(f32[384,896]{1,0:T(8,128)} %add.144), channel_id=1, source_target_pairs={{0,6},{1,7},{2,4},{3,5},{4,2},{5,3},{6,0},{7,1},{8,14},{9,15},{10,... | collective-permute-start | bytes 4128776 | tf_op jit(solution)/shard_map/ppermute | solution.py:401
  748.6 145.1 %collective-permute-start.38 = (f32[112,3584]{1,0:T(8,128)}, f32[112,3584]{1,0:T(8,128)S(1)}, u32[]{:S(2)}, u32[]{:S(2)}) collective-permute-start(f32[112,3584]{1,0:T(8,128)} %get-tuple-element.116), channel_id=1, source_target_pairs={{0,1},{1,0},{2,3},{3,2},{4,5},{5,4},{6,7},{7,6},{8,9},{9,8},{10,11... | collective-permute-start | bytes 4816904 | tf_op jit(solution)/shard_map/ppermute | solution.py:401
  748.7 146.6 %collective-permute-start.39 = (f32[112,3584]{1,0:T(8,128)}, f32[112,3584]{1,0:T(8,128)S(1)}, u32[]{:S(2)}, u32[]{:S(2)}) collective-permute-start(f32[112,3584]{1,0:T(8,128)} %get-tuple-element.117), channel_id=1, source_target_pairs={{0,2},{1,3},{2,0},{3,1},{4,6},{5,7},{6,4},{7,5},{8,10},{9,11},{10,... | collective-permute-start | bytes 4816904 | tf_op jit(solution)/shard_map/ppermute | solution.py:401
  772.6 61.9 %collective-permute-start.35 = (f32[112,3072]{1,0:T(8,128)}, f32[112,3072]{1,0:T(8,128)}, u32[]{:S(2)}, u32[]{:S(2)}) collective-permute-start(f32[112,3072]{1,0:T(8,128)} %get-tuple-element.113), channel_id=1, source_target_pairs={{0,5},{1,4},{2,7},{3,6},{4,1},{5,0},{6,3},{7,2},{8,13},{9,12},{10,... | collective-permute-start | bytes 4128776 | tf_op jit(solution)/shard_map/ppermute | solution.py:401
  806.5 86.9 %collective-permute-start.36 = (f32[112,3072]{1,0:T(8,128)}, f32[112,3072]{1,0:T(8,128)}, u32[]{:S(2)}, u32[]{:S(2)}) collective-permute-start(f32[112,3072]{1,0:T(8,128)} %get-tuple-element.114), channel_id=1, source_target_pairs={{0,6},{1,7},{2,4},{3,5},{4,2},{5,3},{6,0},{7,1},{8,14},{9,15},{10,... | collective-permute-start | bytes 4128776 | tf_op jit(solution)/shard_map/ppermute | solution.py:401
  807.0 86.4 %collective-permute-start.37 = (f32[112,3072]{1,0:T(8,128)}, f32[112,3072]{1,0:T(8,128)}, u32[]{:S(2)}, u32[]{:S(2)}) collective-permute-start(f32[112,3072]{1,0:T(8,128)} %get-tuple-element.115), channel_id=1, source_target_pairs={{0,7},{1,6},{2,5},{3,4},{4,3},{5,2},{6,1},{7,0},{8,15},{9,14},{10,... | collective-permute-start | bytes 4128776 | tf_op jit(solution)/shard_map/ppermute | solution.py:401
  834.6 62.1 %collective-permute-start.19 = (f32[1,897]{1,0:T(1,128)S(1)}, f32[1,897]{1,0:T(1,128)S(1)}, u32[]{:S(2)}, u32[]{:S(2)}) collective-permute-start(f32[1,897]{1,0:T(1,128)S(1)} %bitcast.92), channel_id=1, source_target_pairs={{0,1},{1,0},{2,3},{3,2},{4,5},{5,4},{6,7},{7,6},{8,9},{9,8},{10,11... | collective-permute-start | bytes 10772 | tf_op jit(solution)/shard_map/ppermute | solution.py:401
  893.4 37.5 %collective-permute-start.40 = (f32[112,3584]{1,0:T(8,128)}, f32[112,3584]{1,0:T(8,128)}, u32[]{:S(2)}, u32[]{:S(2)}) collective-permute-start(f32[112,3584]{1,0:T(8,128)} %get-tuple-element.118), channel_id=1, source_target_pairs={{0,3},{1,2},{2,1},{3,0},{4,7},{5,6},{6,5},{7,4},{8,11},{9,10},{10,... | collective-permute-start | bytes 4816904 | tf_op jit(solution)/shard_map/ppermute | solution.py:401
  893.4 107.1 %collective-permute-start.41 = (f32[112,3584]{1,0:T(8,128)}, f32[112,3584]{1,0:T(8,128)}, u32[]{:S(2)}, u32[]{:S(2)}) collective-permute-start(f32[112,3584]{1,0:T(8,128)} %get-tuple-element.119), channel_id=1, source_target_pairs={{0,4},{1,5},{2,6},{3,7},{4,0},{5,1},{6,2},{7,3},{8,12},{9,13},{10,... | collective-permute-start | bytes 4816904 | tf_op jit(solution)/shard_map/ppermute | solution.py:401
  893.7 140.3 %collective-permute-start.42 = (f32[112,3584]{1,0:T(8,128)}, f32[112,3584]{1,0:T(8,128)}, u32[]{:S(2)}, u32[]{:S(2)}) collective-permute-start(f32[112,3584]{1,0:T(8,128)} %get-tuple-element.120), channel_id=1, source_target_pairs={{0,5},{1,4},{2,7},{3,6},{4,1},{5,0},{6,3},{7,2},{8,13},{9,12},{10,... | collective-permute-start | bytes 4816904 | tf_op jit(solution)/shard_map/ppermute | solution.py:401
  895.3 140.3 %collective-permute-start.43 = (f32[112,3584]{1,0:T(8,128)}, f32[112,3584]{1,0:T(8,128)}, u32[]{:S(2)}, u32[]{:S(2)}) collective-permute-start(f32[112,3584]{1,0:T(8,128)} %get-tuple-element.121), channel_id=1, source_target_pairs={{0,6},{1,7},{2,4},{3,5},{4,2},{5,3},{6,0},{7,1},{8,14},{9,15},{10,... | collective-permute-start | bytes 4816904 | tf_op jit(solution)/shard_map/ppermute | solution.py:401
  896.7 156.7 %collective-permute-start.44 = (f32[112,3584]{1,0:T(8,128)}, f32[112,3584]{1,0:T(8,128)}, u32[]{:S(2)}, u32[]{:S(2)}) collective-permute-start(f32[112,3584]{1,0:T(8,128)} %get-tuple-element.122), channel_id=1, source_target_pairs={{0,7},{1,6},{2,5},{3,4},{4,3},{5,2},{6,1},{7,0},{8,15},{9,14},{10,... | collective-permute-start | bytes 4816904 | tf_op jit(solution)/shard_map/ppermute | solution.py:401
  931.0 122.9 %collective-permute-start.24 = (f32[112,1536]{1,0:T(8,128)}, f32[112,1536]{1,0:T(8,128)S(1)}, u32[]{:S(2)}, u32[]{:S(2)}) collective-permute-start(f32[112,1536]{1,0:T(8,128)} %get-tuple-element.102), channel_id=1, source_target_pairs={{0,1},{1,0},{2,3},{3,2},{4,5},{5,4},{6,7},{7,6},{8,9},{9,8},{10,11... | collective-permute-start | bytes 2064392 | tf_op jit(solution)/shard_map/ppermute | solution.py:401
  1000.6 55.8 %collective-permute-start.25 = (f32[112,1536]{1,0:T(8,128)}, f32[112,1536]{1,0:T(8,128)S(1)}, u32[]{:S(2)}, u32[]{:S(2)}) collective-permute-start(f32[112,1536]{1,0:T(8,128)} %get-tuple-element.103), channel_id=1, source_target_pairs={{0,2},{1,3},{2,0},{3,1},{4,6},{5,7},{6,4},{7,5},{8,10},{9,11},{10,... | collective-permute-start | bytes 2064392 | tf_op jit(solution)/shard_map/ppermute | solution.py:401
  1033.9 23.3 %collective-permute-start.26 = (f32[112,1536]{1,0:T(8,128)}, f32[112,1536]{1,0:T(8,128)S(1)}, u32[]{:S(2)}, u32[]{:S(2)}) collective-permute-start(f32[112,1536]{1,0:T(8,128)} %get-tuple-element.104), channel_id=1, source_target_pairs={{0,3},{1,2},{2,1},{3,0},{4,7},{5,6},{6,5},{7,4},{8,11},{9,10},{10,... | collective-permute-start | bytes 2064392 | tf_op jit(solution)/shard_map/ppermute | solution.py:401
  1035.5 16.4 %collective-permute-start.20 = (f32[1,897]{1,0:T(1,128)S(1)}, f32[1,897]{1,0:T(1,128)S(1)}, u32[]{:S(2)}, u32[]{:S(2)}) collective-permute-start(f32[1,897]{1,0:T(1,128)S(1)} %add.155), channel_id=1, source_target_pairs={{0,2},{1,3},{2,0},{3,1},{4,6},{5,7},{6,4},{7,5},{8,10},{9,11},{10,... | collective-permute-start | bytes 10772 | tf_op jit(solution)/shard_map/ppermute | solution.py:401
  1035.9 68.9 %copy-start.17 = (s32[2]{0:T(128)S(1)}, s32[2]{0:T(128)}, u32[]{:S(2)}) copy-start(s32[2]{0:T(128)} %pad_add_fusion.d_ref) | copy-start | bytes 28
  1052.0 108.4 %collective-permute-start.23 = (f32[384,896]{1,0:T(8,128)}, f32[384,896]{1,0:T(8,128)}, u32[]{:S(2)}, u32[]{:S(2)}) collective-permute-start(f32[384,896]{1,0:T(8,128)} %fusion.6), channel_id=1, source_target_pairs={{0,8},{8,0},{1,9},{9,1},{2,10},{10,2},{3,11},{11,3},{4,12},{12,4},... | collective-permute-start | bytes 4128776 | tf_op jit(solution)/shard_map/ppermute | solution.py:401
  1053.4 6.4 collective-permute-start.21
  1054.7 47.8 %collective-permute-start.27 = (f32[112,1536]{1,0:T(8,128)S(1)}, f32[112,1536]{1,0:T(8,128)S(1)}, u32[]{:S(2)}, u32[]{:S(2)}) collective-permute-start(f32[112,1536]{1,0:T(8,128)S(1)} %copy-done.42), channel_id=1, source_target_pairs={{0,4},{1,5},{2,6},{3,7},{4,0},{5,1},{6,2},{7,3},{8,12},{9,13},{10,... | collective-permute-start | bytes 2064392 | tf_op jit(solution)/shard_map/ppermute | solution.py:401
  1057.2 95.5 %collective-permute-start.28 = (f32[112,1536]{1,0:T(8,128)}, f32[112,1536]{1,0:T(8,128)}, u32[]{:S(2)}, u32[]{:S(2)}) collective-permute-start(f32[112,1536]{1,0:T(8,128)} %get-tuple-element.106), channel_id=1, source_target_pairs={{0,5},{1,4},{2,7},{3,6},{4,1},{5,0},{6,3},{7,2},{8,13},{9,12},{10,... | collective-permute-start | bytes 2064392 | tf_op jit(solution)/shard_map/ppermute | solution.py:401
  1058.1 94.6 %collective-permute-start.29 = (f32[112,1536]{1,0:T(8,128)}, f32[112,1536]{1,0:T(8,128)}, u32[]{:S(2)}, u32[]{:S(2)}) collective-permute-start(f32[112,1536]{1,0:T(8,128)} %get-tuple-element.107), channel_id=1, source_target_pairs={{0,6},{1,7},{2,4},{3,5},{4,2},{5,3},{6,0},{7,1},{8,14},{9,15},{10,... | collective-permute-start | bytes 2064392 | tf_op jit(solution)/shard_map/ppermute | solution.py:401
  1059.8 92.9 %collective-permute-start.30 = (f32[112,1536]{1,0:T(8,128)}, f32[112,1536]{1,0:T(8,128)}, u32[]{:S(2)}, u32[]{:S(2)}) collective-permute-start(f32[112,1536]{1,0:T(8,128)} %get-tuple-element.108), channel_id=1, source_target_pairs={{0,7},{1,6},{2,5},{3,4},{4,3},{5,2},{6,1},{7,0},{8,15},{9,14},{10,... | collective-permute-start | bytes 2064392 | tf_op jit(solution)/shard_map/ppermute | solution.py:401
  1103.4 55.1 %collective-permute-start.22 = (f32[1,897]{1,0:T(1,128)S(1)}, f32[1,897]{1,0:T(1,128)S(1)}, u32[]{:S(2)}, u32[]{:S(2)}) collective-permute-start(f32[1,897]{1,0:T(1,128)S(1)} %add.157), channel_id=1, source_target_pairs={{0,8},{8,0},{1,9},{9,1},{2,10},{10,2},{3,11},{11,3},{4,12},{12,4},... | collective-permute-start | bytes 10772 | tf_op jit(solution)/shard_map/ppermute | solution.py:401
  (34 other events, 314.6 us)
